TPU v7x, 32 devices: a whole 2x2x4 slice. The times are simulated.
32 devices in a mesh: dp: 4 (over y, core), expert: 8 (over z, x).
Axes of the slice: x: 2, y: 2, z: 4, core: 2. Of those that a mesh axis runs over, the one named last changes fastest.
Arguments:
- tokens: bfloat16 [16, 1024, 768], P('dp', 'expert'), may hold values from -6 to 6
- segments: int32 [16, 1024], P('dp'), may hold values from 0 to 3, never falling along the last dimension, each value on 1 to 800 neighbouring positions
- routes: int32 [16, 1024, 2], P('dp', 'expert'), may hold values from 0 to 7, as said below
- slots: int32 [16, 1024, 2], P('dp', 'expert'), may hold values from -1 to 191, as said below
- cotangent: bfloat16 [16, 1024, 768], P('dp', 'expert'), may hold values from -6 to 6
- attn_gain: bfloat16 [768], replicated, may hold values from 0.25 to 1.75
- w_qkv: bfloat16 [768, 2304], replicated, may hold values from -0.21875 to 0.21875
- w_out: bfloat16 [768, 768], replicated, may hold values from -0.875 to 0.875
- ffn_gain: bfloat16 [768], replicated, may hold values from 0.25 to 1.75
- w_router: bfloat16 [768, 8], replicated, may hold values from -0.14941406 to 0.14941406
- shared_gate: bfloat16 [768, 2048], replicated, may hold values from -0.21875 to 0.21875
- shared_up: bfloat16 [768, 2048], replicated, may hold values from -0.21875 to 0.21875
- shared_down: bfloat16 [2048, 768], replicated, may hold values from -0.125 to 0.125
- expert_gate: bfloat16 [8, 768, 2048], P('expert'), may hold values from -0.21875 to 0.21875
- expert_up: bfloat16 [8, 768, 2048], P('expert'), may hold values from -0.21875 to 0.21875
- expert_down: bfloat16 [8, 2048, 768], P('expert'), may hold values from -0.125 to 0.125
Outputs:
- layer_out: bfloat16 [16, 1024, 768], P('dp', 'expert')
- token_grad: bfloat16 [16, 1024, 768], P('dp', 'expert')
- grad_attn_gain: float32 [768], P(('dp', 'expert'))
- grad_w_qkv: float32 [768, 2304], P(('dp', 'expert'))
- grad_w_out: float32 [768, 768], P(('dp', 'expert'))
- grad_ffn_gain: float32 [768], P(('dp', 'expert'))
- grad_w_router: float32 [768, 8], P(('dp', 'expert'))
- grad_shared_gate: float32 [768, 2048], P(('dp', 'expert'))
- grad_shared_up: float32 [768, 2048], P(('dp', 'expert'))
- grad_shared_down: float32 [2048, 768], P(None, ('dp', 'expert'))
- grad_expert_gate: float32 [8, 768, 2048], P('expert', None, 'dp')
- grad_expert_up: float32 [8, 768, 2048], P('expert', None, 'dp')
- grad_expert_down: float32 [8, 2048, 768], P('expert', 'dp')
Inputs may be any that keep to these rules, and one draw needn't show every extreme that they name: `segments`: documents are numbered from 0 in order along each sequence, 4 of them, each of at most 800 tokens. `routes`: the 2 experts of a token differ; among the tokens of one device (positions r * 128 to (r + 1) * 128 - 1 of the 4 sequences of one index of dp), exactly 256 name as first choice one expert, the same for all devices of that index of dp. On one device, taking its tokens in order of sequence, then position, then choice, the routes to one expert get slots 0, 1, 2, ... and those from 192 on get -1; in every index of dp one expert takes 192 slots from every device.
All inputs are finite; a program needn't handle non-finite values.
Results may differ from a plain program's by a relative error of at most 0.015.
Values may be sent and summed in bfloat16 or wider, within the bound.
No kernel may reach another device: no remote copies, remote signals or barrier semaphores. Data moves between devices by JAX's collectives and lax.ppermute only.
A program may use at most 320 MiB of HBM per device.

v0:
```python
import math

import jax
import jax.numpy as jnp
from jax import lax
from jax.sharding import PartitionSpec as P

HEAD_DIM = 64


eps = 1e-06


def rms_scale(values):
    return lax.rsqrt(jnp.mean(values * values, axis=-1, keepdims=True) + eps)


def rotate(tensor, cosine, sine_table):
    middle = tensor.shape[-1] // 2
    leading = tensor[..., :middle]
    trailing = tensor[..., middle:]
    return jnp.concatenate(
        [leading * cosine - trailing * sine_table, trailing * cosine + leading * sine_table],
        axis=-1,
    )


def rope_tables(position, head_dim):
    frequency = jnp.power(10000.0, -2.0 * jnp.arange(head_dim // 2, dtype=jnp.float32) / head_dim)
    angles = position.astype(jnp.float32)[:, None] * frequency[None, :]
    return (jnp.cos(angles)[None, :, None, :], jnp.sin(angles)[None, :, None, :])


def silu_grads(gate_val, up_val, grad_act):
    sigmoid = jax.nn.sigmoid(gate_val)
    grad_gate = grad_act * up_val * sigmoid * (1.0 + gate_val * (1.0 - sigmoid))
    grad_up = grad_act * (gate_val * sigmoid)
    return (grad_gate, grad_up)


def norm_back(inputs, scaling, gain, grad_normed):
    weighted = grad_normed * gain
    grad_gain = jnp.sum(grad_normed * inputs * scaling, axis=0)
    grad_in = scaling * weighted - inputs * scaling * scaling * scaling * jnp.mean(
        weighted * inputs, axis=-1, keepdims=True
    )
    return (grad_in, grad_gain)


def masked_scores(queries, key_rows, allowed, scaling):
    products = (
        jnp.einsum("sqhd,skhd->shqk", queries, key_rows, preferred_element_type=jnp.float32)
        * scaling
    )
    return jnp.where(allowed[:, None], products, -1e30)


def on_device(
    tokens,
    segments,
    routes,
    slots,
    cotangent,
    attn_gain,
    w_qkv,
    w_out,
    ffn_gain,
    w_router,
    shared_gate,
    shared_up,
    shared_down,
    expert_gate,
    expert_up,
    expert_down,
):
    seq_count, span_len, width = tokens.shape
    head_dim = HEAD_DIM
    head_count = width // head_dim
    group_heads = math.gcd(head_count, 4)
    block_count = head_count // group_heads
    scaling = 1.0 / math.sqrt(head_dim)
    rank_count = lax.axis_size("expert")
    my_rank = lax.axis_index("expert")
    seq_len = span_len * rank_count
    token_count = seq_count * span_len
    local_experts = expert_gate.shape[0]
    expert_total = local_experts * rank_count
    capacity = 3 * token_count // expert_total
    buffer_size = expert_total * capacity
    choice_count = routes.shape[2]
    head_shape = (seq_count, span_len, head_count, head_dim)
    flat_shape = (seq_count, span_len, width)
    full_shape = (seq_count, seq_len, head_count, head_dim)
    attn_scale = attn_gain.astype(jnp.float32)
    ffn_scale = ffn_gain.astype(jnp.float32)
    token_rows = tokens.reshape(token_count, width).astype(jnp.float32)
    scale_one = rms_scale(token_rows)
    normed = (token_rows * scale_one * attn_scale).astype(jnp.bfloat16)
    projected = jnp.dot(normed, w_qkv, preferred_element_type=jnp.float32)
    local_pos = my_rank * span_len + jnp.arange(span_len, dtype=jnp.int32)
    cosine, sine_table = rope_tables(local_pos, head_dim)
    query_heads = rotate(projected[:, :width].reshape(head_shape), cosine, sine_table).astype(
        jnp.bfloat16
    )
    key_local = rotate(
        projected[:, width : 2 * width].reshape(head_shape), cosine, sine_table
    ).astype(jnp.bfloat16)
    value_local = projected[:, 2 * width :].reshape(head_shape).astype(jnp.bfloat16)
    key_send = key_local.reshape(flat_shape)
    value_send = value_local.reshape(flat_shape)
    key_full, value_full = (
        lax.all_gather(key_send, "expert", axis=1, tiled=True),
        lax.all_gather(value_send, "expert", axis=1, tiled=True),
    )
    key_full = key_full.reshape(full_shape)
    value_full = value_full.reshape(full_shape)
    query_seg = lax.dynamic_slice_in_dim(segments, my_rank * span_len, span_len, 1)
    key_pos = jnp.arange(seq_len, dtype=jnp.int32)
    allowed = (query_seg[:, :, None] == segments[:, None, :]) & (
        key_pos[None, None, :] <= local_pos[None, :, None]
    )
    attended_parts = []
    lse_parts = []
    for block_index in range(block_count):
        head_lo = block_index * group_heads
        head_hi = head_lo + group_heads
        scores = masked_scores(
            query_heads[:, :, head_lo:head_hi], key_full[:, :, head_lo:head_hi], allowed, scaling
        )
        row_max = jnp.max(scores, axis=-1, keepdims=True)
        exponent = jnp.exp(scores - row_max)
        row_sum = jnp.sum(exponent, axis=-1, keepdims=True)
        prob_rows = (exponent / row_sum).astype(jnp.bfloat16)
        attended_parts.append(
            jnp.einsum(
                "shqk,skhd->sqhd",
                prob_rows,
                value_full[:, :, head_lo:head_hi],
                preferred_element_type=jnp.float32,
            )
        )
        lse_parts.append((row_max + jnp.log(row_sum))[..., 0])
    log_totals = jnp.concatenate(lse_parts, axis=1)
    attended = (
        jnp.concatenate(attended_parts, axis=2).reshape(token_count, width).astype(jnp.bfloat16)
    )
    attn_out = jnp.dot(attended, w_out, preferred_element_type=jnp.float32)
    hidden = token_rows + attn_out
    scale_two = rms_scale(hidden)
    branch_in = (hidden * scale_two * ffn_scale).astype(jnp.bfloat16)
    logits = jnp.dot(branch_in, w_router, preferred_element_type=jnp.float32)
    route_rows = routes.reshape(token_count, choice_count)
    route_hot = (
        route_rows[:, :, None] == jnp.arange(expert_total, dtype=jnp.int32)[None, None, :]
    ).astype(jnp.float32)
    chosen = jnp.sum(logits[:, None, :] * route_hot, axis=-1)
    gates = jax.nn.softmax(chosen, axis=-1)
    shared_gval = jnp.dot(branch_in, shared_gate, preferred_element_type=jnp.float32)
    shared_uval = jnp.dot(branch_in, shared_up, preferred_element_type=jnp.float32)
    shared_hid = (jax.nn.silu(shared_gval) * shared_uval).astype(jnp.bfloat16)
    shared_out = jnp.dot(shared_hid, shared_down, preferred_element_type=jnp.float32)
    slot_rows = slots.reshape(token_count, choice_count)
    target = jnp.where(slot_rows >= 0, route_rows * capacity + slot_rows, buffer_size)
    row_ids = jnp.arange(token_count * choice_count, dtype=jnp.int32)
    buffer_row = (
        jnp.full((buffer_size,), token_count * choice_count, jnp.int32)
        .at[target.reshape(-1)]
        .set(row_ids, mode="drop")
    )
    buffer_tok = buffer_row // choice_count
    zero_row = jnp.zeros((1, width), jnp.bfloat16)
    send_rows = jnp.concatenate([branch_in, zero_row], axis=0)[buffer_tok].reshape(
        rank_count, local_experts, capacity, width
    )
    received = lax.all_to_all(send_rows, "expert", split_axis=0, concat_axis=0, tiled=True)
    gate_val = jnp.einsum(
        "necd,edf->necf", received, expert_gate, preferred_element_type=jnp.float32
    )
    up_val = jnp.einsum("necd,edf->necf", received, expert_up, preferred_element_type=jnp.float32)
    hidden_act = (jax.nn.silu(gate_val) * up_val).astype(jnp.bfloat16)
    produced = jnp.einsum(
        "necf,efd->necd", hidden_act, expert_down, preferred_element_type=jnp.float32
    ).astype(jnp.bfloat16)
    returned = lax.all_to_all(produced, "expert", split_axis=0, concat_axis=0, tiled=True)
    returned_rows = jnp.concatenate([returned.reshape(buffer_size, width), zero_row], axis=0)[
        target
    ].astype(jnp.float32)
    routed = jnp.sum(gates[:, :, None] * returned_rows, axis=1)
    layer_out = (hidden + shared_out + routed).astype(jnp.bfloat16).reshape(tokens.shape)
    grad_out = cotangent.reshape(token_count, width).astype(jnp.float32)
    grad_shared = grad_out.astype(jnp.bfloat16)
    grad_shared_down = jnp.einsum(
        "tf,td->fd", shared_hid, grad_shared, preferred_element_type=jnp.float32
    )
    grad_shared_hid = jnp.einsum(
        "td,fd->tf", grad_shared, shared_down, preferred_element_type=jnp.float32
    )
    grad_sgval, grad_suval = silu_grads(shared_gval, shared_uval, grad_shared_hid)
    grad_sgval = grad_sgval.astype(jnp.bfloat16)
    grad_suval = grad_suval.astype(jnp.bfloat16)
    grad_shared_gate = jnp.einsum(
        "td,tf->df", branch_in, grad_sgval, preferred_element_type=jnp.float32
    )
    grad_shared_up = jnp.einsum(
        "td,tf->df", branch_in, grad_suval, preferred_element_type=jnp.float32
    )
    gate_pad = jnp.concatenate([gates.reshape(-1), jnp.zeros((1,), jnp.float32)], axis=0)
    grad_pad = jnp.concatenate([grad_out, jnp.zeros((1, width), jnp.float32)], axis=0)
    grad_send = (
        (gate_pad[buffer_row][:, None] * grad_pad[buffer_tok])
        .astype(jnp.bfloat16)
        .reshape(rank_count, local_experts, capacity, width)
    )
    grad_recv = lax.all_to_all(grad_send, "expert", split_axis=0, concat_axis=0, tiled=True)
    grad_expert_down = jnp.einsum(
        "necf,necd->efd", hidden_act, grad_recv, preferred_element_type=jnp.float32
    )
    grad_hidden_act = jnp.einsum(
        "necd,efd->necf", grad_recv, expert_down, preferred_element_type=jnp.float32
    )
    grad_egval, grad_euval = silu_grads(gate_val, up_val, grad_hidden_act)
    grad_egval = grad_egval.astype(jnp.bfloat16)
    grad_euval = grad_euval.astype(jnp.bfloat16)
    grad_expert_gate = jnp.einsum(
        "necd,necf->edf", received, grad_egval, preferred_element_type=jnp.float32
    )
    grad_expert_up = jnp.einsum(
        "necd,necf->edf", received, grad_euval, preferred_element_type=jnp.float32
    )
    grad_expert_in = (
        jnp.einsum("necf,edf->necd", grad_egval, expert_gate, preferred_element_type=jnp.float32)
        + jnp.einsum("necf,edf->necd", grad_euval, expert_up, preferred_element_type=jnp.float32)
    ).astype(jnp.bfloat16)
    grad_back = lax.all_to_all(grad_expert_in, "expert", split_axis=0, concat_axis=0, tiled=True)
    grad_rows = jnp.concatenate([grad_back.reshape(buffer_size, width), zero_row], axis=0)[
        target
    ].astype(jnp.float32)
    grad_gates = jnp.sum(grad_out[:, None, :] * returned_rows, axis=-1)
    grad_chosen = gates * (grad_gates - jnp.sum(gates * grad_gates, axis=-1, keepdims=True))
    grad_logits = jnp.sum(grad_chosen[:, :, None] * route_hot, axis=1).astype(jnp.bfloat16)
    grad_w_router = jnp.einsum(
        "td,te->de", branch_in, grad_logits, preferred_element_type=jnp.float32
    )
    grad_branch = jnp.einsum(
        "tf,df->td", grad_sgval, shared_gate, preferred_element_type=jnp.float32
    )
    grad_branch = grad_branch + jnp.einsum(
        "tf,df->td", grad_suval, shared_up, preferred_element_type=jnp.float32
    )
    grad_branch = grad_branch + jnp.einsum(
        "te,de->td", grad_logits, w_router, preferred_element_type=jnp.float32
    )
    grad_branch = grad_branch + jnp.sum(grad_rows, axis=1)
    grad_in_two, grad_ffn_gain = norm_back(hidden, scale_two, ffn_scale, grad_branch)
    grad_hidden = grad_out + grad_in_two
    grad_attn = grad_hidden.astype(jnp.bfloat16)
    grad_w_out = jnp.einsum("td,te->de", attended, grad_attn, preferred_element_type=jnp.float32)
    grad_heads = (
        jnp.einsum("te,de->td", grad_attn, w_out, preferred_element_type=jnp.float32)
        .astype(jnp.bfloat16)
        .reshape(head_shape)
    )
    grad_query_parts = []
    delta_parts = []
    key_grad_parts = []
    value_grad_parts = []
    for block_index in range(block_count):
        head_lo = block_index * group_heads
        head_hi = head_lo + group_heads
        query_block = query_heads[:, :, head_lo:head_hi]
        grad_block = grad_heads[:, :, head_lo:head_hi]
        scores = masked_scores(query_block, key_full[:, :, head_lo:head_hi], allowed, scaling)
        prob_rows = jnp.exp(scores - log_totals[:, head_lo:head_hi, :, None])
        grad_probs = jnp.einsum(
            "sqhd,skhd->shqk",
            grad_block,
            value_full[:, :, head_lo:head_hi],
            preferred_element_type=jnp.float32,
        )
        row_delta = jnp.sum(prob_rows * grad_probs, axis=-1, keepdims=True)
        grad_scores = (prob_rows * (grad_probs - row_delta)).astype(jnp.bfloat16)
        grad_query_parts.append(
            jnp.einsum(
                "shqk,skhd->sqhd",
                grad_scores,
                key_full[:, :, head_lo:head_hi],
                preferred_element_type=jnp.float32,
            )
            * scaling
        )
        delta_parts.append(row_delta[..., 0])
        key_grad_parts.append(
            jnp.einsum(
                "shqk,sqhd->skhd", grad_scores, query_block, preferred_element_type=jnp.float32
            )
            * scaling
        )
        value_grad_parts.append(
            jnp.einsum(
                "shqk,sqhd->skhd",
                prob_rows.astype(jnp.bfloat16),
                grad_block,
                preferred_element_type=jnp.float32,
            )
        )
    key_grad_all = jnp.concatenate(key_grad_parts, axis=2).reshape(seq_count, seq_len, width)
    value_grad_all = jnp.concatenate(value_grad_parts, axis=2).reshape(seq_count, seq_len, width)
    key_grad, value_grad = (
        lax.psum_scatter(
            key_grad_all.astype(jnp.bfloat16), "expert", scatter_dimension=1, tiled=True
        ).astype(jnp.float32),
        lax.psum_scatter(
            value_grad_all.astype(jnp.bfloat16), "expert", scatter_dimension=1, tiled=True
        ).astype(jnp.float32),
    )
    grad_query = jnp.concatenate(grad_query_parts, axis=2)
    grad_q_pre = rotate(grad_query, cosine, -sine_table).reshape(token_count, width)
    grad_k_pre = rotate(key_grad.reshape(head_shape), cosine, -sine_table).reshape(
        token_count, width
    )
    grad_projected = jnp.concatenate(
        [grad_q_pre, grad_k_pre, value_grad.reshape(token_count, width)], axis=-1
    ).astype(jnp.bfloat16)
    grad_w_qkv = jnp.einsum("td,te->de", normed, grad_projected, preferred_element_type=jnp.float32)
    grad_normed = jnp.einsum("te,de->td", grad_projected, w_qkv, preferred_element_type=jnp.float32)
    grad_in_one, grad_attn_gain = norm_back(token_rows, scale_one, attn_scale, grad_normed)
    token_grad = (grad_hidden + grad_in_one).astype(jnp.bfloat16).reshape(tokens.shape)
    dense = (
        lax.psum_scatter(grad_attn_gain, ("dp", "expert"), scatter_dimension=0, tiled=True),
        lax.psum_scatter(grad_w_qkv, ("dp", "expert"), scatter_dimension=0, tiled=True),
        lax.psum_scatter(grad_w_out, ("dp", "expert"), scatter_dimension=0, tiled=True),
        lax.psum_scatter(grad_ffn_gain, ("dp", "expert"), scatter_dimension=0, tiled=True),
        lax.psum_scatter(grad_w_router, ("dp", "expert"), scatter_dimension=0, tiled=True),
        lax.psum_scatter(grad_shared_gate, ("dp", "expert"), scatter_dimension=0, tiled=True),
        lax.psum_scatter(grad_shared_up, ("dp", "expert"), scatter_dimension=0, tiled=True),
        lax.psum_scatter(grad_shared_down, ("dp", "expert"), scatter_dimension=1, tiled=True),
    )
    expert_sums = (
        lax.psum_scatter(
            grad_expert_gate.astype(jnp.bfloat16), "dp", scatter_dimension=2, tiled=True
        ).astype(jnp.float32),
        lax.psum_scatter(
            grad_expert_up.astype(jnp.bfloat16), "dp", scatter_dimension=2, tiled=True
        ).astype(jnp.float32),
        lax.psum_scatter(
            grad_expert_down.astype(jnp.bfloat16), "dp", scatter_dimension=1, tiled=True
        ).astype(jnp.float32),
    )
    return (
        layer_out,
        token_grad,
        dense[0],
        dense[1],
        dense[2],
        dense[3],
        dense[4],
        dense[5],
        dense[6],
        dense[7],
        expert_sums[0],
        expert_sums[1],
        expert_sums[2],
    )


def solution(mesh):
    placed = (
        P("dp", "expert", None),
        P("dp", None),
        P("dp", "expert", None),
        P("dp", "expert", None),
        P("dp", "expert", None),
        P(),
        P(),
        P(),
        P(),
        P(),
        P(),
        P(),
        P(),
        P("expert", None, None),
        P("expert", None, None),
        P("expert", None, None),
    )
    return jax.shard_map(
        on_device,
        mesh=mesh,
        in_specs=placed,
        out_specs=(
            P("dp", "expert", None),
            P("dp", "expert", None),
            P(("dp", "expert")),
            P(("dp", "expert"), None),
            P(("dp", "expert"), None),
            P(("dp", "expert")),
            P(("dp", "expert"), None),
            P(("dp", "expert"), None),
            P(("dp", "expert"), None),
            P(None, ("dp", "expert")),
            P("expert", None, "dp"),
            P("expert", None, "dp"),
            P("expert", "dp", None),
        ),
        check_vma=False,
    )
```

profile of v0, /device:TPU:0, one launch (start us, length us, event | category | flops | bytes accessed | tf_op | source)
XLA Modules:
  0.0 1589.9 jit_solution(10749424462307013123)
XLA Ops:
  49.8 8.2 gather_fusion.3
  60.8 77.3 %all-gather.5.cloned.1.call-done = bf16[4,1024,768]{1,2,0:T(8,128)(2,1)} async-done(((bf16[4,128,768]{1,2,0:T(8,128)(2,1)}), bf16[4,1024,768]{1,2,0:T(8,128)(2,1)}) %all-gather.5.cloned.1.call-update) | async-done | bytes 6291472 | tf_op jit(solution)/shard_map/all_gather | solution.py:112
  158.5 79.2 %all-gather.3.cloned.1.call-done = bf16[4,1024,768]{2,1,0:T(8,128)(2,1)} async-done(((bf16[4,128,768]{2,1,0:T(8,128)(2,1)}), bf16[4,1024,768]{2,1,0:T(8,128)(2,1)}) %all-gather.3.cloned.1.call-update) | async-done | bytes 6291472 | tf_op jit(solution)/shard_map/all_gather | solution.py:113
  237.7 8.7 copy.112
  269.6 11.9 gather_fusion.2
  292.9 7.9 gather_fusion
  300.9 42.8 %all-to-all-done.2 = bf16[8,1,192,768]{3,2,1,0:T(8,128)(2,1)} async-done(((bf16[8,1,192,768]{3,2,1,0:T(8,128)(2,1)}), bf16[8,1,192,768]{3,2,1,0:T(8,128)(2,1)}, u32[]{:S(2)}, u32[]{:S(2)}) %all-to-all-start.2) | async-done | bytes 2359328 | tf_op jit(solution)/shard_map/all_to_all | solution.py:214
  348.1 10.2 fusion.36
  358.2 43.2 %all-to-all-done = bf16[8,1,192,768]{3,2,1,0:T(8,128)(2,1)} async-done(((bf16[8,1,192,768]{3,2,1,0:T(8,128)(2,1)}), bf16[8,1,192,768]{3,2,1,0:T(8,128)(2,1)}, u32[]{:S(2)}, u32[]{:S(2)}) %all-to-all-start) | async-done | bytes 2359328 | tf_op jit(solution)/shard_map/all_to_all | solution.py:175
  401.4 10.1 fusion.42
  411.6 21.6 %fusion.16 = (bf16[8,192,2048]{2,1,0:T(8,128)(2,1)}, bf16[8,1,192,2048]{3,2,0,1:T(8,128)(2,1)}, bf16[8,192,2048]{2,1,0:T(8,128)(2,1)}) fusion(f32[8,192,2048]{2,1,0:T(8,128)} %fusion.36, f32[8,192,2048]{2,1,0:T(8,128)} %fusion.42, bf16[1,768,2048]{2,1,0:T(8,128)(2,1)} %param.29, bf16[8,1,192,768]{3,2,1,0:T(8,128)(2,1)} %all-to-all-done), kind=kOutput, calls=%fused_computation.46 | convolution fusion | flops 4879024128 | bytes 49545216 | tf_op jit(solution)/shard_map/necd,edf->necf/dot_general | solution.py:176
  433.2 9.1 convert_bitcast_fusion
  451.6 8.3 fusion.19
  459.9 9.6 fusion.52
  469.5 31.1 %all-to-all-done.1 = bf16[8,1,192,768]{3,2,1,0:T(8,128)(2,1)} async-done(((bf16[8,1,192,768]{3,2,1,0:T(8,128)(2,1)}), bf16[8,1,192,768]{3,2,1,0:T(8,128)(2,1)}, u32[]{:S(2)}, u32[]{:S(2)}) %all-to-all-start.1) | async-done | bytes 2359328 | tf_op jit(solution)/shard_map/all_to_all | solution.py:184
  541.6 16.8 %all-to-all-done.3 = bf16[8,1,192,768]{3,2,1,0:T(8,128)(2,1)} async-done(((bf16[8,1,192,768]{3,2,1,0:T(8,128)(2,1)}), bf16[8,1,192,768]{3,2,1,0:T(8,128)(2,1)}, u32[]{:S(2)}, u32[]{:S(2)}) %all-to-all-start.3) | async-done | bytes 2359328 | tf_op jit(solution)/shard_map/all_to_all | solution.py:234
  581.1 9.6 multiply_reduce_fusion.3
  625.8 8.7 copy.138
  673.5 10.8 copy.140
  691.4 9.2 fusion.47
  700.7 9.6 fusion.50
  710.4 9.2 fusion.51
  756.3 116.1 %reduce-scatter.32.cloned.1.call-done = bf16[128,3072]{1,0:T(8,128)(2,1)} async-done(((bf16[1024,3072]{1,0:T(8,128)(2,1)}), bf16[128,3072]{1,0:T(8,128)(2,1)}) %reduce-scatter.32.cloned.1.call-update) | async-done | bytes 786448
  897.5 14.3 reduce-scatter.26.cloned.1.call-done
  914.3 37.6 %reduce-scatter.28.cloned.1.call-done = bf16[1,768,512]{2,1,0:T(8,128)(2,1)} async-done(((bf16[1,768,2048]{2,1,0:T(8,128)(2,1)}), bf16[1,768,512]{2,1,0:T(8,128)(2,1)}) %reduce-scatter.28.cloned.1.call-update) | async-done | bytes 786448 | tf_op jit(solution)/shard_map/reduce_scatter | solution.py:342
  954.5 38.0 %reduce-scatter.30.cloned.1.call-done = bf16[1,512,768]{2,1,0:T(8,128)(2,1)} async-done(((bf16[1,2048,768]{2,1,0:T(8,128)(2,1)}), bf16[1,512,768]{2,1,0:T(8,128)(2,1)}) %reduce-scatter.30.cloned.1.call-update) | async-done | bytes 786448 | tf_op jit(solution)/shard_map/reduce_scatter | solution.py:345
  1000.7 40.3 %all-reduce.7 = (f32[768]{0:T(1024)}, f32[768]{0:T(1024)}, f32[768,8]{0,1:T(8,128)}) all-reduce(f32[768]{0:T(1024)S(1)} %get-tuple-element.17, f32[768]{0:T(1024)S(1)} %copy-done.64, f32[768,8]{0,1:T(8,128)} %fusion.150), channel_id=4, replica_groups=mesh['dp'=4,'expert'=8] {'dp','expert'}, use_global_device_ids=true, to_apply=%region_25.26.clone | all-reduce | flops 7680 | bytes 61440
  1049.1 64.6 %reduce-scatter.20.cloned.1.call-done = f32[24,2048]{1,0:T(8,128)} async-done(((f32[768,2048]{1,0:T(8,128)}), f32[24,2048]{1,0:T(8,128)}) %reduce-scatter.20.cloned.1.call-update) | async-done | bytes 196624 | tf_op jit(solution)/shard_map/reduce_scatter | solution.py:334
  1113.7 120.1 %reduce-scatter.22.cloned.1.call-done = f32[24,2048]{1,0:T(8,128)} async-done(((f32[768,2048]{1,0:T(8,128)}), f32[24,2048]{1,0:T(8,128)}) %reduce-scatter.22.cloned.1.call-update) | async-done | bytes 196624 | tf_op jit(solution)/shard_map/reduce_scatter | solution.py:335
  1233.8 120.0 %reduce-scatter.24.cloned.1.call-done = f32[2048,24]{0,1:T(8,128)} async-done(((f32[2048,768]{0,1:T(8,128)}), f32[2048,24]{0,1:T(8,128)}) %reduce-scatter.24.cloned.1.call-update) | async-done | bytes 196624 | tf_op jit(solution)/shard_map/reduce_scatter | solution.py:336
  1353.8 104.4 %reduce-scatter.18.cloned.1.call-done = f32[24,768]{1,0:T(8,128)} async-done(((f32[768,768]{1,0:T(8,128)}), f32[24,768]{1,0:T(8,128)}) %reduce-scatter.18.cloned.1.call-update) | async-done | bytes 73744 | tf_op jit(solution)/shard_map/reduce_scatter | solution.py:331
  1458.2 124.7 %reduce-scatter.16.cloned.1.call-done = f32[24,2304]{1,0:T(8,128)} async-done(((f32[768,2304]{1,0:T(8,128)}), f32[24,2304]{1,0:T(8,128)}) %reduce-scatter.16.cloned.1.call-update) | async-done | bytes 221200 | tf_op jit(solution)/shard_map/reduce_scatter | solution.py:330
  (336 shorter events, 341.1 us)
Async XLA Ops:
  7.2 130.8 %all-gather.5.cloned.1.call-start = ((), (), s32[]{:S(2)}) async-start(), calls=%async_computation.15 | async-start | bytes 7077888 | tf_op jit(solution)/shard_map/all_gather | solution.py:112
  35.7 202.0 %all-gather.3.cloned.1.call-start = ((), (), s32[]{:S(2)}) async-start(), calls=%async_computation.14 | async-start | bytes 7077888 | tf_op jit(solution)/shard_map/all_gather | solution.py:113
  49.8 8.2 copy-start.42
  49.8 8.9 copy-start.66
  142.1 104.3 %copy-start.54 = (f32[4,4,128]{2,1,0:T(4,128)}, f32[4,4,128]{2,1,0:T(4,128)S(1)}, u32[]{:S(2)}) copy-start(f32[4,4,128]{2,1,0:T(4,128)S(1)} %get-tuple-element.56) | copy-start | bytes 24580
  246.4 8.3 copy-start.5
  286.3 57.3 %all-to-all-start.2 = ((bf16[8,1,192,768]{3,2,1,0:T(8,128)(2,1)}), bf16[8,1,192,768]{3,2,1,0:T(8,128)(2,1)}, u32[]{:S(2)}, u32[]{:S(2)}) async-start(bf16[8,1,192,768]{3,2,1,0:T(8,128)(2,1)} %multiply_convert_fusion.3), calls=%async_computation.2 | async-start | bytes 4718592 | tf_op jit(solution)/shard_map/all_to_all | solution.py:214
  343.7 57.8 %all-to-all-start = ((bf16[8,1,192,768]{3,2,1,0:T(8,128)(2,1)}), bf16[8,1,192,768]{3,2,1,0:T(8,128)(2,1)}, u32[]{:S(2)}, u32[]{:S(2)}) async-start(bf16[8,1,192,768]{3,2,1,0:T(8,128)(2,1)} %bitcast.347), calls=%async_computation | async-start | bytes 4718592 | tf_op jit(solution)/shard_map/all_to_all | solution.py:175
  442.3 58.3 %all-to-all-start.1 = ((bf16[8,1,192,768]{3,2,1,0:T(8,128)(2,1)}), bf16[8,1,192,768]{3,2,1,0:T(8,128)(2,1)}, u32[]{:S(2)}, u32[]{:S(2)}) async-start(bf16[8,1,192,768]{3,2,1,0:T(8,128)(2,1)} %convert_bitcast_fusion), calls=%async_computation.1 | async-start | bytes 4718592 | tf_op jit(solution)/shard_map/all_to_all | solution.py:184
  451.6 8.3 copy-start.67
  500.6 57.8 %all-to-all-start.3 = ((bf16[8,1,192,768]{3,2,1,0:T(8,128)(2,1)}), bf16[8,1,192,768]{3,2,1,0:T(8,128)(2,1)}, u32[]{:S(2)}, u32[]{:S(2)}) async-start(bf16[8,1,192,768]{3,2,1,0:T(8,128)(2,1)} %fusion.52), calls=%async_computation.3 | async-start | bytes 4718592 | tf_op jit(solution)/shard_map/all_to_all | solution.py:234
  505.0 248.9 %reduce-scatter.14.cloned.1.call-start = ((), (), s32[]{:S(2)}) async-start(), calls=%async_computation.16 | async-start | bytes 7077888 | tf_op jit(solution)/shard_map/reduce_scatter | solution.py:312
  581.1 10.7 copy-start.47
  600.0 8.3 copy-start.40
  608.3 10.6 copy-start.18
  608.4 10.6 slice-start.2
  634.5 237.9 %reduce-scatter.32.cloned.1.call-start = ((), (), s32[]{:S(2)}) async-start(), calls=%async_computation.25 | async-start | bytes 7077888
  634.6 15.4 slice-start.8
  641.3 8.7 slice-start.9
  650.0 10.0 slice-start.4
  691.4 220.4 %reduce-scatter.26.cloned.1.call-start = ((), (), s32[]{:S(2)}) async-start(), calls=%async_computation.22 | async-start | bytes 3932160 | tf_op jit(solution)/shard_map/reduce_scatter | solution.py:339
  700.7 251.3 %reduce-scatter.28.cloned.1.call-start = ((), (), s32[]{:S(2)}) async-start(), calls=%async_computation.23 | async-start | bytes 3932160 | tf_op jit(solution)/shard_map/reduce_scatter | solution.py:342
  710.4 282.0 %reduce-scatter.30.cloned.1.call-start = ((), (), s32[]{:S(2)}) async-start(), calls=%async_computation.24 | async-start | bytes 3932160 | tf_op jit(solution)/shard_map/reduce_scatter | solution.py:345
  719.6 394.0 %reduce-scatter.20.cloned.1.call-start = ((), (), s32[]{:S(2)}) async-start(), calls=%async_computation.19 | async-start | bytes 6488064 | tf_op jit(solution)/shard_map/reduce_scatter | solution.py:334
  725.9 507.8 %reduce-scatter.22.cloned.1.call-start = ((), (), s32[]{:S(2)}) async-start(), calls=%async_computation.20 | async-start | bytes 6488064 | tf_op jit(solution)/shard_map/reduce_scatter | solution.py:335
  732.4 621.4 %reduce-scatter.24.cloned.1.call-start = ((), (), s32[]{:S(2)}) async-start(), calls=%async_computation.21 | async-start | bytes 6488064 | tf_op jit(solution)/shard_map/reduce_scatter | solution.py:336
  738.7 719.6 %reduce-scatter.18.cloned.1.call-start = ((), (), s32[]{:S(2)}) async-start(), calls=%async_computation.18 | async-start | bytes 2433024 | tf_op jit(solution)/shard_map/reduce_scatter | solution.py:331
  742.7 840.2 %reduce-scatter.16.cloned.1.call-start = ((), (), s32[]{:S(2)}) async-start(), calls=%async_computation.17 | async-start | bytes 7299072 | tf_op jit(solution)/shard_map/reduce_scatter | solution.py:330
  742.8 8.0 slice-start.10
  753.9 124.8 %copy-start.37 = (f32[128,32]{0,1:T(8,128)S(1)}, f32[128,32]{0,1:T(8,128)}, u32[]{:S(2)}) copy-start(f32[128,32]{0,1:T(8,128)} %copy-done.36) | copy-start | bytes 49156
  897.5 97.3 %copy-start.50 = (f32[768]{0:T(1024)S(1)}, f32[768]{0:T(1024)}, u32[]{:S(2)}) copy-start(f32[768]{0:T(1024)} %copy-done.49) | copy-start | bytes 9220
  897.5 97.3 %copy-start.62 = (f32[512]{0:T(512)S(1)}, f32[512]{0:T(512)}, u32[]{:S(2)}) copy-start(f32[512]{0:T(512)} %copy-done.61) | copy-start | bytes 6148
  (69 other events, 249.2 us)
Sparse Core Ops, SparseCore 0:
  35.8 102.1 all-gather.4
  140.8 96.8 all-gather.2
  634.6 117.0 reduce-scatter.13
  755.1 117.2 reduce-scatter.31
  874.8 36.9 reduce-scatter.25
  914.2 37.7 reduce-scatter.27
  954.5 37.8 reduce-scatter.29
  998.6 114.9 reduce-scatter.19
  1119.9 113.8 reduce-scatter.21
  1239.8 113.9 reduce-scatter.23
  1359.7 98.5 reduce-scatter.17
  1464.3 118.5 reduce-scatter.15
where the time goes:
time: 1600 us; the launch traced here: 1590 us
  waiting for transfers between devices  1030 us (64%)
  matrix products  231 us (14%)
  local copies, waits for them, and re-layouts  169 us (11%)
  other arithmetic  84.5 us (5%)
  blocking collectives  40.3 us (3%)
  starting transfers between devices  18.7 us (1%)
    reduce_scatter x1, waiting for transfers between devices, on_device(): lax.psum_scatter(grad_w_qkv, ('dp', 'expert'), scatter_dimension=0, tiled...  125 us
    reduce_scatter x1, waiting for transfers between devices, on_device(): lax.psum_scatter(grad_shared_up, ('dp', 'expert'), scatter_dimension=0, t...  120 us
    reduce_scatter x1, waiting for transfers between devices, on_device(): lax.psum_scatter(grad_shared_down, ('dp', 'expert'), scatter_dimension=1,...  120 us
    unnamed x13, waiting for transfers between devices  116 us
    reduce_scatter x1, waiting for transfers between devices, on_device(): lax.psum_scatter(grad_w_out, ('dp', 'expert'), scatter_dimension=0, tiled...  104 us
    all_gather x1, waiting for transfers between devices, on_device(): lax.all_gather(value_send, 'expert', axis=1, tiled=True)  79.2 us
    all_gather x1, waiting for transfers between devices, on_device(): lax.all_gather(key_send, 'expert', axis=1, tiled=True)  77.3 us
    reduce_scatter x1, waiting for transfers between devices, on_device(): lax.psum_scatter(grad_shared_gate, ('dp', 'expert'), scatter_dimension=0,...  64.6 us
  transfers between devices with their start and end apart: 16, of which 15 were waited for; matrix products, arithmetic and copies ran while one was open for 18% of the time, Pallas kernels for 0%

commit v1 on v0

v1 whole, which is shorter than its diff:
```python
import jax
import jax.numpy as jnp
from jax import lax
from jax.experimental import pallas as pl
from jax.experimental.pallas import tpu as pltpu
from jax.sharding import Mesh
from jax.sharding import PartitionSpec as P

HEAD_DIM = 64
EPS = 1e-06
BF = jnp.bfloat16
F32 = jnp.float32
NEG = -1e30
NN = (((1,), (0,)), ((), ()))
NT = (((1,), (1,)), ((), ()))
TN = (((0,), (0,)), ((), ()))
VMEM_MOST = 60 << 20


def mm(left, right, dims=NN):
    return lax.dot_general(left, right, dims, preferred_element_type=F32)


def sds(shape, dtype):
    return jax.ShapeDtypeStruct(shape, dtype)


def call(body, grid, in_specs, out_specs, out_shape, args, scratch=(), prefetch=0, flops=0):
    leaves = jax.tree.leaves(out_shape)
    moved = sum(a.size * a.dtype.itemsize for a in args) + sum(
        a.size * a.dtype.itemsize for a in leaves
    )
    return pl.pallas_call(
        body,
        out_shape=out_shape,
        grid_spec=pltpu.PrefetchScalarGridSpec(
            num_scalar_prefetch=prefetch,
            grid=grid,
            in_specs=in_specs,
            out_specs=out_specs,
            scratch_shapes=list(scratch),
        ),
        compiler_params=pltpu.CompilerParams(
            dimension_semantics=("arbitrary",) * len(grid), vmem_limit_bytes=VMEM_MOST
        ),
        cost_estimate=pl.CostEstimate(
            flops=int(flops), transcendentals=0, bytes_accessed=int(moved)
        ),
    )(*args)


def whole(shape):
    rank = len(shape)
    return pl.BlockSpec(tuple(shape), lambda *_: (0,) * rank)


def swap_halves(value):
    lane = lax.broadcasted_iota(jnp.int32, value.shape, 1)
    return jnp.where(lane % 64 < 32, pltpu.roll(value, 96, 1), pltpu.roll(value, 32, 1))


def rms(values):
    return lax.rsqrt(jnp.mean(values * values, axis=1, keepdims=True) + EPS)


def project(rows, gain, weight, cosine, sine):
    parts, blocks, span, width = rows.shape
    cols = weight.shape[1]
    group = cols // 3
    height = parts * span
    length = height * blocks

    def body(r_ref, g_ref, w_ref, c_ref, s_ref, qkv_ref, n_ref):
        tok = r_ref[...].reshape(height, width).astype(F32)
        normed = (tok * rms(tok) * g_ref[...]).astype(BF)
        n_ref[...] = normed
        proj = mm(normed, w_ref[...])
        for at in range(0, 2 * group, 128):
            part = proj[:, at : at + 128]
            lane = lax.broadcasted_iota(jnp.int32, part.shape, 1) + at
            turned = part * c_ref[...] + swap_halves(part) * s_ref[...]
            turned = turned * jnp.where(lane < group, HEAD_DIM**-0.5, 1.0)
            qkv_ref[:, at : at + 128] = turned.astype(BF)
        qkv_ref[:, 2 * group :] = proj[:, 2 * group :].astype(BF)

    return call(
        body,
        (blocks,),
        [
            pl.BlockSpec((parts, 1, span, width), lambda i: (0, i, 0, 0)),
            whole((1, width)),
            whole((width, cols)),
            pl.BlockSpec((height, 128), lambda i: (i, 0)),
            pl.BlockSpec((height, 128), lambda i: (i, 0)),
        ],
        [
            pl.BlockSpec((height, cols), lambda i: (i, 0)),
            pl.BlockSpec((height, width), lambda i: (i, 0)),
        ],
        [sds((length, cols), BF), sds((length, width), BF)],
        (rows, gain, weight, cosine, sine),
        flops=2 * length * width * cols,
    )


def project_back(grads, weight, rows, gain):
    parts, blocks, span, width = rows.shape
    group = grads[0].shape[1]
    height = parts * span
    length = height * blocks

    def body(q_ref, k_ref, v_ref, w_ref, r_ref, out_ref, gain_ref, acc_ref):
        step = pl.program_id(0)
        back = mm(q_ref[...], w_ref[:, :group], NT)
        back += mm(k_ref[...], w_ref[:, group : 2 * group], NT)
        back += mm(v_ref[...], w_ref[:, 2 * group :], NT)
        tok = r_ref[...].reshape(height, width).astype(F32)
        part = jnp.sum(back * tok * rms(tok), axis=0, keepdims=True)

        @pl.when(step == 0)
        def _():
            acc_ref[...] = jnp.zeros_like(acc_ref)

        acc_ref[...] += jnp.broadcast_to(part, acc_ref.shape)
        out_ref[...] = back.astype(BF).reshape(parts, 1, span, width)

        @pl.when(step == blocks - 1)
        def _():
            column = jnp.transpose(acc_ref[...])
            gain_ref[...] = jnp.broadcast_to(column[:, :1], gain_ref.shape)

    block = pl.BlockSpec((height, group), lambda i: (i, 0))
    return call(
        body,
        (blocks,),
        [
            block,
            block,
            block,
            whole(weight.shape),
            pl.BlockSpec((parts, 1, span, width), lambda i: (0, i, 0, 0)),
        ],
        [
            pl.BlockSpec((parts, 1, span, width), lambda i: (0, i, 0, 0)),
            whole((width, 128)),
        ],
        [sds((parts, blocks, span, width), BF), sds((width, 128), F32)],
        (*grads, weight, rows),
        scratch=[pltpu.VMEM((8, width), F32)],
        flops=6 * length * width * group,
    )


def attend(qkv, seg_row, seg_col):
    length, cols = qkv.shape
    group = cols // 3
    pairs = group // 128
    high = min(256, length)

    def body(q_ref, k_ref, v_ref, sr_ref, sc_ref, o_ref, l_ref):
        lane = lax.broadcasted_iota(jnp.int32, (high, 128), 1)
        for at in range(0, length, high):
            end = at + high
            query = q_ref[at:end, :]
            keys = k_ref[:end, :]
            vals = v_ref[:end, :]
            q_pos = lax.broadcasted_iota(jnp.int32, (high, end), 0) + at
            k_pos = lax.broadcasted_iota(jnp.int32, (high, end), 1)
            allowed = (sc_ref[at:end, :] == sr_ref[:, :end]) & (k_pos <= q_pos)
            outs = []
            for head in range(2):
                mine = (lane // 64) == head
                scores = mm(jnp.where(mine, query, jnp.zeros_like(query)), keys, NT)
                scores = jnp.where(allowed, scores, NEG)
                most = jnp.max(scores, axis=1, keepdims=True)
                expo = jnp.exp(scores - most)
                total = jnp.sum(expo, axis=1, keepdims=True)
                outs.append(mm(expo.astype(BF), vals) / total)
                lse = jnp.broadcast_to(most + jnp.log(total), (high, 128))
                l_ref[0, head : head + 1, at:end] = jnp.transpose(lse)[:1, :]
            o_ref[at:end, :] = jnp.where(lane < 64, outs[0], outs[1]).astype(BF)

    def col(offset):
        return pl.BlockSpec((length, 128), lambda i: (0, offset * pairs + i))

    return call(
        body,
        (pairs,),
        [col(0), col(1), col(2), whole((1, length)), whole((length, 1))],
        [col(0), pl.BlockSpec((1, 2, length), lambda i: (i, 0, 0))],
        [sds((length, group), BF), sds((pairs, 2, length), F32)],
        (qkv, qkv, qkv, seg_row, seg_col),
        flops=4 * length * length * group,
    )


def attend_back(qkv, grad, lse, seg_row, seg_col, cosine, sine):
    length, cols = qkv.shape
    group = cols // 3
    pairs = group // 128
    high = min(256, length)

    def body(
        q_ref, k_ref, v_ref, g_ref, l_ref, sr_ref, sc_ref, c_ref, s_ref, dq_ref, dk_ref, dv_ref,
        ka_ref, va_ref,
    ):
        lane = lax.broadcasted_iota(jnp.int32, (high, 128), 1)
        ka_ref[...] = jnp.zeros_like(ka_ref)
        va_ref[...] = jnp.zeros_like(va_ref)
        for at in range(0, length, high):
            end = at + high
            query = q_ref[at:end, :]
            grads = g_ref[at:end, :]
            keys = k_ref[:end, :]
            vals = v_ref[:end, :]
            k_pos = lax.broadcasted_iota(jnp.int32, (end, high), 0)
            q_pos = lax.broadcasted_iota(jnp.int32, (end, high), 1) + at
            allowed = (sc_ref[:end, :] == sr_ref[:, at:end]) & (k_pos <= q_pos)
            outs = []
            for head in range(2):
                mine = (lane // 64) == head
                q_own = jnp.where(mine, query, jnp.zeros_like(query))
                g_own = jnp.where(mine, grads, jnp.zeros_like(grads))
                scores = jnp.where(allowed, mm(keys, q_own, NT), NEG)
                probs = jnp.exp(scores - l_ref[0, head : head + 1, at:end])
                grad_probs = mm(vals, g_own, NT)
                delta = jnp.sum(probs * grad_probs, axis=0, keepdims=True)
                grad_scores = (probs * (grad_probs - delta)).astype(BF)
                va_ref[:end, :] += mm(probs.astype(BF), g_own)
                ka_ref[:end, :] += mm(grad_scores, q_own)
                outs.append(mm(grad_scores, keys, TN))
            found = jnp.where(lane < 64, outs[0], outs[1]) * HEAD_DIM**-0.5
            back = found * c_ref[at:end, :] - swap_halves(found) * s_ref[at:end, :]
            dq_ref[at:end, :] = back.astype(BF)
        found = ka_ref[...]
        dk_ref[...] = (found * c_ref[...] - swap_halves(found) * s_ref[...]).astype(BF)
        dv_ref[...] = va_ref[...].astype(BF)

    def col(offset):
        return pl.BlockSpec((length, 128), lambda i: (0, offset * pairs + i))

    return call(
        body,
        (pairs,),
        [
            col(0),
            col(1),
            col(2),
            col(0),
            pl.BlockSpec((1, 2, length), lambda i: (i, 0, 0)),
            whole((1, length)),
            whole((length, 1)),
            whole((length, 128)),
            whole((length, 128)),
        ],
        [col(0), col(0), col(0)],
        [sds((length, group), BF)] * 3,
        (qkv, qkv, qkv, grad, lse, seg_row, seg_col, cosine, sine),
        scratch=[pltpu.VMEM((length, 128), F32)] * 2,
        flops=10 * length * length * group,
    )


def heads_of(flat):
    return flat.reshape(flat.shape[0], -1, HEAD_DIM)


def plain_mask(seg_row, seg_col):
    length = seg_col.shape[0]
    spots = jnp.arange(length, dtype=jnp.int32)
    return (seg_row == seg_col) & (spots[None, :] <= spots[:, None])


def plain_attend(qkv, seg_row, seg_col):
    query, keys, vals = (heads_of(part) for part in jnp.split(qkv, 3, axis=1))
    scores = jnp.einsum("qhd,khd->hqk", query, keys, preferred_element_type=F32)
    scores = jnp.where(plain_mask(seg_row, seg_col)[None], scores, NEG)
    lse = jax.nn.logsumexp(scores, axis=-1, keepdims=True)
    probs = jnp.exp(scores - lse).astype(BF)
    found = jnp.einsum("hqk,khd->qhd", probs, vals, preferred_element_type=F32)
    return found.astype(BF).reshape(qkv.shape[0], -1), lse


def plain_turn_back(grads, cosine, sine):
    table_c, table_s = cosine[:, None, :HEAD_DIM], sine[:, None, :HEAD_DIM]
    swapped = jnp.roll(grads, HEAD_DIM // 2, axis=-1)
    return (grads * table_c - swapped * table_s).astype(BF).reshape(grads.shape[0], -1)


def plain_attend_back(qkv, grad, lse, seg_row, seg_col, cosine, sine):
    query, keys, vals = (heads_of(part) for part in jnp.split(qkv, 3, axis=1))
    grad = heads_of(grad)
    scores = jnp.einsum("qhd,khd->hqk", query, keys, preferred_element_type=F32)
    scores = jnp.where(plain_mask(seg_row, seg_col)[None], scores, NEG)
    probs = jnp.exp(scores - lse)
    grad_probs = jnp.einsum("qhd,khd->hqk", grad, vals, preferred_element_type=F32)
    delta = jnp.sum(probs * grad_probs, axis=-1, keepdims=True)
    grad_scores = (probs * (grad_probs - delta)).astype(BF)
    gq = jnp.einsum("hqk,khd->qhd", grad_scores, keys, preferred_element_type=F32)
    gk = jnp.einsum("hqk,qhd->khd", grad_scores, query, preferred_element_type=F32)
    gv = jnp.einsum("hqk,qhd->khd", probs.astype(BF), grad, preferred_element_type=F32)
    return (
        plain_turn_back(gq * HEAD_DIM**-0.5, cosine, sine),
        plain_turn_back(gk, cosine, sine),
        gv.astype(BF).reshape(qkv.shape[0], -1),
    )


def after_attention(tokens, attended, w_out, gain):
    seqs, parts, span, group = attended.shape
    count, width = tokens.shape

    def body(t_ref, a_ref, w_ref, g_ref, h_ref, b_ref):
        hidden = t_ref[...].astype(F32)
        for part in range(parts):
            rows = a_ref[:, part].reshape(count, group)
            hidden += mm(rows, w_ref[part * group : (part + 1) * group, :])
        h_ref[...] = hidden
        b_ref[...] = (hidden * rms(hidden) * g_ref[...]).astype(BF)

    return call(
        body,
        (1,),
        [whole(a.shape) for a in (tokens, attended, w_out, gain)],
        [whole(tokens.shape)] * 2,
        [sds(tokens.shape, F32), sds(tokens.shape, BF)],
        (tokens, attended, w_out, gain),
        flops=2 * count * width * width,
    )


def dispatch(rows, target_rows, experts, capacity):
    count, width = rows.shape

    def body(r_ref, t_ref, o_ref):
        slot = lax.broadcasted_iota(jnp.int32, (capacity, count), 0)
        slot += pl.program_id(0) * capacity
        hit = (slot == t_ref[0:1, :]) | (slot == t_ref[1:2, :])
        o_ref[0] = mm(hit.astype(F32).astype(BF), r_ref[...]).astype(BF)

    return call(
        body,
        (experts,),
        [whole(rows.shape), whole(target_rows.shape)],
        pl.BlockSpec((1, capacity, width), lambda i: (i, 0, 0)),
        sds((experts, capacity, width), BF),
        (rows, target_rows),
        flops=2 * experts * capacity * count * width,
    )


def pick(target, rows):
    spot = lax.broadcasted_iota(jnp.int32, (target.shape[0], rows.shape[0]), 1)
    hit = (spot == target[:, 0:1]) | (spot == target[:, 1:2])
    return mm(hit.astype(F32).astype(BF), rows)


def layer_end(hidden, shared_out, rows, target):
    count, width = hidden.shape
    high = count // 2

    def body(h_ref, s_ref, r_ref, t_ref, o_ref):
        o_ref[...] = (h_ref[...] + s_ref[...] + pick(t_ref[...], r_ref[...])).astype(BF)

    block = pl.BlockSpec((high, width), lambda i: (i, 0))
    return call(
        body,
        (2,),
        [block, block, whole(rows.shape), pl.BlockSpec((high, 2), lambda i: (i, 0))],
        block,
        sds(hidden.shape, BF),
        (hidden, shared_out, rows, target),
        flops=2 * count * width * rows.shape[0],
    )


def middle_back(hidden, grad_shared, rows, target, cotangent, gain, w_out, parts, span):
    count, width = hidden.shape
    seqs = count // span
    each = 2 if seqs % 2 == 0 else 1
    high = each * span
    steps = count // high
    group = width // parts

    def body(h_ref, s_ref, r_ref, t_ref, c_ref, g_ref, w_ref, gh_ref, ga_ref, d_ref, n_ref, acc_ref):
        step = pl.program_id(0)
        branch = s_ref[...] + pick(t_ref[...], r_ref[...])
        hidden = h_ref[...]
        scale = rms(hidden)
        weighted = branch * g_ref[...]
        inner = jnp.mean(weighted * hidden, axis=1, keepdims=True)
        part = jnp.sum(branch * hidden * scale, axis=0, keepdims=True)
        out = c_ref[...].astype(F32) + scale * weighted - hidden * (scale * scale * scale * inner)
        gh_ref[...] = out
        out = out.astype(BF)
        ga_ref[...] = out
        for at in range(parts):
            sent = mm(out, w_ref[at * group : (at + 1) * group, :], NT).astype(BF)
            d_ref[:, at] = sent.reshape(each, span, group)

        @pl.when(step == 0)
        def _():
            acc_ref[...] = jnp.zeros_like(acc_ref)

        acc_ref[...] += jnp.broadcast_to(part, acc_ref.shape)

        @pl.when(step == steps - 1)
        def _():
            column = jnp.transpose(acc_ref[...])
            n_ref[...] = jnp.broadcast_to(column[:, :1], n_ref.shape)

    block = pl.BlockSpec((high, width), lambda i: (i, 0))
    return call(
        body,
        (steps,),
        [
            block,
            block,
            whole(rows.shape),
            pl.BlockSpec((high, 2), lambda i: (i, 0)),
            block,
            whole(gain.shape),
            whole(w_out.shape),
        ],
        [
            block,
            block,
            pl.BlockSpec((each, parts, span, group), lambda i: (i, 0, 0, 0)),
            whole((width, 128)),
        ],
        [
            sds(hidden.shape, F32),
            sds(hidden.shape, BF),
            sds((seqs, parts, span, group), BF),
            sds((width, 128), F32),
        ],
        (hidden, grad_shared, rows, target, cotangent, gain, w_out),
        scratch=[pltpu.VMEM((8, width), F32)],
        flops=2 * count * width * (rows.shape[0] + width),
    )


def first_norm_back(tokens, gain, grad_normed, grad_hidden):
    count, width = tokens.shape
    high = count // 2

    def body(t_ref, g_ref, n_ref, h_ref, o_ref):
        tok = t_ref[...].astype(F32)
        scale = rms(tok)
        weighted = n_ref[...].astype(F32) * g_ref[...]
        inner = jnp.mean(weighted * tok, axis=1, keepdims=True)
        out = h_ref[...] + scale * weighted - tok * (scale * scale * scale * inner)
        o_ref[...] = out.astype(BF)

    block = pl.BlockSpec((high, width), lambda i: (i, 0))
    return call(
        body,
        (2,),
        [block, whole(gain.shape), block, block],
        block,
        sds(tokens.shape, BF),
        (tokens, gain, grad_normed, grad_hidden),
    )


def feed_forward(rows, grads, w_gate, w_up, w_down, router=None, other=None, own=None):
    count, width = rows.shape
    units = w_gate.shape[1]
    wide = 512
    steps = units // wide
    high = 256
    gated = router is not None
    kind = BF if gated else F32

    def body(*refs):
        if gated:
            (own_ref, x_ref, g_ref, wg_ref, wu_ref, wd_ref, wr_ref, ot_ref,
             y_ref, gi_ref, hid_ref, dg_ref, du_ref, eo_ref, gl_ref, ya_ref, ga_ref, gate_ref) = refs
        else:
            (x_ref, g_ref, wg_ref, wu_ref, wd_ref,
             y_ref, gi_ref, hid_ref, dg_ref, du_ref, ya_ref, ga_ref) = refs
        step = pl.program_id(0)

        if gated:

            @pl.when(step == 0)
            def _():
                logits = mm(x_ref[...], wr_ref[...])
                lane = lax.broadcasted_iota(jnp.int32, logits.shape, 1)
                mine = jnp.sum(jnp.where(lane == own_ref[0], logits, 0.0), axis=1, keepdims=True)
                theirs = jnp.sum(jnp.where(lane == ot_ref[...], logits, 0.0), axis=1, keepdims=True)
                gate = 1.0 / (1.0 + jnp.exp(theirs - mine))
                rest = 1.0 / (1.0 + jnp.exp(mine - theirs))
                gate_ref[:, 0:1] = gate
                gate_ref[:, 1:2] = rest
                eo_ref[...] = (g_ref[...].astype(F32) * gate).astype(BF)

        def rows_at(index, carry):
            at = pl.ds(pl.multiple_of(index * high, high), high)
            row = x_ref[at, :]
            grad = eo_ref[at, :] if gated else g_ref[at, :]
            gval = mm(row, wg_ref[...])
            uval = mm(row, wu_ref[...])
            sigma = 1.0 / (1.0 + jnp.exp(-gval))
            silu = gval * sigma
            hid = (silu * uval).astype(BF)
            hid_ref[at, :] = hid
            grad_hid = mm(grad, wd_ref[...], NT)
            du = (grad_hid * silu).astype(BF)
            dg = (grad_hid * uval * sigma * (1.0 + gval * (1.0 - sigma))).astype(BF)
            du_ref[at, :] = du
            dg_ref[at, :] = dg
            out = mm(hid, wd_ref[...])
            back = mm(dg, wg_ref[...], NT) + mm(du, wu_ref[...], NT)

            @pl.when(step == 0)
            def _():
                ya_ref[at, :] = out
                ga_ref[at, :] = back

            @pl.when(step > 0)
            def _():
                ya_ref[at, :] += out
                ga_ref[at, :] += back

            return carry

        lax.fori_loop(0, count // high, rows_at, 0)

        @pl.when(step == steps - 1)
        def _():
            if gated:
                out = ya_ref[...]
                gate = gate_ref[:, 0:1]
                lean = jnp.sum(out * g_ref[...].astype(F32), axis=1, keepdims=True)
                lean = lean * gate * gate_ref[:, 1:2]
                lane = lax.broadcasted_iota(jnp.int32, (count, 128), 1)
                sign = (lane == own_ref[0]).astype(F32) - (lane == ot_ref[...]).astype(F32)
                grad_logits = (lean * sign).astype(BF)
                gl_ref[...] = grad_logits
                y_ref[...] = (out * gate).astype(BF)
                gi_ref[...] = (ga_ref[...] + mm(grad_logits, wr_ref[...], NT)).astype(BF)
            else:
                y_ref[...] = ya_ref[...]
                gi_ref[...] = ga_ref[...]

    full = whole((count, width))
    hidden = pl.BlockSpec((count, wide), lambda i, *_: (0, i))
    in_specs = [
        full,
        full,
        pl.BlockSpec((width, wide), lambda i, *_: (0, i)),
        pl.BlockSpec((width, wide), lambda i, *_: (0, i)),
        pl.BlockSpec((wide, width), lambda i, *_: (i, 0)),
    ]
    out_specs = [full, full, hidden, hidden, hidden]
    out_shape = [sds((count, width), kind)] * 2 + [sds((count, units), BF)] * 3
    scratch = [pltpu.VMEM((count, width), F32)] * 2
    args = [rows, grads, w_gate, w_up, w_down]
    if gated:
        in_specs += [whole(router.shape), whole(other.shape)]
        out_specs += [full, whole((count, 128))]
        out_shape += [sds((count, width), BF), sds((count, 128), BF)]
        scratch += [pltpu.VMEM((count, 128), F32)]
        args = [own, *args, router, other]
    return call(
        body,
        (steps,),
        in_specs,
        out_specs,
        out_shape,
        tuple(args),
        scratch=scratch,
        prefetch=1 if gated else 0,
        flops=12 * count * width * units,
    )


def expert_weight_grads(rows, grads, dg, du, hid, grad_logits, sizes):
    outer, cores = sizes["y"], sizes["core"]
    count, width = rows.shape
    units = dg.shape[1]
    wide = units // (outer * cores)

    def body(x_ref, g_ref, dg_ref, du_ref, hid_ref, gl_ref, o_ref, r_ref):
        o_ref[0, 0, 0] = mm(x_ref[...], dg_ref[...], TN).astype(BF)
        o_ref[0, 0, 1] = mm(x_ref[...], du_ref[...], TN).astype(BF)
        o_ref[0, 0, 2] = mm(g_ref[...], hid_ref[...], TN).astype(BF)

        @pl.when(pl.program_id(0) == 0)
        def _():
            r_ref[...] = mm(x_ref[...], gl_ref[...], TN)

    hidden = pl.BlockSpec((count, wide), lambda i: (0, i))
    return call(
        body,
        (outer * cores,),
        [whole(rows.shape), whole(grads.shape), hidden, hidden, hidden, whole(grad_logits.shape)],
        [
            pl.BlockSpec((1, 1, 3, width, wide), lambda i: (i % cores, i // cores, 0, 0, 0)),
            whole((width, 128)),
        ],
        [sds((cores, outer, 3, width, wide), BF), sds((width, 128), F32)],
        (rows, grads, dg, du, hid, grad_logits),
        flops=6 * count * width * units,
    )


def spread(value, sizes, names):
    order = ("y", "core", "z", "x")
    split = value.reshape(*(sizes[n] for n in order), -1, value.shape[-1])
    return jnp.transpose(split, (*(order.index(n) for n in names), 4, 5))


def spread_places(sizes, names):
    found = []
    for y in range(sizes["y"]):
        for core in range(sizes["core"]):
            for z in range(sizes["z"]):
                for x in range(sizes["x"]):
                    at = {"y": y, "core": core, "z": z, "x": x}
                    found.append(tuple(at[n] for n in names))
    return found


def spread_shape(sizes, names):
    return tuple(sizes[n] for n in names)


def shared_weight_grads(rows, grads, dg, du, hid, sizes):
    names = ("core", "y", "x", "z")
    lead = spread_shape(sizes, names)
    places = spread_places(sizes, names)
    count, width = rows.shape
    units = dg.shape[1]
    wide = 512
    each = width // len(places)
    direct = each % 8 == 0

    def body(x_ref, g_ref, dg_ref, du_ref, hid_ref, o_ref):
        pairs = ((x_ref, dg_ref), (x_ref, du_ref), (g_ref, hid_ref))
        for index, (left, right) in enumerate(pairs):
            found = mm(left[...], right[...], TN)
            if direct:
                for at, place in enumerate(places):
                    o_ref[(*place, index)] = found[at * each : (at + 1) * each].astype(BF)
            else:
                o_ref[index] = found.astype(BF)

    hidden = pl.BlockSpec((count, wide), lambda i: (0, i))
    if direct:
        shape = (*lead, 3, each, units)
        spec = pl.BlockSpec((*lead, 3, each, wide), lambda i: (0,) * 6 + (i,))
    else:
        shape = (3, width, units)
        spec = pl.BlockSpec((3, width, wide), lambda i: (0, 0, i))
    out = call(
        body,
        (units // wide,),
        [whole(rows.shape), whole(grads.shape), hidden, hidden, hidden],
        spec,
        sds(shape, BF),
        (rows, grads, dg, du, hid),
        flops=6 * count * width * units,
    )
    if direct:
        return out
    return jnp.stack([spread(out[i], sizes, names) for i in range(3)], axis=4)


def tall_weight_grads(lefts, rights, extras, sizes, names):
    lead = spread_shape(sizes, names)
    places = spread_places(sizes, names)
    width = sum(left.shape[1] for left in lefts)
    cols = sum(right.shape[1] for right in rights)
    each = width // len(places)
    direct = each % 8 == 0
    flops = 2 * lefts[0].shape[0] * width * cols

    def body(*refs):
        left_refs = refs[: len(lefts)]
        right_refs = refs[len(lefts) : len(lefts) + len(rights)]
        extra_refs = refs[len(lefts) + len(rights) : -1]
        out_ref = refs[-1]

        def store(row, found, col):
            span = found.shape[1]
            if not direct:
                out_ref[row : row + found.shape[0], col : col + span] = found.astype(BF)
                return
            for at in range(found.shape[0] // each):
                place = places[row // each + at]
                piece = found[at * each : (at + 1) * each].astype(BF)
                out_ref[(*place, slice(None), slice(col, col + span))] = piece

        row = 0
        for left in left_refs:
            col = 0
            for right in right_refs:
                store(row, mm(left[...], right[...], TN), col)
                col += right.shape[1]
            row += left.shape[1]
        more = extra_refs[0][...]
        for extra in extra_refs[1:]:
            more = more + extra[...]
        store(0, more, cols)

    args = (*lefts, *rights, *extras)
    shape = (*lead, each, cols + 128) if direct else (width, cols + 128)
    out = call(
        body,
        (1,),
        [whole(a.shape) for a in args],
        whole(shape),
        sds(shape, BF),
        args,
        flops=flops,
    )
    return out if direct else spread(out, sizes, names)


def scatter_sum(value, name):
    return lax.psum_scatter(value, name, scatter_dimension=0, tiled=False)


def swap_all(value, names):
    return lax.all_to_all(value, names, 0, 0, tiled=True)


def on_device(
    tokens,
    segments,
    routes,
    slots,
    cotangent,
    attn_gain,
    w_qkv,
    w_out,
    ffn_gain,
    w_router,
    shared_gate,
    shared_up,
    shared_down,
    expert_gate,
    expert_up,
    expert_down,
):
    sizes = {name: lax.axis_size(name) for name in ("y", "core", "z", "x")}
    ranks = ("z", "x")
    seqs, span, width = tokens.shape
    blocks, parts = sizes["z"], sizes["x"]
    experts = blocks * parts
    count = seqs * span
    capacity = 3 * count // experts
    length = span * experts
    group = width // parts
    z_at, x_at = lax.axis_index("z"), lax.axis_index("x")
    own = (z_at * parts + x_at).astype(jnp.int32).reshape(1)
    attn_scale = attn_gain.astype(F32).reshape(1, width)
    ffn_scale = ffn_gain.astype(F32).reshape(1, width)
    flat_tokens = tokens.reshape(count, width)
    flat_cot = cotangent.reshape(count, width)

    by_seq = swap_all(tokens, "z")
    if parts == 2:
        theirs = lax.ppermute(by_seq, "x", [(0, 1), (1, 0)])
        first = x_at == 0
        rows = jnp.stack([jnp.where(first, by_seq, theirs), jnp.where(first, theirs, by_seq)])
    else:
        rows = lax.all_gather(by_seq, "x", axis=0, tiled=False)

    route_rows = routes.reshape(count, 2)
    slot_rows = slots.reshape(count, 2)
    target = jnp.where(slot_rows >= 0, route_rows * capacity + slot_rows, -1)
    target_rows = jnp.transpose(target)
    grad_sent = dispatch(flat_cot, target_rows, experts, capacity)
    spots = jnp.where(target >= 0, target, experts * capacity).reshape(-1)
    other = (
        jnp.zeros((experts * capacity,), F32)
        .at[spots]
        .set(route_rows[:, ::-1].reshape(-1).astype(F32), mode="drop")
    )
    other = swap_all(other.reshape(experts, capacity), ranks)
    other = other.reshape(-1, 1).astype(jnp.int32)
    grad_rows = swap_all(grad_sent, ranks).reshape(-1, width)

    frequency = jnp.power(10000.0, -2.0 * jnp.arange(32, dtype=F32) / HEAD_DIM)
    angles = jnp.arange(length, dtype=jnp.int32).astype(F32)[:, None] * jnp.tile(frequency, 4)
    sign = jnp.where(jnp.arange(128) % 64 < 32, -1.0, 1.0)
    cosine, sine = jnp.cos(angles), jnp.sin(angles) * sign
    w_group = lax.dynamic_index_in_dim(
        w_qkv.reshape(width, 3, parts, group), x_at, 2, keepdims=False
    ).reshape(width, 3 * group)
    seg_row = lax.dynamic_slice_in_dim(segments, z_at, 1, 0)
    seg_col = seg_row.reshape(length, 1)
    qkv, normed = project(rows, attn_scale, w_group, cosine, sine)
    fused = group % 128 == 0
    attended, lse = (attend if fused else plain_attend)(qkv, seg_row, seg_col)
    attended = swap_all(attended.reshape(experts, span, group), ranks)
    attended = attended.reshape(seqs, parts, span, group)

    hidden, branch_in = after_attention(flat_tokens, attended, w_out, ffn_scale)
    sent = dispatch(branch_in, target_rows, experts, capacity)
    received = swap_all(sent, ranks).reshape(-1, width)

    shared_out, shared_back, hid, dg, du = feed_forward(
        branch_in, flat_cot, shared_gate, shared_up, shared_down
    )
    shared_sums = shared_weight_grads(branch_in, flat_cot, dg, du, hid, sizes)
    for name in ("core", "y", "x", "z"):
        shared_sums = scatter_sum(shared_sums, name)

    router = jnp.pad(w_router, ((0, 0), (0, 128 - experts)))
    made, made_back, hid, dg, du, gated_grads, grad_logits = feed_forward(
        received, grad_rows, expert_gate[0], expert_up[0], expert_down[0], router, other, own
    )
    back_rows = swap_all(made_back.reshape(experts, capacity, width), ranks).reshape(-1, width)
    made_rows = swap_all(made.reshape(experts, capacity, width), ranks).reshape(-1, width)
    expert_sums, grad_router = expert_weight_grads(
        received, gated_grads, dg, du, hid, grad_logits, sizes
    )
    for name in ("core", "y"):
        expert_sums = scatter_sum(expert_sums, name)
    layer_out = layer_end(hidden, shared_out, made_rows, target).reshape(tokens.shape)

    grad_hidden, grad_attn, grad_att, grad_ffn = middle_back(
        hidden, shared_back, back_rows, target, flat_cot, ffn_scale, w_out, parts, span
    )
    grad_att = swap_all(grad_att.reshape(experts, span, group), ranks).reshape(length, group)

    column = lax.broadcasted_iota(jnp.int32, (width, 128), 1)
    small = jnp.where(column < experts, grad_router, jnp.where(column == experts, grad_ffn, 0.0))
    out_sums = tall_weight_grads(
        [attended[:, part].reshape(count, group) for part in range(parts)],
        [grad_attn],
        [small],
        sizes,
        ("core", "y", "x", "z"),
    )
    for name in ("core", "y", "x", "z"):
        out_sums = scatter_sum(out_sums, name)

    grads = (attend_back if fused else plain_attend_back)(
        qkv, grad_att, lse, seg_row, seg_col, cosine, sine
    )
    normed_back, grad_gain = project_back(grads, w_group, rows, attn_scale)
    if parts == 2:
        keep = lax.dynamic_index_in_dim(normed_back, x_at, 0, keepdims=False)
        give = lax.dynamic_index_in_dim(normed_back, 1 - x_at, 0, keepdims=False)
        got = lax.ppermute(give, "x", [(0, 1), (1, 0)])
        normed_back = (keep.astype(F32) + got.astype(F32)).astype(BF)
    else:
        normed_back = scatter_sum(normed_back, "x")
    normed_back = swap_all(normed_back, "z").reshape(count, width)
    token_grad = first_norm_back(flat_tokens, attn_scale, normed_back, grad_hidden)

    qkv_sums = tall_weight_grads([normed], list(grads), [grad_gain], sizes, ("core", "y", "z", "x"))
    for name in ("core", "y", "z"):
        qkv_sums = scatter_sum(qkv_sums, name)
    qkv_sums = swap_all(qkv_sums, "x").astype(F32)
    grad_attn_gain = jnp.sum(qkv_sums[:, :, 3 * group], axis=0)
    each = qkv_sums.shape[1]
    grad_w_qkv = qkv_sums[:, :, : 3 * group].reshape(parts, each, 3, group)
    grad_w_qkv = jnp.transpose(grad_w_qkv, (1, 2, 0, 3)).reshape(each, 3 * width)

    out_sums = out_sums.astype(F32)
    shared_sums = shared_sums.astype(F32)
    expert_sums = expert_sums.astype(F32)
    return (
        layer_out,
        token_grad.reshape(tokens.shape),
        grad_attn_gain,
        grad_w_qkv,
        out_sums[:, :width],
        out_sums[:, width + experts],
        out_sums[:, width : width + experts],
        shared_sums[0],
        shared_sums[1],
        jnp.transpose(shared_sums[2]),
        expert_sums[0][None],
        expert_sums[1][None],
        jnp.transpose(expert_sums[2])[None],
    )


def solution(mesh):
    dp, experts = mesh.shape["dp"], mesh.shape["expert"]

    def step(*args):
        seqs = args[0].shape[0] // dp
        cores = 2 if dp % 2 == 0 else 1
        fine = Mesh(
            mesh.devices.reshape(dp // cores, cores, seqs, experts // seqs),
            ("y", "core", "z", "x"),
        )
        data, ranks, every = ("y", "core"), ("z", "x"), ("y", "core", "z", "x")
        placed = (
            P(data, ranks, None),
            P(data, None),
            P(data, ranks, None),
            P(data, ranks, None),
            P(data, ranks, None),
            *([P()] * 8),
            P(ranks, None, None),
            P(ranks, None, None),
            P(ranks, None, None),
        )
        return jax.shard_map(
            on_device,
            mesh=fine,
            in_specs=placed,
            out_specs=(
                P(data, ranks, None),
                P(data, ranks, None),
                P(every),
                P(every, None),
                P(every, None),
                P(every),
                P(every, None),
                P(every, None),
                P(every, None),
                P(None, every),
                P(ranks, None, data),
                P(ranks, None, data),
                P(ranks, data, None),
            ),
            check_vma=False,
        )(*args)

    return step
```

time: 1600 us -> 783 us (0.49)
  waiting for transfers between devices: 1030 us -> 451 us
  matrix products: 231 us -> 0 us
  Pallas kernels: 0 us -> 188 us
  local copies, waits for them, and re-layouts: 169 us -> 40.8 us
  other arithmetic: 84.5 us -> 16.2 us
  blocking collectives: 40.3 us -> 0 us
  starting transfers between devices: 18.7 us -> 58.1 us
    reduce_scatter x9 -> x12, waiting for transfers between devices: 624 us -> 285 us  [scatter_sum(): return lax.psum_scatter(value, name, scatter_dimension=0, tiled=False)]
    dot_general x45 -> x0, matrix products: 231 us -> none  [the longest x1 21.6 us: on_device(): jnp.einsum('necd,edf->necf', received, expert_gate, preferred_element_typ...]
    pallas_call x0 -> x16, Pallas kernels: none -> 188 us  [call(): pl.pallas_call(body, out_shape=out_shape, grid_spec=pltpu.PrefetchScalarG...]
    all_gather x2 -> x0, waiting for transfers between devices: 156 us -> none  [the longest x1 79.2 us: on_device(): lax.all_gather(value_send, 'expert', axis=1, tiled=True)]
    unnamed x13 -> x14, waiting for transfers between devices: 116 us -> 2.51 us
    gather x5 -> x0, local copies, waits for them, and re-layouts: 43.1 us -> none  [the longest x1 11.9 us: on_device(): gate_pad[buffer_row][:, None] * grad_pad[buffer_tok]]
    unnamed x1 -> x0, blocking collectives: 40.3 us -> none
    unnamed x179 -> x44, local copies, waits for them, and re-layouts: 44.4 us -> 14.8 us
  transfers between devices with their start and end apart: 16 -> 25, of which waited for: 15 -> 18; matrix products, arithmetic and copies ran while one was open for 18% -> 6% of each run, Pallas kernels for 0% -> 16%
where the time goes in v1:
time: 783 us; the launch traced here: 769 us
  waiting for transfers between devices  451 us (58%)
  Pallas kernels  188 us (24%)
  starting transfers between devices  58.1 us (7%)
  local copies, waits for them, and re-layouts  40.8 us (5%)
  other arithmetic  16.2 us (2%)
  between operations  14.5 us (2%)
    reduce_scatter x12, waiting for transfers between devices, scatter_sum(): return lax.psum_scatter(value, name, scatter_dimension=0, tiled=False)  285 us
    pallas_call x16, Pallas kernels, call(): pl.pallas_call(body, out_shape=out_shape, grid_spec=pltpu.PrefetchScalarG...  188 us
    all_to_all x10, waiting for transfers between devices, swap_all(): return lax.all_to_all(value, names, 0, 0, tiled=True)  162 us
    all_to_all x10, starting transfers between devices, swap_all(): return lax.all_to_all(value, names, 0, 0, tiled=True)  44.6 us
  transfers between devices with their start and end apart: 25, of which 18 were waited for; matrix products, arithmetic and copies ran while one was open for 6% of the time, Pallas kernels for 16%

profile of v1, /device:TPU:0, one launch (start us, length us, event | category | flops | bytes accessed | tf_op | source)
XLA Modules:
  0.0 768.8 jit_solution(3825030205202691244)
XLA Ops:
  7.2 6.5 all-to-all-start
  21.3 12.6 %all-to-all-done = bf16[4,128,768]{2,1,0:T(8,128)(2,1)} async-done(((bf16[4,128,768]{2,1,0:T(8,128)(2,1)}), bf16[4,128,768]{2,1,0:T(8,128)(2,1)}, u32[]{:S(2)}, u32[]{:S(2)}) %all-to-all-start) | async-done | bytes 786464 | tf_op jit(solution)/shard_map/all_to_all | solution.py:727
  59.6 6.6 shard_map.255
  66.2 13.2 %shard_map.256 = (bf16[1024,384]{1,0:T(8,128)(2,1)}, f32[3,2,1024]{2,1,0:T(2,128)}) custom-call(bf16[1024,1152]{1,0:T(8,128)(2,1)} %get-tuple-element.42.q_ref.k_ref.v_ref, bf16[1024,1152]{1,0:T(8,128)(2,1)} %get-tuple-element.42.q_ref.k_ref.v_ref, bf16[1024,1152]{1,0:T(8,128)(2,1)} %get-tuple-element.42.q_ref.k_ref.v_ref, ...), custom_call_target="tpu_custom_call" | custom-call | flops 1610612736 | bytes 7897088 | tf_op jit(solution)/shard_map/pallas_call | solution.py:33
  79.4 5.5 all-to-all-start.1
  85.9 5.7 shard_map.260
  91.6 11.8 %all-to-all-done.1 = bf16[8,128,384]{2,1,0:T(8,128)(2,1)S(1)} async-done(((bf16[8,128,384]{2,1,0:T(8,128)(2,1)}), bf16[8,128,384]{2,1,0:T(8,128)(2,1)S(1)}, u32[]{:S(2)}, u32[]{:S(2)}) %all-to-all-start.1) | async-done | bytes 786464 | tf_op jit(solution)/shard_map/all_to_all | solution.py:727
  112.6 5.7 shard_map.259
  118.3 42.3 %all-to-all-done.3 = bf16[8,192,768]{2,1,0:T(8,128)(2,1)S(1)} async-done(((bf16[8,192,768]{2,1,0:T(8,128)(2,1)}), bf16[8,192,768]{2,1,0:T(8,128)(2,1)S(1)}, u32[]{:S(2)}, u32[]{:S(2)}) %all-to-all-start.3) | async-done | bytes 2359328 | tf_op jit(solution)/shard_map/all_to_all | solution.py:727
  169.1 50.8 %all-to-all-done.2 = bf16[8,192,768]{2,1,0:T(8,128)(2,1)S(1)} async-done(((bf16[8,192,768]{2,1,0:T(8,128)(2,1)}), bf16[8,192,768]{2,1,0:T(8,128)(2,1)S(1)}, u32[]{:S(2)}, u32[]{:S(2)}) %all-to-all-start.2) | async-done | bytes 2359328 | tf_op jit(solution)/shard_map/all_to_all | solution.py:727
  221.3 49.9 %shard_map.261 = (bf16[1536,768]{1,0:T(8,128)(2,1)}, bf16[1536,768]{1,0:T(8,128)(2,1)}, bf16[1536,2048]{1,0:T(8,128)(2,1)}, bf16[1536,2048]{1,0:T(8,128)(2,1)}, ...) custom-call(s32[1]{0:T(128)} %bitcast.9.refs_0_, bf16[1536,768]{1,0:T(8,128)(2,1)} %bitcast.94, ...), custom_call_target="tpu_custom_call" | custom-call | flops 28991029248 | bytes 40704004 | tf_op jit(solution)/shard_map/pallas_call | solution.py:33
  276.1 17.8 %shard_map.258 = (f32[512,768]{1,0:T(8,128)}, f32[512,768]{1,0:T(8,128)}, bf16[512,2048]{1,0:T(8,128)(2,1)}, bf16[512,2048]{1,0:T(8,128)(2,1)}, bf16[512,2048]{1,0:T(8,128)(2,1)}) custom-call(bf16[512,768]{1,0:T(8,128)(2,1)} %get-tuple-element.45.refs_0_.r_ref.x_ref, bf16[512,768]{1,0:T(8,128)(2,1)} %bitcast.104, bf16[768,2048]{1,0:T(8,128)(2,1)} %refs_2_.1, ...), custom_call_target="tpu_custom_call" | custom-call | flops 9663676416 | bytes 20447232 | tf_op jit(solution)/shard_map/pallas_call | solution.py:33
  293.9 22.3 %shard_map.268 = (bf16[2,2,3,768,512]{4,3,2,1,0:T(8,128)(2,1)}, f32[768,128]{1,0:T(8,128)}) custom-call(bf16[1536,768]{1,0:T(8,128)(2,1)} %bitcast.95, bf16[1536,768]{1,0:T(8,128)(2,1)} %get-tuple-element.60.g_ref, bf16[1536,2048]{1,0:T(8,128)(2,1)} %get-tuple-element.61.dg_ref, bf16[1536,2048]{1,0:T(8,128)(2,1)} %get-tuple-element.62.du_ref, ...), custom_call_target="tpu_custom_call" | custom-call | flops 14495514624 | bytes 33816576 | tf_op jit(solution)/shard_map/pallas_call | solution.py:33
  316.1 12.9 %all-to-all-done.6 = bf16[8,192,768]{2,1,0:T(8,128)(2,1)S(1)} async-done(((bf16[8,192,768]{2,1,0:T(8,128)(2,1)}), bf16[8,192,768]{2,1,0:T(8,128)(2,1)S(1)}, u32[]{:S(2)}, u32[]{:S(2)}) %all-to-all-start.6) | async-done | bytes 2359328 | tf_op jit(solution)/shard_map/all_to_all | solution.py:727
  330.4 8.4 %shard_map.263 = (f32[512,768]{1,0:T(8,128)}, bf16[512,768]{1,0:T(8,128)(2,1)}, bf16[4,2,128,384]{3,2,1,0:T(8,128)(2,1)}, f32[768,128]{1,0:T(8,128)}) custom-call(f32[512,768]{1,0:T(8,128)} %get-tuple-element.44.h_ref, f32[512,768]{1,0:T(8,128)} %get-tuple-element.48.s_ref, bf16[1536,768]{1,0:T(8,128)(2,1)} %bitcast.80, s32[512,2]{1,0:T(8,128)} %copy-done.6, ...), custom_call_target="tpu_custom_call" | custom-call | flops 1811939328 | bytes 11017216 | tf_op jit(solution)/shard_map/pallas_call | solution.py:33
  344.2 10.3 %shard_map.270 = bf16[2,2,2,4,3,24,2048]{6,5,4,3,2,1,0:T(8,128)(2,1)} custom-call(bf16[512,768]{1,0:T(8,128)(2,1)} %get-tuple-element.45.refs_0_.r_ref.x_ref, bf16[512,768]{1,0:T(8,128)(2,1)} %bitcast.106, bf16[512,2048]{1,0:T(8,128)(2,1)} %get-tuple-element.67.dg_ref, bf16[512,2048]{1,0:T(8,128)(2,1)} %get-tuple-element.68.du_ref, ...), custom_call_target="tpu_custom_call" | custom-call | flops 4831838208 | bytes 17301504 | tf_op jit(solution)/shard_map/pallas_call | solution.py:33
  358.8 9.2 %reduce-scatter.16.cloned.1.call-start = ((), (), s32[]{:S(2)}) async-start(), calls=%async_computation.23 | async-start | bytes 2949120 | tf_op jit(solution)/shard_map/reduce_scatter | solution.py:723
  368.0 10.5 %all-to-all-done.7 = bf16[8,128,384]{2,1,0:T(8,128)(2,1)S(1)} async-done(((bf16[8,128,384]{2,1,0:T(8,128)(2,1)}), bf16[8,128,384]{2,1,0:T(8,128)(2,1)S(1)}, u32[]{:S(2)}, u32[]{:S(2)}) %all-to-all-start.7) | async-done | bytes 786464 | tf_op jit(solution)/shard_map/all_to_all | solution.py:727
  379.3 18.9 %shard_map.264 = (bf16[1024,384]{1,0:T(8,128)(2,1)}, bf16[1024,384]{1,0:T(8,128)(2,1)}, bf16[1024,384]{1,0:T(8,128)(2,1)}) custom-call(bf16[1024,1152]{1,0:T(8,128)(2,1)} %get-tuple-element.42.q_ref.k_ref.v_ref, bf16[1024,1152]{1,0:T(8,128)(2,1)} %get-tuple-element.42.q_ref.k_ref.v_ref, bf16[1024,1152]{1,0:T(8,128)(2,1)} %get-tuple-element.42.q_ref.k_ref.v_ref, ...), custom_call_target="tpu_custom_call" | custom-call | flops 4026531840 | bytes 11304960 | tf_op jit(solution)/shard_map/pallas_call | solution.py:33
  398.2 7.2 shard_map.265
  405.4 6.1 shard_map.267
  412.7 7.5 reduce-scatter.16.cloned.1.call-done
  421.1 62.7 %reduce-scatter.30.cloned.1.call-done = bf16[1,2,4,3,24,2048]{5,4,3,2,1,0:T(8,128)(2,1)} async-done(((bf16[2,2,4,3,24,2048]{5,4,3,2,1,0:T(8,128)(2,1)}), bf16[1,2,4,3,24,2048]{5,4,3,2,1,0:T(8,128)(2,1)}) %reduce-scatter.30.cloned.1.call-update) | async-done | bytes 2359312 | tf_op jit(solution)/shard_map/reduce_scatter | solution.py:723
  483.9 14.7 %reduce-scatter.26.cloned.1.call-done = bf16[1,4,24,896]{3,2,1,0:T(8,128)(2,1)} async-done(((bf16[2,4,24,896]{3,2,1,0:T(8,128)(2,1)}), bf16[1,4,24,896]{3,2,1,0:T(8,128)(2,1)}) %reduce-scatter.26.cloned.1.call-update) | async-done | bytes 172048 | tf_op jit(solution)/shard_map/reduce_scatter | solution.py:723
  498.7 21.9 %reduce-scatter.18.cloned.1.call-done = bf16[1,4,2,24,1280]{4,3,2,1,0:T(8,128)(2,1)} async-done(((bf16[2,4,2,24,1280]{4,3,2,1,0:T(8,128)(2,1)}), bf16[1,4,2,24,1280]{4,3,2,1,0:T(8,128)(2,1)}) %reduce-scatter.18.cloned.1.call-update) | async-done | bytes 491536 | tf_op jit(solution)/shard_map/reduce_scatter | solution.py:723
  520.6 19.5 %reduce-scatter.36.cloned.1.call-done = bf16[1,2,3,768,512]{4,3,2,1,0:T(8,128)(2,1)} async-done(((bf16[2,2,3,768,512]{4,3,2,1,0:T(8,128)(2,1)}), bf16[1,2,3,768,512]{4,3,2,1,0:T(8,128)(2,1)}) %reduce-scatter.36.cloned.1.call-update) | async-done | bytes 4718608 | tf_op jit(solution)/shard_map/reduce_scatter | solution.py:723
  540.1 5.9 all-to-all-start.5
  550.1 67.6 %reduce-scatter.32.cloned.1.call-done = bf16[1,4,3,24,2048]{4,3,2,1,0:T(8,128)(2,1)} async-done(((bf16[2,4,3,24,2048]{4,3,2,1,0:T(8,128)(2,1)}), bf16[1,4,3,24,2048]{4,3,2,1,0:T(8,128)(2,1)}) %reduce-scatter.32.cloned.1.call-update) | async-done | bytes 1179664 | tf_op jit(solution)/shard_map/reduce_scatter | solution.py:723
  629.6 17.9 %all-to-all-done.8 = bf16[4,128,768]{2,1,0:T(8,128)(2,1)S(1)} async-done(((bf16[4,128,768]{2,1,0:T(8,128)(2,1)}), bf16[4,128,768]{2,1,0:T(8,128)(2,1)S(1)}, u32[]{:S(2)}, u32[]{:S(2)}) %all-to-all-start.8) | async-done | bytes 786464 | tf_op jit(solution)/shard_map/all_to_all | solution.py:727
  653.4 14.8 %reduce-scatter.20.cloned.1.call-done = bf16[1,2,24,1280]{3,2,1,0:T(8,128)(2,1)} async-done(((bf16[4,2,24,1280]{3,2,1,0:T(8,128)(2,1)}), bf16[1,2,24,1280]{3,2,1,0:T(8,128)(2,1)}) %reduce-scatter.20.cloned.1.call-update) | async-done | bytes 122896 | tf_op jit(solution)/shard_map/reduce_scatter | solution.py:723
  677.7 50.8 %reduce-scatter.38.cloned.1.call-done = bf16[1,3,768,512]{3,2,1,0:T(8,128)(2,1)} async-done(((bf16[2,3,768,512]{3,2,1,0:T(8,128)(2,1)}), bf16[1,3,768,512]{3,2,1,0:T(8,128)(2,1)}) %reduce-scatter.38.cloned.1.call-update) | async-done | bytes 2359312 | tf_op jit(solution)/shard_map/reduce_scatter | solution.py:723
  734.7 25.6 %reduce-scatter.34.cloned.1.call-done = bf16[1,3,24,2048]{3,2,1,0:T(8,128)(2,1)} async-done(((bf16[4,3,24,2048]{3,2,1,0:T(8,128)(2,1)}), bf16[1,3,24,2048]{3,2,1,0:T(8,128)(2,1)}) %reduce-scatter.34.cloned.1.call-update) | async-done | bytes 294928 | tf_op jit(solution)/shard_map/reduce_scatter | solution.py:723
  (139 shorter events, 111.5 us)
Async XLA Ops:
  7.2 33.2 %copy-start.17 = (bf16[768]{0:T(1024)(128)(2,1)S(1)}, bf16[768]{0:T(1024)(128)(2,1)}, u32[]{:S(2)}) copy-start(bf16[768]{0:T(1024)(128)(2,1)} %param.21) | copy-start | bytes 4612
  7.2 26.7 %all-to-all-start = ((bf16[4,128,768]{2,1,0:T(8,128)(2,1)}), bf16[4,128,768]{2,1,0:T(8,128)(2,1)}, u32[]{:S(2)}, u32[]{:S(2)}) async-start(bf16[4,128,768]{2,1,0:T(8,128)(2,1)} %param.16), calls=%async_computation | async-start | bytes 1572864 | tf_op jit(solution)/shard_map/all_to_all | solution.py:727
  14.5 26.4 %copy-start.8 = (s32[4,128,2]{2,1,0:T(8,128)}, s32[4,128,2]{2,1,0:T(8,128)S(1)}, u32[]{:S(2)}) copy-start(s32[4,128,2]{2,1,0:T(8,128)S(1)} %copy.70) | copy-start | bytes 12292
  33.9 45.5 %all-to-all-start.4 = ((f32[8,1,192]{2,1,0:T(1,128)}), f32[8,1,192]{2,1,0:T(1,128)}, u32[]{:S(2)}, u32[]{:S(2)}) async-start(f32[8,1,192]{2,1,0:T(1,128)} %all_to_all.37), calls=%async_computation.4 | async-start | bytes 16384 | tf_op jit(solution)/shard_map/all_to_all | solution.py:727
  37.9 19.0 %collective-permute-start = (bf16[4,128,768]{2,1,0:T(8,128)(2,1)}, bf16[4,128,768]{2,1,0:T(8,128)(2,1)}, u32[]{:S(2)}, u32[]{:S(2)}) collective-permute-start(bf16[4,128,768]{2,1,0:T(8,128)(2,1)} %all-to-all-done), channel_id=1, source_target_pairs={{0,1},{1,0},{2,3},{3,2},{4,5},{5,4},{6,7},{7,6},{8,9},{9,8},{10,11... | collective-permute-start | bytes 2359304 | tf_op jit(solution)/shard_map/ppermute | solution.py:766
  66.2 18.7 %copy-start.14 = (s32[4,128,2]{1,2,0:T(2,128)S(1)}, s32[4,128,2]{1,2,0:T(2,128)}, u32[]{:S(2)}) copy-start(s32[4,128,2]{1,2,0:T(2,128)} %param.19) | copy-start | bytes 12292
  66.2 18.9 %copy-start.9 = (s32[4,128,2]{2,1,0:T(8,128)S(1)}, s32[4,128,2]{2,1,0:T(8,128)}, u32[]{:S(2)}) copy-start(s32[4,128,2]{2,1,0:T(8,128)} %copy-done.8) | copy-start | bytes 12292
  79.4 24.0 %all-to-all-start.1 = ((bf16[8,128,384]{2,1,0:T(8,128)(2,1)}), bf16[8,128,384]{2,1,0:T(8,128)(2,1)S(1)}, u32[]{:S(2)}, u32[]{:S(2)}) async-start(bf16[8,128,384]{2,1,0:T(8,128)(2,1)} %bitcast.109), calls=%async_computation.1 | async-start | bytes 1572864 | tf_op jit(solution)/shard_map/all_to_all | solution.py:727
  91.6 16.3 %copy-start.18 = (bf16[768]{0:T(1024)(128)(2,1)S(1)}, bf16[768]{0:T(1024)(128)(2,1)}, u32[]{:S(2)}) copy-start(bf16[768]{0:T(1024)(128)(2,1)} %param.24) | copy-start | bytes 4612
  104.2 56.3 %all-to-all-start.3 = ((bf16[8,192,768]{2,1,0:T(8,128)(2,1)}), bf16[8,192,768]{2,1,0:T(8,128)(2,1)S(1)}, u32[]{:S(2)}, u32[]{:S(2)}) async-start(bf16[8,192,768]{2,1,0:T(8,128)(2,1)} %shard_map.260), calls=%async_computation.3 | async-start | bytes 4718592 | tf_op jit(solution)/shard_map/all_to_all | solution.py:727
  118.3 47.6 %copy-start.15 = (bf16[768,8]{0,1:T(8,128)(2,1)S(1)}, bf16[768,8]{0,1:T(8,128)(2,1)}, u32[]{:S(2)}) copy-start(bf16[768,8]{0,1:T(8,128)(2,1)} %param.25) | copy-start | bytes 36868
  162.0 57.9 %all-to-all-start.2 = ((bf16[8,192,768]{2,1,0:T(8,128)(2,1)}), bf16[8,192,768]{2,1,0:T(8,128)(2,1)S(1)}, u32[]{:S(2)}, u32[]{:S(2)}) async-start(bf16[8,192,768]{2,1,0:T(8,128)(2,1)} %shard_map.259), calls=%async_computation.2 | async-start | bytes 4718592 | tf_op jit(solution)/shard_map/all_to_all | solution.py:727
  271.2 57.8 %all-to-all-start.6 = ((bf16[8,192,768]{2,1,0:T(8,128)(2,1)}), bf16[8,192,768]{2,1,0:T(8,128)(2,1)S(1)}, u32[]{:S(2)}, u32[]{:S(2)}) async-start(bf16[8,192,768]{2,1,0:T(8,128)(2,1)} %bitcast.97), calls=%async_computation.6 | async-start | bytes 4718592 | tf_op jit(solution)/shard_map/all_to_all | solution.py:727
  275.0 83.1 %reduce-scatter.22.cloned.1.call-start = ((), (), s32[]{:S(2)}) async-start(), calls=%async_computation.26 | async-start | bytes 2064384 | tf_op jit(solution)/shard_map/reduce_scatter | solution.py:723
  344.2 67.4 %reduce-scatter.28.cloned.1.call-start = ((), (), s32[]{:S(2)}) async-start(), calls=%async_computation.29 | async-start | bytes 14155776 | tf_op jit(solution)/shard_map/reduce_scatter | solution.py:723
  354.5 23.9 %all-to-all-start.7 = ((bf16[8,128,384]{2,1,0:T(8,128)(2,1)}), bf16[8,128,384]{2,1,0:T(8,128)(2,1)S(1)}, u32[]{:S(2)}, u32[]{:S(2)}) async-start(bf16[8,128,384]{2,1,0:T(8,128)(2,1)} %bitcast.24), calls=%async_computation.7 | async-start | bytes 1572864 | tf_op jit(solution)/shard_map/all_to_all | solution.py:727
  358.1 54.1 %reduce-scatter.24.cloned.1.call-start = ((), (), s32[]{:S(2)}) async-start(), calls=%async_computation.27 | async-start | bytes 1032192 | tf_op jit(solution)/shard_map/reduce_scatter | solution.py:723
  358.8 61.5 %reduce-scatter.16.cloned.1.call-start = ((), (), s32[]{:S(2)}) async-start(), calls=%async_computation.23 | async-start | bytes 2949120 | tf_op jit(solution)/shard_map/reduce_scatter | solution.py:723
  411.5 72.3 %reduce-scatter.30.cloned.1.call-start = ((), (), s32[]{:S(2)}) async-start(), calls=%async_computation.30 | async-start | bytes 7077888 | tf_op jit(solution)/shard_map/reduce_scatter | solution.py:723
  412.1 86.5 %reduce-scatter.26.cloned.1.call-start = ((), (), s32[]{:S(2)}) async-start(), calls=%async_computation.28 | async-start | bytes 516096 | tf_op jit(solution)/shard_map/reduce_scatter | solution.py:723
  412.7 107.9 %reduce-scatter.18.cloned.1.call-start = ((), (), s32[]{:S(2)}) async-start(), calls=%async_computation.24 | async-start | bytes 1474560 | tf_op jit(solution)/shard_map/reduce_scatter | solution.py:723
  420.3 119.8 %reduce-scatter.36.cloned.1.call-start = ((), (), s32[]{:S(2)}) async-start(), calls=%async_computation.33 | async-start | bytes 14155776 | tf_op jit(solution)/shard_map/reduce_scatter | solution.py:723
  421.1 196.6 %reduce-scatter.32.cloned.1.call-start = ((), (), s32[]{:S(2)}) async-start(), calls=%async_computation.31 | async-start | bytes 3538944 | tf_op jit(solution)/shard_map/reduce_scatter | solution.py:723
  483.8 167.4 %reduce-scatter.40.cloned.1.call-start = ((), (), s32[]{:S(2)}) async-start(), calls=%async_computation.35 | async-start | bytes 215040
  498.6 169.5 %reduce-scatter.20.cloned.1.call-start = ((), (), s32[]{:S(2)}) async-start(), calls=%async_computation.25 | async-start | bytes 614400 | tf_op jit(solution)/shard_map/reduce_scatter | solution.py:723
  520.6 208.0 %reduce-scatter.38.cloned.1.call-start = ((), (), s32[]{:S(2)}) async-start(), calls=%async_computation.34 | async-start | bytes 7077888 | tf_op jit(solution)/shard_map/reduce_scatter | solution.py:723
  540.1 79.8 %all-to-all-start.5 = ((bf16[8,192,768]{2,1,0:T(8,128)(2,1)}), bf16[8,192,768]{2,1,0:T(8,128)(2,1)S(1)}, u32[]{:S(2)}, u32[]{:S(2)}) async-start(bf16[8,192,768]{2,1,0:T(8,128)(2,1)} %bitcast.92), calls=%async_computation.5 | async-start | bytes 4718592 | tf_op jit(solution)/shard_map/all_to_all | solution.py:727
  546.0 214.2 %reduce-scatter.34.cloned.1.call-start = ((), (), s32[]{:S(2)}) async-start(), calls=%async_computation.32 | async-start | bytes 1474560 | tf_op jit(solution)/shard_map/reduce_scatter | solution.py:723
  548.1 69.6 %collective-permute-start.1 = (bf16[4,128,768]{2,1,0:T(8,128)(2,1)}, bf16[4,128,768]{2,1,0:T(8,128)(2,1)S(1)}, u32[]{:S(2)}, u32[]{:S(2)}) collective-permute-start(bf16[4,128,768]{2,1,0:T(8,128)(2,1)} %dynamic-slice_bitcast_fusion), channel_id=1, source_target_pairs={{0,1},{1,0},{2,3},{3,2},{4,5},{5,4},{6,7},{7,6},{8,9},{9,8},{10,11... | collective-permute-start | bytes 2359304 | tf_op jit(solution)/shard_map/ppermute | solution.py:850
  619.9 27.5 %all-to-all-start.8 = ((bf16[4,128,768]{2,1,0:T(8,128)(2,1)}), bf16[4,128,768]{2,1,0:T(8,128)(2,1)S(1)}, u32[]{:S(2)}, u32[]{:S(2)}) async-start(bf16[4,128,768]{2,1,0:T(8,128)(2,1)} %fusion), calls=%async_computation.8 | async-start | bytes 1572864 | tf_op jit(solution)/shard_map/all_to_all | solution.py:727
  668.1 7.8 %all-to-all-start.9 = ((bf16[2,24,1280]{2,1,0:T(8,128)(2,1)}), bf16[2,24,1280]{2,1,0:T(8,128)(2,1)S(1)}, u32[]{:S(2)}, u32[]{:S(2)}) async-start(bf16[2,24,1280]{2,1,0:T(8,128)(2,1)} %bitcast.115), calls=%async_computation.12 | async-start | bytes 245760 | tf_op jit(solution)/shard_map/all_to_all | solution.py:727
  733.1 29.0 %copy-start.1 = (s32[4,1024]{1,0:T(4,128)S(1)}, s32[4,1024]{1,0:T(4,128)}, u32[]{:S(2)}) copy-start(s32[4,1024]{1,0:T(4,128)} %param.17) | copy-start | bytes 49156
  (12 other events, 48.6 us)
Sparse Core Ops, SparseCore 0:
  344.3 7.8 reduce-scatter.21
  354.6 18.3 reduce-scatter.27
  375.3 17.7 reduce-scatter.23
  411.6 8.5 reduce-scatter.15
  422.4 61.3 reduce-scatter.29
  485.9 12.6 reduce-scatter.25
  500.9 19.6 reduce-scatter.17
  522.9 17.2 reduce-scatter.35
  542.4 75.2 reduce-scatter.31
  619.8 21.9 reduce-scatter.39
  644.1 24.0 reduce-scatter.19
  670.3 58.2 reduce-scatter.37
  730.9 29.3 reduce-scatter.33

commit v2 on v1

--- a/solution.py
+++ b/solution.py
@@ -63,58 +63,104 @@
     return lax.rsqrt(jnp.mean(values * values, axis=1, keepdims=True) + EPS)
 
 
-def project(rows, gain, weight, cosine, sine):
-    parts, blocks, span, width = rows.shape
-    cols = weight.shape[1]
-    group = cols // 3
+def row_specs(rows):
+    if len(rows) == 2:
+        _, span, width = rows[0].shape
+        return [pl.BlockSpec((1, span, width), lambda i, *_: (i, 0, 0))] * 2
+    parts, _, span, width = rows[0].shape
+    return [pl.BlockSpec((parts, 1, span, width), lambda i, *_: (0, i, 0, 0))]
+
+
+def load_rows(refs, at_ref):
+    if len(refs) == 2:
+        mine, theirs = refs[0][0].astype(F32), refs[1][0].astype(F32)
+        first = at_ref[0] == 0
+        pair = [jnp.where(first, mine, theirs), jnp.where(first, theirs, mine)]
+        return jnp.concatenate(pair, axis=0)
+    value = refs[0][...]
+    return value.reshape(value.shape[0] * value.shape[2], value.shape[3]).astype(F32)
+
+
+def weight_specs(weights, group):
+    if len(weights) == 1:
+        return [whole(weights[0].shape)]
+    width, cols = weights[0].shape
+    parts = cols // (3 * group)
+
+    def spec(index):
+        return pl.BlockSpec((width, group), lambda i, at: (0, index * parts + at[0]))
+
+    return [spec(index) for index in range(3)]
+
+
+def load_weights(refs, group):
+    if len(refs) == 3:
+        return [ref[...] for ref in refs]
+    return [refs[0][:, at * group : (at + 1) * group] for at in range(3)]
+
+
+def project(rows, gain, weights, group, cosine, sine, x_at, parts):
+    blocks, span, width = rows[0].shape[-3:]
     height = parts * span
     length = height * blocks
-
-    def body(r_ref, g_ref, w_ref, c_ref, s_ref, qkv_ref, n_ref):
-        tok = r_ref[...].reshape(height, width).astype(F32)
+    cut = len(rows)
+
+    def body(at_ref, *refs):
+        r_refs, (g_ref, c_ref, s_ref) = refs[:cut], refs[cut : cut + 3]
+        w_refs, (qkv_ref, n_ref) = refs[cut + 3 : -2], refs[-2:]
+        tok = load_rows(r_refs, at_ref)
         normed = (tok * rms(tok) * g_ref[...]).astype(BF)
         n_ref[...] = normed
-        proj = mm(normed, w_ref[...])
-        for at in range(0, 2 * group, 128):
-            part = proj[:, at : at + 128]
-            lane = lax.broadcasted_iota(jnp.int32, part.shape, 1) + at
-            turned = part * c_ref[...] + swap_halves(part) * s_ref[...]
-            turned = turned * jnp.where(lane < group, HEAD_DIM**-0.5, 1.0)
-            qkv_ref[:, at : at + 128] = turned.astype(BF)
-        qkv_ref[:, 2 * group :] = proj[:, 2 * group :].astype(BF)
+        if len(w_refs) == 3:
+            found = [mm(normed, ref[...]) for ref in w_refs]
+            turning = [(found[0], 0), (found[1], group)]
+            last = found[2]
+        else:
+            found = mm(normed, w_refs[0][...])
+            turning, last = [(found[:, : 2 * group], 0)], found[:, 2 * group :]
+        for value, base in turning:
+            for at in range(0, value.shape[1], 128):
+                part = value[:, at : at + 128]
+                lane = lax.broadcasted_iota(jnp.int32, part.shape, 1) + (base + at)
+                turned = part * c_ref[...] + swap_halves(part) * s_ref[...]
+                turned = turned * jnp.where(lane < group, HEAD_DIM**-0.5, 1.0)
+                qkv_ref[:, base + at : base + at + 128] = turned.astype(BF)
+        qkv_ref[:, 2 * group :] = last.astype(BF)
 
     return call(
         body,
         (blocks,),
         [
-            pl.BlockSpec((parts, 1, span, width), lambda i: (0, i, 0, 0)),
+            *row_specs(rows),
             whole((1, width)),
-            whole((width, cols)),
-            pl.BlockSpec((height, 128), lambda i: (i, 0)),
-            pl.BlockSpec((height, 128), lambda i: (i, 0)),
+            pl.BlockSpec((height, 128), lambda i, *_: (i, 0)),
+            pl.BlockSpec((height, 128), lambda i, *_: (i, 0)),
+            *weight_specs(weights, group),
         ],
         [
-            pl.BlockSpec((height, cols), lambda i: (i, 0)),
-            pl.BlockSpec((height, width), lambda i: (i, 0)),
+            pl.BlockSpec((height, 3 * group), lambda i, *_: (i, 0)),
+            pl.BlockSpec((height, width), lambda i, *_: (i, 0)),
         ],
-        [sds((length, cols), BF), sds((length, width), BF)],
-        (rows, gain, weight, cosine, sine),
-        flops=2 * length * width * cols,
-    )
-
-
-def project_back(grads, weight, rows, gain):
-    parts, blocks, span, width = rows.shape
+        [sds((length, 3 * group), BF), sds((length, width), BF)],
+        (x_at, *rows, gain, cosine, sine, *weights),
+        prefetch=1,
+        flops=6 * length * width * group,
+    )
+
+
+def project_back(grads, weights, rows, x_at, parts):
+    blocks, span, width = rows[0].shape[-3:]
     group = grads[0].shape[1]
     height = parts * span
     length = height * blocks
-
-    def body(q_ref, k_ref, v_ref, w_ref, r_ref, out_ref, gain_ref, acc_ref):
+    cut = len(rows)
+
+    def body(at_ref, q_ref, k_ref, v_ref, *refs):
+        r_refs, w_refs, (out_ref, gain_ref, acc_ref) = refs[:cut], refs[cut:-3], refs[-3:]
         step = pl.program_id(0)
-        back = mm(q_ref[...], w_ref[:, :group], NT)
-        back += mm(k_ref[...], w_ref[:, group : 2 * group], NT)
-        back += mm(v_ref[...], w_ref[:, 2 * group :], NT)
-        tok = r_ref[...].reshape(height, width).astype(F32)
+        w_q, w_k, w_v = load_weights(w_refs, group)
+        back = mm(q_ref[...], w_q, NT) + mm(k_ref[...], w_k, NT) + mm(v_ref[...], w_v, NT)
+        tok = load_rows(r_refs, at_ref)
         part = jnp.sum(back * tok * rms(tok), axis=0, keepdims=True)
 
         @pl.when(step == 0)
@@ -129,24 +175,19 @@
             column = jnp.transpose(acc_ref[...])
             gain_ref[...] = jnp.broadcast_to(column[:, :1], gain_ref.shape)
 
-    block = pl.BlockSpec((height, group), lambda i: (i, 0))
+    block = pl.BlockSpec((height, group), lambda i, *_: (i, 0))
     return call(
         body,
         (blocks,),
+        [block, block, block, *row_specs(rows), *weight_specs(weights, group)],
         [
-            block,
-            block,
-            block,
-            whole(weight.shape),
-            pl.BlockSpec((parts, 1, span, width), lambda i: (0, i, 0, 0)),
-        ],
-        [
-            pl.BlockSpec((parts, 1, span, width), lambda i: (0, i, 0, 0)),
+            pl.BlockSpec((parts, 1, span, width), lambda i, *_: (0, i, 0, 0)),
             whole((width, 128)),
         ],
         [sds((parts, blocks, span, width), BF), sds((width, 128), F32)],
-        (*grads, weight, rows),
+        (x_at, *grads, *rows, *weights),
         scratch=[pltpu.VMEM((8, width), F32)],
+        prefetch=1,
         flops=6 * length * width * group,
     )
 
@@ -329,22 +370,33 @@
     )
 
 
-def dispatch(rows, target_rows, experts, capacity):
+def dispatch(rows, target_rows, experts, capacity, route_rows=None):
     count, width = rows.shape
-
-    def body(r_ref, t_ref, o_ref):
+    more = 0 if route_rows is None else 16
+    tables = () if route_rows is None else (route_rows,)
+
+    def body(r_ref, t_ref, *refs):
+        o_ref = refs[-1]
         slot = lax.broadcasted_iota(jnp.int32, (capacity, count), 0)
         slot += pl.program_id(0) * capacity
-        hit = (slot == t_ref[0:1, :]) | (slot == t_ref[1:2, :])
-        o_ref[0] = mm(hit.astype(F32).astype(BF), r_ref[...]).astype(BF)
+        hits = [slot == t_ref[k : k + 1, :] for k in range(2)]
+        hot = (hits[0] | hits[1]).astype(F32).astype(BF)
+        o_ref[0, :capacity, :] = mm(hot, r_ref[...]).astype(BF)
+        if more:
+            o_ref[0, capacity:, :] = jnp.zeros((more, width), BF)
+            other = jnp.zeros((8, capacity), F32)
+            for k in range(2):
+                route = jnp.broadcast_to(refs[0][1 - k : 2 - k, :].astype(F32), (8, count))
+                other += mm(route.astype(BF), hits[k].astype(F32).astype(BF), NT)
+            o_ref[0, capacity : capacity + 8, :capacity] = other.astype(BF)
 
     return call(
         body,
         (experts,),
-        [whole(rows.shape), whole(target_rows.shape)],
-        pl.BlockSpec((1, capacity, width), lambda i: (i, 0, 0)),
-        sds((experts, capacity, width), BF),
-        (rows, target_rows),
+        [whole(a.shape) for a in (rows, target_rows, *tables)],
+        pl.BlockSpec((1, capacity + more, width), lambda i: (i, 0, 0)),
+        sds((experts, capacity + more, width), BF),
+        (rows, target_rows, *tables),
         flops=2 * experts * capacity * count * width,
     )
 
@@ -440,26 +492,31 @@
     )
 
 
-def first_norm_back(tokens, gain, grad_normed, grad_hidden):
+def first_norm_back(tokens, gain, pieces, grad_hidden, z_at):
     count, width = tokens.shape
-    high = count // 2
-
-    def body(t_ref, g_ref, n_ref, h_ref, o_ref):
-        tok = t_ref[...].astype(F32)
-        scale = rms(tok)
-        weighted = n_ref[...].astype(F32) * g_ref[...]
-        inner = jnp.mean(weighted * tok, axis=1, keepdims=True)
-        out = h_ref[...] + scale * weighted - tok * (scale * scale * scale * inner)
-        o_ref[...] = out.astype(BF)
-
-    block = pl.BlockSpec((high, width), lambda i: (i, 0))
+    blocks = len(pieces)
+    span = count // blocks
+
+    def body(at_ref, t_ref, g_ref, h_ref, *refs):
+        o_ref = refs[-1]
+        for index in range(blocks):
+            seq = (at_ref[0] + blocks - index) % blocks
+            spot = pl.ds(pl.multiple_of(seq * span, span), span)
+            tok = t_ref[spot, :].astype(F32)
+            scale = rms(tok)
+            weighted = refs[index][...].astype(F32) * g_ref[...]
+            inner = jnp.mean(weighted * tok, axis=1, keepdims=True)
+            out = h_ref[spot, :] + scale * weighted - tok * (scale * scale * scale * inner)
+            o_ref[spot, :] = out.astype(BF)
+
     return call(
         body,
-        (2,),
-        [block, whole(gain.shape), block, block],
-        block,
+        (1,),
+        [whole(a.shape) for a in (tokens, gain, grad_hidden, *pieces)],
+        whole(tokens.shape),
         sds(tokens.shape, BF),
-        (tokens, gain, grad_normed, grad_hidden),
+        (z_at, tokens, gain, grad_hidden, *pieces),
+        prefetch=1,
     )
 
 
@@ -576,40 +633,54 @@
     )
 
 
-def expert_weight_grads(rows, grads, dg, du, hid, grad_logits, sizes):
+def expert_weight_grads(rows, grads, dg, du, hid, grad_logits, sizes, core_at):
     outer, cores = sizes["y"], sizes["core"]
     count, width = rows.shape
     units = dg.shape[1]
     wide = units // (outer * cores)
 
-    def body(x_ref, g_ref, dg_ref, du_ref, hid_ref, gl_ref, o_ref, r_ref):
-        o_ref[0, 0, 0] = mm(x_ref[...], dg_ref[...], TN).astype(BF)
-        o_ref[0, 0, 1] = mm(x_ref[...], du_ref[...], TN).astype(BF)
-        o_ref[0, 0, 2] = mm(g_ref[...], hid_ref[...], TN).astype(BF)
-
-        @pl.when(pl.program_id(0) == 0)
+    def body(at_ref, x_ref, g_ref, dg_ref, du_ref, hid_ref, gl_ref, keep_ref, give_ref, r_ref):
+        step = pl.program_id(0)
+        found = [
+            mm(x_ref[...], dg_ref[...], TN).astype(BF),
+            mm(x_ref[...], du_ref[...], TN).astype(BF),
+            mm(g_ref[...], hid_ref[...], TN).astype(BF),
+        ]
+
+        @pl.when(step < outer)
+        def _():
+            for index in range(3):
+                give_ref[0, index] = found[index]
+
+        @pl.when(step >= outer)
+        def _():
+            for index in range(3):
+                keep_ref[0, index] = found[index]
+
+        @pl.when(step == 0)
         def _():
             r_ref[...] = mm(x_ref[...], gl_ref[...], TN)
 
-    hidden = pl.BlockSpec((count, wide), lambda i: (0, i))
+    def taken(i, at):
+        core = jnp.where(i < outer, 1 - at[0], at[0])
+        return (0, (i % outer) * cores + core)
+
+    hidden = pl.BlockSpec((count, wide), taken)
+    part = (1, 3, width, wide)
     return call(
         body,
         (outer * cores,),
         [whole(rows.shape), whole(grads.shape), hidden, hidden, hidden, whole(grad_logits.shape)],
         [
-            pl.BlockSpec((1, 1, 3, width, wide), lambda i: (i % cores, i // cores, 0, 0, 0)),
+            pl.BlockSpec(part, lambda i, *_: (jnp.maximum(i - outer, 0), 0, 0, 0)),
+            pl.BlockSpec(part, lambda i, *_: (jnp.minimum(i, outer - 1), 0, 0, 0)),
             whole((width, 128)),
         ],
-        [sds((cores, outer, 3, width, wide), BF), sds((width, 128), F32)],
-        (rows, grads, dg, du, hid, grad_logits),
+        [sds((outer, *part[1:]), BF)] * 2 + [sds((width, 128), F32)],
+        (core_at, rows, grads, dg, du, hid, grad_logits),
+        prefetch=1,
         flops=6 * count * width * units,
     )
-
-
-def spread(value, sizes, names):
-    order = ("y", "core", "z", "x")
-    split = value.reshape(*(sizes[n] for n in order), -1, value.shape[-1])
-    return jnp.transpose(split, (*(order.index(n) for n in names), 4, 5))
 
 
 def spread_places(sizes, names):
@@ -619,17 +690,33 @@
             for z in range(sizes["z"]):
                 for x in range(sizes["x"]):
                     at = {"y": y, "core": core, "z": z, "x": x}
-                    found.append(tuple(at[n] for n in names))
+                    found.append((core, tuple(at[n] for n in names)))
     return found
 
 
-def spread_shape(sizes, names):
-    return tuple(sizes[n] for n in names)
-
-
-def shared_weight_grads(rows, grads, dg, du, hid, sizes):
-    names = ("core", "y", "x", "z")
-    lead = spread_shape(sizes, names)
+def spread(value, sizes, names, core_at):
+    order = ("y", "core", "z", "x")
+    split = value.reshape(*(sizes[n] for n in order), -1, value.shape[-1])
+    split = jnp.transpose(split, (1, *(order.index(n) for n in names), 4, 5))
+    return at_index(split, core_at[0]), at_index(split, 1 - core_at[0])
+
+
+def store_spread(places, each, core_at, found, row, keep, give):
+    first = row // each
+    for core in range(2):
+        todo = [at for at in range(found.shape[0] // each) if places[first + at][0] == core]
+
+        def put(store, todo=todo):
+            for at in todo:
+                store(places[first + at][1], found[at * each : (at + 1) * each].astype(BF))
+
+        pl.when(core_at == core)(lambda put=put: put(keep))
+        pl.when(core_at != core)(lambda put=put: put(give))
+
+
+def shared_weight_grads(rows, grads, dg, du, hid, sizes, core_at):
+    names = ("y", "x", "z")
+    lead = tuple(sizes[n] for n in names)
     places = spread_places(sizes, names)
     count, width = rows.shape
     units = dg.shape[1]
@@ -637,39 +724,48 @@
     each = width // len(places)
     direct = each % 8 == 0
 
-    def body(x_ref, g_ref, dg_ref, du_ref, hid_ref, o_ref):
+    def body(at_ref, x_ref, g_ref, dg_ref, du_ref, hid_ref, *outs):
         pairs = ((x_ref, dg_ref), (x_ref, du_ref), (g_ref, hid_ref))
         for index, (left, right) in enumerate(pairs):
             found = mm(left[...], right[...], TN)
-            if direct:
-                for at, place in enumerate(places):
-                    o_ref[(*place, index)] = found[at * each : (at + 1) * each].astype(BF)
-            else:
-                o_ref[index] = found.astype(BF)
-
-    hidden = pl.BlockSpec((count, wide), lambda i: (0, i))
+            if not direct:
+                outs[0][index] = found.astype(BF)
+                continue
+
+            def into(ref, index=index):
+                def store(place, piece):
+                    ref[(*place, index)] = piece
+
+                return store
+
+            store_spread(places, each, at_ref[0], found, 0, into(outs[0]), into(outs[1]))
+
+    hidden = pl.BlockSpec((count, wide), lambda i, *_: (0, i))
     if direct:
-        shape = (*lead, 3, each, units)
-        spec = pl.BlockSpec((*lead, 3, each, wide), lambda i: (0,) * 6 + (i,))
+        shapes = [(*lead, 3, each, units)] * 2
+        spec = [pl.BlockSpec((*lead, 3, each, wide), lambda i, *_: (0,) * 5 + (i,))] * 2
     else:
-        shape = (3, width, units)
-        spec = pl.BlockSpec((3, width, wide), lambda i: (0, 0, i))
+        shapes = [(3, width, units)]
+        spec = [pl.BlockSpec((3, width, wide), lambda i, *_: (0, 0, i))]
     out = call(
         body,
         (units // wide,),
         [whole(rows.shape), whole(grads.shape), hidden, hidden, hidden],
         spec,
-        sds(shape, BF),
-        (rows, grads, dg, du, hid),
+        [sds(shape, BF) for shape in shapes],
+        (core_at, rows, grads, dg, du, hid),
+        prefetch=1,
         flops=6 * count * width * units,
     )
     if direct:
         return out
-    return jnp.stack([spread(out[i], sizes, names) for i in range(3)], axis=4)
-
-
-def tall_weight_grads(lefts, rights, extras, sizes, names):
-    lead = spread_shape(sizes, names)
+    found = [spread(out[0][i], sizes, names, core_at) for i in range(3)]
+    return [jnp.stack([part[side] for part in found], axis=3) for side in range(2)]
+
+
+def tall_weight_grads(lefts, rights, extras, sizes, core_at):
+    names = ("y", "z", "x")
+    lead = tuple(sizes[n] for n in names)
     places = spread_places(sizes, names)
     width = sum(left.shape[1] for left in lefts)
     cols = sum(right.shape[1] for right in rights)
@@ -677,46 +773,51 @@
     direct = each % 8 == 0
     flops = 2 * lefts[0].shape[0] * width * cols
 
-    def body(*refs):
+    def body(at_ref, *refs):
         left_refs = refs[: len(lefts)]
         right_refs = refs[len(lefts) : len(lefts) + len(rights)]
-        extra_refs = refs[len(lefts) + len(rights) : -1]
-        out_ref = refs[-1]
-
-        def store(row, found, col):
+        rest = refs[len(lefts) + len(rights) :]
+        extra_refs, outs = rest[: len(extras)], rest[len(extras) :]
+
+        def save(row, found, col):
             span = found.shape[1]
             if not direct:
-                out_ref[row : row + found.shape[0], col : col + span] = found.astype(BF)
+                outs[0][row : row + found.shape[0], col : col + span] = found.astype(BF)
                 return
-            for at in range(found.shape[0] // each):
-                place = places[row // each + at]
-                piece = found[at * each : (at + 1) * each].astype(BF)
-                out_ref[(*place, slice(None), slice(col, col + span))] = piece
+
+            def into(ref):
+                def store(place, piece):
+                    ref[(*place, slice(None), slice(col, col + span))] = piece
+
+                return store
+
+            store_spread(places, each, at_ref[0], found, row, into(outs[0]), into(outs[1]))
 
         row = 0
         for left in left_refs:
             col = 0
             for right in right_refs:
-                store(row, mm(left[...], right[...], TN), col)
+                save(row, mm(left[...], right[...], TN), col)
                 col += right.shape[1]
             row += left.shape[1]
         more = extra_refs[0][...]
         for extra in extra_refs[1:]:
             more = more + extra[...]
-        store(0, more, cols)
+        save(0, more, cols)
 
     args = (*lefts, *rights, *extras)
-    shape = (*lead, each, cols + 128) if direct else (width, cols + 128)
+    shapes = [(*lead, each, cols + 128)] * 2 if direct else [(width, cols + 128)]
     out = call(
         body,
         (1,),
         [whole(a.shape) for a in args],
-        whole(shape),
-        sds(shape, BF),
-        args,
+        [whole(shape) for shape in shapes],
+        [sds(shape, BF) for shape in shapes],
+        (core_at, *args),
+        prefetch=1,
         flops=flops,
     )
-    return out if direct else spread(out, sizes, names)
+    return out if direct else spread(out[0], sizes, names, core_at)
 
 
 def scatter_sum(value, name):
@@ -725,6 +826,36 @@
 
 def swap_all(value, names):
     return lax.all_to_all(value, names, 0, 0, tiled=True)
+
+
+def at_index(value, index):
+    return lax.dynamic_index_in_dim(value, index, 0, keepdims=False)
+
+
+def fold(value, name):
+    if lax.axis_size(name) != 2:
+        return scatter_sum(value, name)
+    at = lax.axis_index(name)
+    got = lax.ppermute(at_index(value, 1 - at), name, [(0, 1), (1, 0)])
+    return (at_index(value, at).astype(F32) + got.astype(F32)).astype(BF)
+
+
+def join(keep, give, name):
+    got = lax.ppermute(give, name, [(0, 1), (1, 0)])
+    return (keep.astype(F32) + got.astype(F32)).astype(BF)
+
+
+def swap_by_steps(value, name):
+    size, at = value.shape[0], lax.axis_index(name)
+    found = [at_index(value, at)]
+    for step in range(1, size):
+        sent = at_index(value, (at + step) % size)
+        found.append(lax.ppermute(sent, name, [(i, (i + step) % size) for i in range(size)]))
+    return found
+
+
+def after(value, *others):
+    return lax.optimization_barrier((value, *others))[0]
 
 
 def on_device(
@@ -756,46 +887,46 @@
     group = width // parts
     z_at, x_at = lax.axis_index("z"), lax.axis_index("x")
     own = (z_at * parts + x_at).astype(jnp.int32).reshape(1)
+    z_ref, x_ref = z_at.astype(jnp.int32).reshape(1), x_at.astype(jnp.int32).reshape(1)
+    core_ref = lax.axis_index("core").astype(jnp.int32).reshape(1)
     attn_scale = attn_gain.astype(F32).reshape(1, width)
     ffn_scale = ffn_gain.astype(F32).reshape(1, width)
     flat_tokens = tokens.reshape(count, width)
     flat_cot = cotangent.reshape(count, width)
 
-    by_seq = swap_all(tokens, "z")
-    if parts == 2:
-        theirs = lax.ppermute(by_seq, "x", [(0, 1), (1, 0)])
-        first = x_at == 0
-        rows = jnp.stack([jnp.where(first, by_seq, theirs), jnp.where(first, theirs, by_seq)])
-    else:
-        rows = lax.all_gather(by_seq, "x", axis=0, tiled=False)
-
     route_rows = routes.reshape(count, 2)
     slot_rows = slots.reshape(count, 2)
     target = jnp.where(slot_rows >= 0, route_rows * capacity + slot_rows, -1)
     target_rows = jnp.transpose(target)
-    grad_sent = dispatch(flat_cot, target_rows, experts, capacity)
-    spots = jnp.where(target >= 0, target, experts * capacity).reshape(-1)
-    other = (
-        jnp.zeros((experts * capacity,), F32)
-        .at[spots]
-        .set(route_rows[:, ::-1].reshape(-1).astype(F32), mode="drop")
-    )
-    other = swap_all(other.reshape(experts, capacity), ranks)
-    other = other.reshape(-1, 1).astype(jnp.int32)
-    grad_rows = swap_all(grad_sent, ranks).reshape(-1, width)
+    grad_sent = dispatch(flat_cot, target_rows, experts, capacity, jnp.transpose(route_rows))
 
     frequency = jnp.power(10000.0, -2.0 * jnp.arange(32, dtype=F32) / HEAD_DIM)
     angles = jnp.arange(length, dtype=jnp.int32).astype(F32)[:, None] * jnp.tile(frequency, 4)
     sign = jnp.where(jnp.arange(128) % 64 < 32, -1.0, 1.0)
     cosine, sine = jnp.cos(angles), jnp.sin(angles) * sign
-    w_group = lax.dynamic_index_in_dim(
-        w_qkv.reshape(width, 3, parts, group), x_at, 2, keepdims=False
-    ).reshape(width, 3 * group)
     seg_row = lax.dynamic_slice_in_dim(segments, z_at, 1, 0)
     seg_col = seg_row.reshape(length, 1)
-    qkv, normed = project(rows, attn_scale, w_group, cosine, sine)
     fused = group % 128 == 0
+    if fused:
+        weights = [w_qkv] * 3
+    else:
+        picked = w_qkv.reshape(width, 3, parts, group)
+        picked = lax.dynamic_index_in_dim(picked, x_at, 2, keepdims=False)
+        weights = [picked.reshape(width, 3 * group)]
+
+    by_seq = swap_all(tokens, "z")
+    by_seq, cosine, sine, seg_col, grad_sent = lax.optimization_barrier(
+        (by_seq, cosine, sine, seg_col, grad_sent)
+    )
+    grad_came = swap_all(grad_sent, ranks)
+    if parts == 2:
+        rows = [by_seq, lax.ppermute(by_seq, "x", [(0, 1), (1, 0)])]
+    else:
+        rows = [lax.all_gather(by_seq, "x", axis=0, tiled=False)]
+
+    qkv, normed = project(rows, attn_scale, weights, group, cosine, sine, x_ref, parts)
     attended, lse = (attend if fused else plain_attend)(qkv, seg_row, seg_col)
+    attended = after(attended, grad_came)
     attended = swap_all(attended.reshape(experts, span, group), ranks)
     attended = attended.reshape(seqs, parts, span, group)
 
@@ -806,22 +937,23 @@
     shared_out, shared_back, hid, dg, du = feed_forward(
         branch_in, flat_cot, shared_gate, shared_up, shared_down
     )
-    shared_sums = shared_weight_grads(branch_in, flat_cot, dg, du, hid, sizes)
-    for name in ("core", "y", "x", "z"):
-        shared_sums = scatter_sum(shared_sums, name)
+    keep, give = shared_weight_grads(branch_in, flat_cot, dg, du, hid, sizes, core_ref)
+    shared_sums = fold(join(keep, give, "core"), "y")
+    grad_rows = grad_came[:, :capacity, :].reshape(-1, width)
+    other = grad_came[:, capacity, :capacity].astype(jnp.int32).reshape(-1, 1)
+    received = after(received, give, grad_rows, other)
 
     router = jnp.pad(w_router, ((0, 0), (0, 128 - experts)))
     made, made_back, hid, dg, du, gated_grads, grad_logits = feed_forward(
         received, grad_rows, expert_gate[0], expert_up[0], expert_down[0], router, other, own
     )
     back_rows = swap_all(made_back.reshape(experts, capacity, width), ranks).reshape(-1, width)
-    made_rows = swap_all(made.reshape(experts, capacity, width), ranks).reshape(-1, width)
-    expert_sums, grad_router = expert_weight_grads(
-        received, gated_grads, dg, du, hid, grad_logits, sizes
-    )
-    for name in ("core", "y"):
-        expert_sums = scatter_sum(expert_sums, name)
-    layer_out = layer_end(hidden, shared_out, made_rows, target).reshape(tokens.shape)
+    keep, give, grad_router = expert_weight_grads(
+        received, gated_grads, dg, du, hid, grad_logits, sizes, core_ref
+    )
+    back_rows = after(back_rows, give)
+    expert_sums = fold(join(keep, give, "core"), "y")
+    shared_sums = swap_by_steps(fold(shared_sums, "x"), "z")
 
     grad_hidden, grad_attn, grad_att, grad_ffn = middle_back(
         hidden, shared_back, back_rows, target, flat_cot, ffn_scale, w_out, parts, span
@@ -835,36 +967,35 @@
         [grad_attn],
         [small],
         sizes,
-        ("core", "y", "x", "z"),
-    )
-    for name in ("core", "y", "x", "z"):
-        out_sums = scatter_sum(out_sums, name)
-
+        core_ref,
+    )
+    out_sums = fold(join(*out_sums, "core"), "y")
+
+    made = after(made, grad_att)
+    made_rows = swap_all(made.reshape(experts, capacity, width), ranks).reshape(-1, width)
     grads = (attend_back if fused else plain_attend_back)(
         qkv, grad_att, lse, seg_row, seg_col, cosine, sine
     )
-    normed_back, grad_gain = project_back(grads, w_group, rows, attn_scale)
-    if parts == 2:
-        keep = lax.dynamic_index_in_dim(normed_back, x_at, 0, keepdims=False)
-        give = lax.dynamic_index_in_dim(normed_back, 1 - x_at, 0, keepdims=False)
-        got = lax.ppermute(give, "x", [(0, 1), (1, 0)])
-        normed_back = (keep.astype(F32) + got.astype(F32)).astype(BF)
-    else:
-        normed_back = scatter_sum(normed_back, "x")
-    normed_back = swap_all(normed_back, "z").reshape(count, width)
-    token_grad = first_norm_back(flat_tokens, attn_scale, normed_back, grad_hidden)
-
-    qkv_sums = tall_weight_grads([normed], list(grads), [grad_gain], sizes, ("core", "y", "z", "x"))
-    for name in ("core", "y", "z"):
-        qkv_sums = scatter_sum(qkv_sums, name)
-    qkv_sums = swap_all(qkv_sums, "x").astype(F32)
+    normed_back, grad_gain = project_back(grads, weights, rows, x_ref, parts)
+    normed_back = fold(normed_back, "x")
+    pieces = swap_by_steps(normed_back, "z")
+
+    qkv_sums = tall_weight_grads([normed], list(grads), [grad_gain], sizes, core_ref)
+    qkv_sums = fold(join(*qkv_sums, "core"), "y")
+    token_grad = first_norm_back(flat_tokens, attn_scale, pieces, grad_hidden, z_ref)
+    layer_out = layer_end(hidden, shared_out, made_rows, target).reshape(tokens.shape)
+
+    last = after(jnp.concatenate([out_sums, qkv_sums], axis=-1), made_rows)
+    each, cols = last.shape[-2:]
+    last = swap_all(last.reshape(experts, each, cols), ranks).astype(F32)
+    last = jnp.sum(last.reshape(blocks, parts, each, cols), axis=0)
+    out_sums = jnp.sum(last[:, :, : width + 128], axis=0)
+    qkv_sums = last[:, :, width + 128 :]
     grad_attn_gain = jnp.sum(qkv_sums[:, :, 3 * group], axis=0)
-    each = qkv_sums.shape[1]
     grad_w_qkv = qkv_sums[:, :, : 3 * group].reshape(parts, each, 3, group)
     grad_w_qkv = jnp.transpose(grad_w_qkv, (1, 2, 0, 3)).reshape(each, 3 * width)
 
-    out_sums = out_sums.astype(F32)
-    shared_sums = shared_sums.astype(F32)
+    shared_sums = sum(part.astype(F32) for part in shared_sums)
     expert_sums = expert_sums.astype(F32)
     return (
         layer_out,

time: 783 us -> 593 us (0.76)
  waiting for transfers between devices: 451 us -> 266 us
  other arithmetic: 16.2 us -> 30.7 us
  between operations: 14.5 us -> 1.27 us
    reduce_scatter x12 -> x0, waiting for transfers between devices: 285 us -> none  [scatter_sum(): return lax.psum_scatter(value, name, scatter_dimension=0, tiled=False)]
    ppermute x2 -> x17, waiting for transfers between devices: 1.44 us -> 169 us  [the longest x6 64 us: fold(): got = lax.ppermute(at_index(value, 1 - at), name, [(0, 1), (1, 0)])]
    all_to_all x10 -> x8, waiting for transfers between devices: 162 us -> 97.5 us  [swap_all(): return lax.all_to_all(value, names, 0, 0, tiled=True)]
    ppermute x2 -> x17, starting transfers between devices: 3.86 us -> 20.5 us  [the longest x6 10.1 us: swap_by_steps(): lax.ppermute(sent, name, [(i, (i + step) % size) for i in range(size)])]
    convert_element_type x6 -> x10, other arithmetic: 4.76 us -> 19.9 us  [the longest x4 13 us: join(): return (keep.astype(F32) + got.astype(F32)).astype(BF)]
    reduce_scatter x12 -> x0, starting transfers between devices: 9.6 us -> none  [scatter_sum(): return lax.psum_scatter(value, name, scatter_dimension=0, tiled=False)]
    all_to_all x10 -> x8, starting transfers between devices: 44.6 us -> 37 us  [swap_all(): return lax.all_to_all(value, names, 0, 0, tiled=True)]
  transfers between devices with their start and end apart: 25 -> 25, of which waited for: 18 -> 12; matrix products, arithmetic and copies ran while one was open for 6% -> 8% of each run, Pallas kernels for 16% -> 27%
where the time goes in v2:
time: 593 us; the launch traced here: 583 us
  waiting for transfers between devices  266 us (45%)
  Pallas kernels  194 us (33%)
  starting transfers between devices  57.5 us (10%)
  local copies, waits for them, and re-layouts  34.1 us (6%)
  other arithmetic  30.7 us (5%)
    pallas_call x16, Pallas kernels, call(): pl.pallas_call(body, out_shape=out_shape, grid_spec=pltpu.PrefetchScalarG...  194 us
    all_to_all x8, waiting for transfers between devices, swap_all(): return lax.all_to_all(value, names, 0, 0, tiled=True)  97.5 us
    ppermute x6, waiting for transfers between devices, fold(): got = lax.ppermute(at_index(value, 1 - at), name, [(0, 1), (1, 0)])  64 us
    ppermute x6, waiting for transfers between devices, swap_by_steps(): lax.ppermute(sent, name, [(i, (i + step) % size) for i in range(size)])  62.8 us
    ppermute x1, waiting for transfers between devices, on_device(): rows = [by_seq, lax.ppermute(by_seq, 'x', [(0, 1), (1, 0)])]  41.9 us
    all_to_all x8, starting transfers between devices, swap_all(): return lax.all_to_all(value, names, 0, 0, tiled=True)  37 us
    convert_element_type x4, other arithmetic, join(): return (keep.astype(F32) + got.astype(F32)).astype(BF)  13 us
    unnamed x51, local copies, waits for them, and re-layouts  11.9 us
  transfers between devices with their start and end apart: 25, of which 12 were waited for; matrix products, arithmetic and copies ran while one was open for 8% of the time, Pallas kernels for 27%

profile of v2, /device:TPU:0, one launch (start us, length us, event | category | flops | bytes accessed | tf_op | source)
XLA Modules:
  0.0 583.3 jit_solution(14004504556563597706)
XLA Ops:
  0.7 6.4 %all-to-all-start = ((bf16[4,128,768]{2,1,0:T(8,128)(2,1)}), bf16[4,128,768]{2,1,0:T(8,128)(2,1)S(1)}, u32[]{:S(2)}, u32[]{:S(2)}) async-start(bf16[4,128,768]{2,1,0:T(8,128)(2,1)} %param.16), calls=%async_computation | async-start | bytes 1572864 | tf_op jit(solution)/shard_map/all_to_all | solution.py:828
  10.3 6.0 %shard_map.255 = bf16[8,208,768]{2,1,0:T(8,128)(2,1)} custom-call(bf16[512,768]{1,0:T(8,128)(2,1)} %bitcast.117, s32[2,512]{1,0:T(2,128)} %copy.74.t_ref, s32[2,512]{1,0:T(2,128)} %copy.75.refs_0_), custom_call_target="tpu_custom_call" | custom-call | flops 1207959552 | bytes 3350528 | tf_op jit(solution)/shard_map/pallas_call | solution.py:33
  19.4 7.7 %all-to-all-done.refs_0_ = bf16[4,128,768]{2,1,0:T(8,128)(2,1)S(1)} async-done(((bf16[4,128,768]{2,1,0:T(8,128)(2,1)}), bf16[4,128,768]{2,1,0:T(8,128)(2,1)S(1)}, u32[]{:S(2)}, u32[]{:S(2)}) %all-to-all-start) | async-done | bytes 786464 | tf_op jit(solution)/shard_map/all_to_all | solution.py:828
  35.1 41.9 %collective-permute-done.refs_1_ = bf16[4,128,768]{2,1,0:T(8,128)(2,1)} collective-permute-done((bf16[4,128,768]{2,1,0:T(8,128)(2,1)S(1)}, bf16[4,128,768]{2,1,0:T(8,128)(2,1)}, u32[]{:S(2)}, u32[]{:S(2)}) %collective-permute-start) | collective-permute-done | bytes 786464 | tf_op jit(solution)/shard_map/ppermute | solution.py:923
  77.1 7.0 %shard_map.256 = (bf16[1024,1152]{1,0:T(8,128)(2,1)}, bf16[1024,768]{1,0:T(8,128)(2,1)}) custom-call(s32[1]{0:T(128)} %bitcast.1.at_ref, bf16[4,128,768]{2,1,0:T(8,128)(2,1)} %copy-done.7, bf16[4,128,768]{2,1,0:T(8,128)(2,1)} %collective-permute-done.refs_1_, f32[1,768]{1,0:T(1,128)} %reshape.193.refs_2_.g_ref, f32[1024,128]{1,0:T(8,128)} %get-tuple-element.60.refs_3_.c_ref, ...), custom_call_target="tpu_custom_call" | custom-call | flops 1811939328 | bytes 17173508 | tf_op jit(solution)/shard_map/pallas_call | solution.py:33
  84.1 13.1 %shard_map.257 = (bf16[1024,384]{1,0:T(8,128)(2,1)}, f32[3,2,1024]{2,1,0:T(2,128)}) custom-call(bf16[1024,1152]{1,0:T(8,128)(2,1)} %get-tuple-element.62.q_ref.k_ref.v_ref, bf16[1024,1152]{1,0:T(8,128)(2,1)} %get-tuple-element.62.q_ref.k_ref.v_ref, bf16[1024,1152]{1,0:T(8,128)(2,1)} %get-tuple-element.62.q_ref.k_ref.v_ref, ...), custom_call_target="tpu_custom_call" | custom-call | flops 1610612736 | bytes 7897088 | tf_op jit(solution)/shard_map/pallas_call | solution.py:33
  97.2 4.6 all-to-all-start.2
  102.4 18.1 %all-to-all-done.2 = bf16[8,128,384]{2,1,0:T(8,128)(2,1)S(1)} async-done(((bf16[8,128,384]{2,1,0:T(8,128)(2,1)}), bf16[8,128,384]{2,1,0:T(8,128)(2,1)S(1)}, u32[]{:S(2)}, u32[]{:S(2)}) %all-to-all-start.2) | async-done | bytes 786464 | tf_op jit(solution)/shard_map/all_to_all | solution.py:828
  121.3 4.2 shard_map.258
  125.5 17.8 %shard_map.259 = (f32[512,768]{1,0:T(8,128)}, f32[512,768]{1,0:T(8,128)}, bf16[512,2048]{1,0:T(8,128)(2,1)}, bf16[512,2048]{1,0:T(8,128)(2,1)}, bf16[512,2048]{1,0:T(8,128)(2,1)}) custom-call(bf16[512,768]{1,0:T(8,128)(2,1)} %get-tuple-element.68.refs_0_.r_ref.x_ref, bf16[512,768]{1,0:T(8,128)(2,1)} %bitcast.118, bf16[768,2048]{1,0:T(8,128)(2,1)} %refs_2_.2, ...), custom_call_target="tpu_custom_call" | custom-call | flops 9663676416 | bytes 20447232 | tf_op jit(solution)/shard_map/pallas_call | solution.py:33
  143.3 12.1 %shard_map.261 = (bf16[2,2,4,3,24,2048]{5,4,3,2,1,0:T(8,128)(2,1)}, bf16[2,2,4,3,24,2048]{5,4,3,2,1,0:T(8,128)(2,1)}) custom-call(s32[1]{0:T(128)} %bitcast.12.at_ref, bf16[512,768]{1,0:T(8,128)(2,1)} %get-tuple-element.68.refs_0_.r_ref.x_ref, bf16[512,768]{1,0:T(8,128)(2,1)} %bitcast.119, bf16[512,2048]{1,0:T(8,128)(2,1)} %get-tuple-element.70.dg_ref, ...), custom_call_target="tpu_custom_call" | custom-call | flops 4831838208 | bytes 17301508 | tf_op jit(solution)/shard_map/pallas_call | solution.py:33
  155.4 5.8 shard_map.260
  161.1 4.7 all-to-all-start.3
  169.7 51.0 %all-to-all-done.3 = bf16[8,192,768]{2,1,0:T(8,128)(2,1)} async-done(((bf16[8,192,768]{2,1,0:T(8,128)(2,1)}), bf16[8,192,768]{2,1,0:T(8,128)(2,1)}, u32[]{:S(2)}, u32[]{:S(2)}) %all-to-all-start.3) | async-done | bytes 2359328 | tf_op jit(solution)/shard_map/all_to_all | solution.py:828
  220.6 6.0 %add_convert_fusion.1 = bf16[2,2,4,3,24,2048]{5,4,3,2,1,0:T(8,128)(2,1)S(1)} fusion(bf16[2,2,4,3,24,2048]{5,4,3,2,1,0:T(8,128)(2,1)} %collective-permute-done.9, bf16[2,2,4,3,24,2048]{5,4,3,2,1,0:T(8,128)(2,1)} %get-tuple-element.103), kind=kLoop, calls=%fused_computation.1 | loop fusion | flops 9437184 | bytes 14155776 | tf_op jit(solution)/shard_map/convert_element_type | solution.py:845
  231.2 49.9 %shard_map.262 = (bf16[1536,768]{1,0:T(8,128)(2,1)}, bf16[1536,768]{1,0:T(8,128)(2,1)}, bf16[1536,2048]{1,0:T(8,128)(2,1)}, bf16[1536,2048]{1,0:T(8,128)(2,1)}, ...) custom-call(s32[1]{0:T(128)} %bitcast.10.refs_0_, ...), custom_call_target="tpu_custom_call" | custom-call | flops 28991029248 | bytes 40704004 | tf_op jit(solution)/shard_map/pallas_call | solution.py:33
  281.1 4.1 all-to-all-start.4
  285.1 24.0 %shard_map.263 = (bf16[2,3,768,512]{3,2,1,0:T(8,128)(2,1)}, bf16[2,3,768,512]{3,2,1,0:T(8,128)(2,1)}, f32[768,128]{1,0:T(8,128)}) custom-call(s32[1]{0:T(128)} %bitcast.12.at_ref, bf16[1536,768]{1,0:T(8,128)(2,1)} %bitcast.11.refs_1_.x_ref, bf16[1536,768]{1,0:T(8,128)(2,1)} %get-tuple-element.78.g_ref, bf16[1536,2048]{1,0:T(8,128)(2,1)} %get-tuple-element.79.dg_ref, ...), custom_call_target="tpu_custom_call" | custom-call | flops 14495514624 | bytes 33816580 | tf_op jit(solution)/shard_map/pallas_call | solution.py:33
  318.2 20.7 %all-to-all-done.4 = bf16[8,192,768]{2,1,0:T(8,128)(2,1)S(1)} async-done(((bf16[8,192,768]{2,1,0:T(8,128)(2,1)}), bf16[8,192,768]{2,1,0:T(8,128)(2,1)S(1)}, u32[]{:S(2)}, u32[]{:S(2)}) %all-to-all-start.4) | async-done | bytes 2359328 | tf_op jit(solution)/shard_map/all_to_all | solution.py:828
  340.4 8.3 %shard_map.264 = (f32[512,768]{1,0:T(8,128)}, bf16[512,768]{1,0:T(8,128)(2,1)}, bf16[4,2,128,384]{3,2,1,0:T(8,128)(2,1)}, f32[768,128]{1,0:T(8,128)}) custom-call(f32[512,768]{1,0:T(8,128)} %get-tuple-element.67.h_ref, f32[512,768]{1,0:T(8,128)} %get-tuple-element.76.s_ref, bf16[1536,768]{1,0:T(8,128)(2,1)} %bitcast.105, s32[512,2]{1,0:T(8,128)} %copy-done.10, ...), custom_call_target="tpu_custom_call" | custom-call | flops 1811939328 | bytes 11017216 | tf_op jit(solution)/shard_map/pallas_call | solution.py:33
  364.4 12.5 %collective-permute-done.12 = bf16[3,24,2048]{2,1,0:T(8,128)(2,1)S(1)} collective-permute-done((bf16[3,24,2048]{2,1,0:T(8,128)(2,1)S(1)}, bf16[3,24,2048]{2,1,0:T(8,128)(2,1)S(1)}, u32[]{:S(2)}, u32[]{:S(2)}) %collective-permute-start.12) | collective-permute-done | bytes 294944 | tf_op jit(solution)/shard_map/ppermute | solution.py:853
  380.3 17.9 %collective-permute-done.13 = bf16[3,24,2048]{2,1,0:T(8,128)(2,1)} collective-permute-done((bf16[3,24,2048]{2,1,0:T(8,128)(2,1)S(1)}, bf16[3,24,2048]{2,1,0:T(8,128)(2,1)}, u32[]{:S(2)}, u32[]{:S(2)}) %collective-permute-start.13) | collective-permute-done | bytes 294944 | tf_op jit(solution)/shard_map/ppermute | solution.py:853
  404.9 18.9 %shard_map.266 = (bf16[1024,384]{1,0:T(8,128)(2,1)}, bf16[1024,384]{1,0:T(8,128)(2,1)}, bf16[1024,384]{1,0:T(8,128)(2,1)}) custom-call(bf16[1024,1152]{1,0:T(8,128)(2,1)} %get-tuple-element.62.q_ref.k_ref.v_ref, bf16[1024,1152]{1,0:T(8,128)(2,1)} %get-tuple-element.62.q_ref.k_ref.v_ref, bf16[1024,1152]{1,0:T(8,128)(2,1)} %get-tuple-element.62.q_ref.k_ref.v_ref, ...), custom_call_target="tpu_custom_call" | custom-call | flops 4026531840 | bytes 11304960 | tf_op jit(solution)/shard_map/pallas_call | solution.py:33
  423.8 7.3 %shard_map.267 = (bf16[2,4,128,768]{3,2,1,0:T(8,128)(2,1)}, f32[768,128]{1,0:T(8,128)}) custom-call(s32[1]{0:T(128)} %bitcast.1.at_ref, bf16[1024,384]{1,0:T(8,128)(2,1)} %get-tuple-element.89.q_ref.refs_1_, bf16[1024,384]{1,0:T(8,128)(2,1)} %get-tuple-element.90.k_ref.refs_2_, bf16[1024,384]{1,0:T(8,128)(2,1)} %get-tuple-element.91.v_ref.refs_3_, ...), custom_call_target="tpu_custom_call" | custom-call | flops 1811939328 | bytes 16515076 | tf_op jit(solution)/shard_map/pallas_call | solution.py:33
  431.1 6.8 %shard_map.270 = (bf16[2,4,2,24,1280]{4,3,2,1,0:T(8,128)(2,1)}, bf16[2,4,2,24,1280]{4,3,2,1,0:T(8,128)(2,1)}) custom-call(s32[1]{0:T(128)} %bitcast.12.at_ref, bf16[1024,768]{1,0:T(8,128)(2,1)} %get-tuple-element.98.refs_0_, bf16[1024,384]{1,0:T(8,128)(2,1)} %get-tuple-element.89.q_ref.refs_1_, bf16[1024,384]{1,0:T(8,128)(2,1)} %get-tuple-element.90.k_ref.refs_2_, ...), custom_call_target="tpu_custom_call" | custom-call | flops 1811939328 | bytes 6291460 | tf_op jit(solution)/shard_map/pallas_call | solution.py:33
  437.9 5.3 add_convert_fusion
  452.8 55.1 %collective-permute-done.6 = bf16[4,2,24,896]{3,2,1,0:T(8,128)(2,1)S(1)} collective-permute-done((bf16[4,2,24,896]{3,2,1,0:T(8,128)(2,1)S(1)}, bf16[4,2,24,896]{3,2,1,0:T(8,128)(2,1)S(1)}, u32[]{:S(2)}, u32[]{:S(2)}) %collective-permute-start.6) | collective-permute-done | bytes 344096 | tf_op jit(solution)/shard_map/ppermute | solution.py:839
  509.0 8.9 %collective-permute-done.8 = bf16[4,2,24,1280]{3,2,1,0:T(8,128)(2,1)S(1)} collective-permute-done((bf16[4,2,24,1280]{3,2,1,0:T(8,128)(2,1)S(1)}, bf16[4,2,24,1280]{3,2,1,0:T(8,128)(2,1)S(1)}, u32[]{:S(2)}, u32[]{:S(2)}) %collective-permute-start.8) | collective-permute-done | bytes 491552 | tf_op jit(solution)/shard_map/ppermute | solution.py:839
  519.0 6.0 %all-to-all-start.7 = ((bf16[8,24,2176]{2,1,0:T(8,128)(2,1)}), bf16[8,24,2176]{2,1,0:T(8,128)(2,1)S(1)}, u32[]{:S(2)}, u32[]{:S(2)}) async-start(bf16[8,24,2176]{2,1,0:T(8,128)(2,1)} %bitcast.38), calls=%async_computation.7 | async-start | bytes 1671168 | tf_op jit(solution)/shard_map/all_to_all | solution.py:828
  534.0 9.9 %collective-permute-done.4.refs_3_ = bf16[128,768]{1,0:T(8,128)(2,1)S(1)} collective-permute-done((bf16[128,768]{1,0:T(8,128)(2,1)S(1)}, bf16[128,768]{1,0:T(8,128)(2,1)S(1)}, u32[]{:S(2)}, u32[]{:S(2)}) %collective-permute-start.4) | collective-permute-done | bytes 196640 | tf_op jit(solution)/shard_map/ppermute | solution.py:853
  543.9 19.1 %collective-permute-done.3.refs_2_ = bf16[128,768]{1,0:T(8,128)(2,1)S(1)} collective-permute-done((bf16[128,768]{1,0:T(8,128)(2,1)S(1)}, bf16[128,768]{1,0:T(8,128)(2,1)S(1)}, u32[]{:S(2)}, u32[]{:S(2)}) %collective-permute-start.3) | collective-permute-done | bytes 196640 | tf_op jit(solution)/shard_map/ppermute | solution.py:853
  574.1 5.0 shard_map.265
  (139 shorter events, 96.0 us)
Async XLA Ops:
  0.6 9.6 %copy-start = (s32[4,1024]{1,0:T(4,128)S(1)}, s32[4,1024]{1,0:T(4,128)}, u32[]{:S(2)}) copy-start(s32[4,1024]{1,0:T(4,128)} %param.17) | copy-start | bytes 49156
  0.7 26.5 %all-to-all-start = ((bf16[4,128,768]{2,1,0:T(8,128)(2,1)}), bf16[4,128,768]{2,1,0:T(8,128)(2,1)S(1)}, u32[]{:S(2)}, u32[]{:S(2)}) async-start(bf16[4,128,768]{2,1,0:T(8,128)(2,1)} %param.16), calls=%async_computation | async-start | bytes 1572864 | tf_op jit(solution)/shard_map/all_to_all | solution.py:828
  27.1 70.1 %all-to-all-start.1 = ((bf16[8,208,768]{2,1,0:T(8,128)(2,1)}), bf16[8,208,768]{2,1,0:T(8,128)(2,1)S(1)}, u32[]{:S(2)}, u32[]{:S(2)}) async-start(bf16[8,208,768]{2,1,0:T(8,128)(2,1)} %shard_map.255), calls=%async_computation.1 | async-start | bytes 5111808 | tf_op jit(solution)/shard_map/all_to_all | solution.py:828
  30.9 46.1 %collective-permute-start = (bf16[4,128,768]{2,1,0:T(8,128)(2,1)S(1)}, bf16[4,128,768]{2,1,0:T(8,128)(2,1)}, u32[]{:S(2)}, u32[]{:S(2)}) collective-permute-start(bf16[4,128,768]{2,1,0:T(8,128)(2,1)S(1)} %all-to-all-done.refs_0_), channel_id=1, source_target_pairs={{0,1},{1,0},{2,3},{3,2},{4,5},{5,4},{6,7},{7,6},{8,9},{9,8},{10,11... | collective-permute-start | bytes 2359304 | tf_op jit(solution)/shard_map/ppermute | solution.py:923
  84.1 17.7 %copy-start.22 = (bf16[768]{0:T(1024)(128)(2,1)S(1)}, bf16[768]{0:T(1024)(128)(2,1)}, u32[]{:S(2)}) copy-start(bf16[768]{0:T(1024)(128)(2,1)} %param.24) | copy-start | bytes 4612
  97.2 23.3 %all-to-all-start.2 = ((bf16[8,128,384]{2,1,0:T(8,128)(2,1)}), bf16[8,128,384]{2,1,0:T(8,128)(2,1)S(1)}, u32[]{:S(2)}, u32[]{:S(2)}) async-start(bf16[8,128,384]{2,1,0:T(8,128)(2,1)} %bitcast.124), calls=%async_computation.2 | async-start | bytes 1572864 | tf_op jit(solution)/shard_map/all_to_all | solution.py:828
  155.4 65.3 %collective-permute-start.9 = (bf16[2,2,4,3,24,2048]{5,4,3,2,1,0:T(8,128)(2,1)}, bf16[2,2,4,3,24,2048]{5,4,3,2,1,0:T(8,128)(2,1)}, u32[]{:S(2)}, u32[]{:S(2)}) collective-permute-start(bf16[2,2,4,3,24,2048]{5,4,3,2,1,0:T(8,128)(2,1)} %get-tuple-element.73), channel_id=1, source_target_pairs={{0,8},{8,0},{1,9},{9,1},{2,10},{10,2},{3,11},{11,3},{4,12},{12,4},... | collective-permute-start | bytes 14155784 | tf_op jit(solution)/shard_map/ppermute | solution.py:844
  161.1 59.5 %all-to-all-start.3 = ((bf16[8,192,768]{2,1,0:T(8,128)(2,1)}), bf16[8,192,768]{2,1,0:T(8,128)(2,1)}, u32[]{:S(2)}, u32[]{:S(2)}) async-start(bf16[8,192,768]{2,1,0:T(8,128)(2,1)} %shard_map.260), calls=%async_computation.3 | async-start | bytes 4718592 | tf_op jit(solution)/shard_map/all_to_all | solution.py:828
  229.6 79.6 %collective-permute-start.10 = (bf16[2,4,3,24,2048]{4,3,2,1,0:T(8,128)(2,1)}, bf16[2,4,3,24,2048]{4,3,2,1,0:T(8,128)(2,1)}, u32[]{:S(2)}, u32[]{:S(2)}) collective-permute-start(bf16[2,4,3,24,2048]{4,3,2,1,0:T(8,128)(2,1)} %dynamic-slice_bitcast_fusion.1), channel_id=1, source_target_pairs={{0,16},{16,0},{1,17},{17,1},{2,18},{18,2},{3,19},{19,3},{4,20},{20... | collective-permute-start | bytes 7077896 | tf_op jit(solution)/shard_map/ppermute | solution.py:839
  281.1 57.9 %all-to-all-start.4 = ((bf16[8,192,768]{2,1,0:T(8,128)(2,1)}), bf16[8,192,768]{2,1,0:T(8,128)(2,1)S(1)}, u32[]{:S(2)}, u32[]{:S(2)}) async-start(bf16[8,192,768]{2,1,0:T(8,128)(2,1)} %bitcast.114), calls=%async_computation.4 | async-start | bytes 4718592 | tf_op jit(solution)/shard_map/all_to_all | solution.py:828
  309.1 128.8 %collective-permute-start.15 = (bf16[2,3,768,512]{3,2,1,0:T(8,128)(2,1)}, bf16[2,3,768,512]{3,2,1,0:T(8,128)(2,1)}, u32[]{:S(2)}, u32[]{:S(2)}) collective-permute-start(bf16[2,3,768,512]{3,2,1,0:T(8,128)(2,1)} %get-tuple-element.83), channel_id=1, source_target_pairs={{0,8},{8,0},{1,9},{9,1},{2,10},{10,2},{3,11},{11,3},{4,12},{12,4},... | collective-permute-start | bytes 14155784 | tf_op jit(solution)/shard_map/ppermute | solution.py:844
  315.2 37.1 %collective-permute-start.11 = (bf16[4,3,24,2048]{3,2,1,0:T(8,128)(2,1)}, bf16[4,3,24,2048]{3,2,1,0:T(8,128)(2,1)}, u32[]{:S(2)}, u32[]{:S(2)}) collective-permute-start(bf16[4,3,24,2048]{3,2,1,0:T(8,128)(2,1)} %dynamic-slice_bitcast_fusion.2), channel_id=1, source_target_pairs={{0,1},{1,0},{2,3},{3,2},{4,5},{5,4},{6,7},{7,6},{8,9},{9,8},{10,11... | collective-permute-start | bytes 3538952 | tf_op jit(solution)/shard_map/ppermute | solution.py:839
  348.7 51.5 %all-to-all-start.5 = ((bf16[8,128,384]{2,1,0:T(8,128)(2,1)}), bf16[8,128,384]{2,1,0:T(8,128)(2,1)S(1)}, u32[]{:S(2)}, u32[]{:S(2)}) async-start(bf16[8,128,384]{2,1,0:T(8,128)(2,1)} %bitcast.123), calls=%async_computation.5 | async-start | bytes 1572864 | tf_op jit(solution)/shard_map/all_to_all | solution.py:828
  352.4 7.3 %copy-start.15 = (f32[768,128]{1,0:T(8,128)S(1)}, f32[768,128]{1,0:T(8,128)}, u32[]{:S(2)}) copy-start(f32[768,128]{1,0:T(8,128)} %get-tuple-element.94) | copy-start | bytes 1179652
  352.4 7.3 %copy-start.16 = (f32[768,128]{1,0:T(8,128)S(1)}, f32[768,128]{1,0:T(8,128)}, u32[]{:S(2)}) copy-start(f32[768,128]{1,0:T(8,128)} %get-tuple-element.95) | copy-start | bytes 1179652
  354.7 22.2 %collective-permute-start.12 = (bf16[3,24,2048]{2,1,0:T(8,128)(2,1)S(1)}, bf16[3,24,2048]{2,1,0:T(8,128)(2,1)S(1)}, u32[]{:S(2)}, u32[]{:S(2)}) collective-permute-start(bf16[3,24,2048]{2,1,0:T(8,128)(2,1)S(1)} %get-tuple-element.173), channel_id=1, source_target_pairs={{0,2},{2,4},{4,6},{6,0},{1,3},{3,5},{5,7},{7,1},{8,10},{10,12},{12... | collective-permute-start | bytes 884744 | tf_op jit(solution)/shard_map/ppermute | solution.py:853
  356.7 23.6 %collective-permute-start.14 = (bf16[3,24,2048]{2,1,0:T(8,128)(2,1)S(1)}, bf16[3,24,2048]{2,1,0:T(8,128)(2,1)}, u32[]{:S(2)}, u32[]{:S(2)}) collective-permute-start(bf16[3,24,2048]{2,1,0:T(8,128)(2,1)S(1)} %get-tuple-element.174), channel_id=1, source_target_pairs={{0,6},{2,0},{4,2},{6,4},{1,7},{3,1},{5,3},{7,5},{8,14},{10,8},{12,... | collective-permute-start | bytes 884744 | tf_op jit(solution)/shard_map/ppermute | solution.py:853
  358.6 39.6 %collective-permute-start.13 = (bf16[3,24,2048]{2,1,0:T(8,128)(2,1)S(1)}, bf16[3,24,2048]{2,1,0:T(8,128)(2,1)}, u32[]{:S(2)}, u32[]{:S(2)}) collective-permute-start(bf16[3,24,2048]{2,1,0:T(8,128)(2,1)S(1)} %get-tuple-element.175), channel_id=1, source_target_pairs={{0,4},{2,6},{4,0},{6,2},{1,5},{3,7},{5,1},{7,3},{8,12},{10,14},{12... | collective-permute-start | bytes 884744 | tf_op jit(solution)/shard_map/ppermute | solution.py:853
  364.4 82.3 %collective-permute-start.5 = (bf16[2,4,2,24,896]{4,3,2,1,0:T(8,128)(2,1)}, bf16[2,4,2,24,896]{4,3,2,1,0:T(8,128)(2,1)}, u32[]{:S(2)}, u32[]{:S(2)}) collective-permute-start(bf16[2,4,2,24,896]{4,3,2,1,0:T(8,128)(2,1)} %get-tuple-element.97), channel_id=1, source_target_pairs={{0,8},{8,0},{1,9},{9,1},{2,10},{10,2},{3,11},{11,3},{4,12},{12,4},... | collective-permute-start | bytes 2064392 | tf_op jit(solution)/shard_map/ppermute | solution.py:844
  401.1 117.9 %all-to-all-start.6 = ((bf16[8,192,768]{2,1,0:T(8,128)(2,1)}), bf16[8,192,768]{2,1,0:T(8,128)(2,1)S(1)}, u32[]{:S(2)}, u32[]{:S(2)}) async-start(bf16[8,192,768]{2,1,0:T(8,128)(2,1)} %bitcast.113), calls=%async_computation.6 | async-start | bytes 4718592 | tf_op jit(solution)/shard_map/all_to_all | solution.py:828
  437.9 13.7 %collective-permute-start.7 = (bf16[2,4,2,24,1280]{4,3,2,1,0:T(8,128)(2,1)}, bf16[2,4,2,24,1280]{4,3,2,1,0:T(8,128)(2,1)S(1)}, u32[]{:S(2)}, u32[]{:S(2)}) collective-permute-start(bf16[2,4,2,24,1280]{4,3,2,1,0:T(8,128)(2,1)} %get-tuple-element.101), channel_id=1, source_target_pairs={{0,8},{8,0},{1,9},{9,1},{2,10},{10,2},{3,11},{11,3},{4,12},{12,4},... | collective-permute-start | bytes 2949128 | tf_op jit(solution)/shard_map/ppermute | solution.py:844
  446.1 121.0 %collective-permute-start.16 = (bf16[3,768,512]{2,1,0:T(8,128)(2,1)}, bf16[3,768,512]{2,1,0:T(8,128)(2,1)}, u32[]{:S(2)}, u32[]{:S(2)}) collective-permute-start(bf16[3,768,512]{2,1,0:T(8,128)(2,1)} %dynamic-slice_bitcast_fusion), channel_id=1, source_target_pairs={{0,16},{16,0},{1,17},{17,1},{2,18},{18,2},{3,19},{19,3},{4,20},{20... | collective-permute-start | bytes 7077896 | tf_op jit(solution)/shard_map/ppermute | solution.py:839
  448.2 59.6 %collective-permute-start.6 = (bf16[4,2,24,896]{3,2,1,0:T(8,128)(2,1)S(1)}, bf16[4,2,24,896]{3,2,1,0:T(8,128)(2,1)S(1)}, u32[]{:S(2)}, u32[]{:S(2)}) collective-permute-start(bf16[4,2,24,896]{3,2,1,0:T(8,128)(2,1)S(1)} %dynamic-slice_bitcast_fusion.5), channel_id=1, source_target_pairs={{0,16},{16,0},{1,17},{17,1},{2,18},{18,2},{3,19},{19,3},{4,20},{20... | collective-permute-start | bytes 1032200 | tf_op jit(solution)/shard_map/ppermute | solution.py:839
  449.6 58.3 %collective-permute-start.1 = (bf16[4,128,768]{2,1,0:T(8,128)(2,1)S(1)}, bf16[4,128,768]{2,1,0:T(8,128)(2,1)S(1)}, u32[]{:S(2)}, u32[]{:S(2)}) collective-permute-start(bf16[4,128,768]{2,1,0:T(8,128)(2,1)S(1)} %dynamic-slice_bitcast_fusion.3), channel_id=1, source_target_pairs={{0,1},{1,0},{2,3},{3,2},{4,5},{5,4},{6,7},{7,6},{8,9},{9,8},{10,11... | collective-permute-start | bytes 2359304 | tf_op jit(solution)/shard_map/ppermute | solution.py:839
  452.0 66.0 %collective-permute-start.8 = (bf16[4,2,24,1280]{3,2,1,0:T(8,128)(2,1)S(1)}, bf16[4,2,24,1280]{3,2,1,0:T(8,128)(2,1)S(1)}, u32[]{:S(2)}, u32[]{:S(2)}) collective-permute-start(bf16[4,2,24,1280]{3,2,1,0:T(8,128)(2,1)S(1)} %dynamic-slice_bitcast_fusion.4), channel_id=1, source_target_pairs={{0,16},{16,0},{1,17},{17,1},{2,18},{18,2},{3,19},{19,3},{4,20},{20... | collective-permute-start | bytes 1474568 | tf_op jit(solution)/shard_map/ppermute | solution.py:839
  519.0 48.2 %copy-start.4 = (bf16[8,192,768]{2,1,0:T(8,128)(2,1)}, bf16[8,192,768]{2,1,0:T(8,128)(2,1)S(1)}, u32[]{:S(2)}) copy-start(bf16[8,192,768]{2,1,0:T(8,128)(2,1)S(1)} %all-to-all-done.6) | copy-start | bytes 7077892
  519.0 60.1 %all-to-all-start.7 = ((bf16[8,24,2176]{2,1,0:T(8,128)(2,1)}), bf16[8,24,2176]{2,1,0:T(8,128)(2,1)S(1)}, u32[]{:S(2)}, u32[]{:S(2)}) async-start(bf16[8,24,2176]{2,1,0:T(8,128)(2,1)} %bitcast.38), calls=%async_computation.7 | async-start | bytes 1671168 | tf_op jit(solution)/shard_map/all_to_all | solution.py:828
  526.9 17.0 %collective-permute-start.4 = (bf16[128,768]{1,0:T(8,128)(2,1)S(1)}, bf16[128,768]{1,0:T(8,128)(2,1)S(1)}, u32[]{:S(2)}, u32[]{:S(2)}) collective-permute-start(bf16[128,768]{1,0:T(8,128)(2,1)S(1)} %get-tuple-element.178), channel_id=1, source_target_pairs={{0,6},{2,0},{4,2},{6,4},{1,7},{3,1},{5,3},{7,5},{8,14},{10,8},{12,... | collective-permute-start | bytes 589832 | tf_op jit(solution)/shard_map/ppermute | solution.py:853
  530.9 32.1 %collective-permute-start.3 = (bf16[128,768]{1,0:T(8,128)(2,1)S(1)}, bf16[128,768]{1,0:T(8,128)(2,1)S(1)}, u32[]{:S(2)}, u32[]{:S(2)}) collective-permute-start(bf16[128,768]{1,0:T(8,128)(2,1)S(1)} %get-tuple-element.179), channel_id=1, source_target_pairs={{0,4},{2,6},{4,0},{6,2},{1,5},{3,7},{5,1},{7,3},{8,12},{10,14},{12... | collective-permute-start | bytes 589832 | tf_op jit(solution)/shard_map/ppermute | solution.py:853
  530.9 32.1 %collective-permute-start.2 = (bf16[128,768]{1,0:T(8,128)(2,1)S(1)}, bf16[128,768]{1,0:T(8,128)(2,1)S(1)}, u32[]{:S(2)}, u32[]{:S(2)}) collective-permute-start(bf16[128,768]{1,0:T(8,128)(2,1)S(1)} %get-tuple-element.180), channel_id=1, source_target_pairs={{0,2},{2,4},{4,6},{6,0},{1,3},{3,5},{5,7},{7,1},{8,10},{10,12},{12... | collective-permute-start | bytes 589832 | tf_op jit(solution)/shard_map/ppermute | solution.py:853
  543.9 19.1 %copy-start.17 = (bf16[128,768]{1,0:T(8,128)(2,1)}, bf16[128,768]{1,0:T(8,128)(2,1)S(1)}, u32[]{:S(2)}) copy-start(bf16[128,768]{1,0:T(8,128)(2,1)S(1)} %collective-permute-done.4.refs_3_) | copy-start | bytes 589828
  574.1 9.0 %copy-start.1 = (s32[4,1024]{1,0:T(4,128)S(1)}, s32[4,1024]{1,0:T(4,128)}, u32[]{:S(2)}) copy-start(s32[4,1024]{1,0:T(4,128)} %param.17) | copy-start | bytes 49156
  (16 other events, 48.6 us)

commit v3 on v2

--- a/solution.py
+++ b/solution.py
@@ -918,11 +918,12 @@
     by_seq, cosine, sine, seg_col, grad_sent = lax.optimization_barrier(
         (by_seq, cosine, sine, seg_col, grad_sent)
     )
-    grad_came = swap_all(grad_sent, ranks)
     if parts == 2:
         rows = [by_seq, lax.ppermute(by_seq, "x", [(0, 1), (1, 0)])]
     else:
         rows = [lax.all_gather(by_seq, "x", axis=0, tiled=False)]
+    *rows, grad_sent = lax.optimization_barrier((*rows, grad_sent))
+    grad_came = swap_all(grad_sent, ranks)
 
     qkv, normed = project(rows, attn_scale, weights, group, cosine, sine, x_ref, parts)
     attended, lse = (attend if fused else plain_attend)(qkv, seg_row, seg_col)
@@ -935,7 +936,7 @@
     received = swap_all(sent, ranks).reshape(-1, width)
 
     shared_out, shared_back, hid, dg, du = feed_forward(
-        branch_in, flat_cot, shared_gate, shared_up, shared_down
+        after(branch_in, sent), flat_cot, shared_gate, shared_up, shared_down
     )
     keep, give = shared_weight_grads(branch_in, flat_cot, dg, du, hid, sizes, core_ref)
     shared_sums = fold(join(keep, give, "core"), "y")
@@ -953,7 +954,7 @@
     )
     back_rows = after(back_rows, give)
     expert_sums = fold(join(keep, give, "core"), "y")
-    shared_sums = swap_by_steps(fold(shared_sums, "x"), "z")
+    shared_sums = fold(shared_sums, "x")
 
     grad_hidden, grad_attn, grad_att, grad_ffn = middle_back(
         hidden, shared_back, back_rows, target, flat_cot, ffn_scale, w_out, parts, span
@@ -985,6 +986,7 @@
     token_grad = first_norm_back(flat_tokens, attn_scale, pieces, grad_hidden, z_ref)
     layer_out = layer_end(hidden, shared_out, made_rows, target).reshape(tokens.shape)
 
+    shared_sums = swap_by_steps(after(shared_sums, *pieces), "z")
     last = after(jnp.concatenate([out_sums, qkv_sums], axis=-1), made_rows)
     each, cols = last.shape[-2:]
     last = swap_all(last.reshape(experts, each, cols), ranks).astype(F32)

time: 593 us -> 541 us (0.912)
  waiting for transfers between devices: 266 us -> 214 us
    ppermute x6, waiting for transfers between devices: 62.8 us -> 29.8 us  [swap_by_steps(): lax.ppermute(sent, name, [(i, (i + step) % size) for i in range(size)])]
    ppermute x1, waiting for transfers between devices: 41.9 us -> 17.2 us  [on_device(): rows = [by_seq, lax.ppermute(by_seq, 'x', [(0, 1), (1, 0)])]]
    ppermute x6, waiting for transfers between devices: 64 us -> 84.8 us  [fold(): got = lax.ppermute(at_index(value, 1 - at), name, [(0, 1), (1, 0)])]
    all_to_all x8, waiting for transfers between devices: 97.5 us -> 81.7 us  [swap_all(): return lax.all_to_all(value, names, 0, 0, tiled=True)]
    unnamed x51 -> x45, local copies, waits for them, and re-layouts: 11.9 us -> 9.65 us
  transfers between devices with their start and end apart: 25 -> 25, of which waited for: 12 -> 11; matrix products, arithmetic and copies ran while one was open for 8% -> 10% of each run, Pallas kernels for 27% -> 34%
where the time goes in v3:
time: 541 us; the launch traced here: 534 us
  waiting for transfers between devices  214 us (40%)
  Pallas kernels  193 us (36%)
  starting transfers between devices  61 us (11%)
  other arithmetic  32.8 us (6%)
  local copies, waits for them, and re-layouts  31.7 us (6%)
    pallas_call x16, Pallas kernels, call(): pl.pallas_call(body, out_shape=out_shape, grid_spec=pltpu.PrefetchScalarG...  193 us
    ppermute x6, waiting for transfers between devices, fold(): got = lax.ppermute(at_index(value, 1 - at), name, [(0, 1), (1, 0)])  84.8 us
    all_to_all x8, waiting for transfers between devices, swap_all(): return lax.all_to_all(value, names, 0, 0, tiled=True)  81.7 us
    all_to_all x8, starting transfers between devices, swap_all(): return lax.all_to_all(value, names, 0, 0, tiled=True)  37.5 us
    ppermute x6, waiting for transfers between devices, swap_by_steps(): lax.ppermute(sent, name, [(i, (i + step) % size) for i in range(size)])  29.8 us
    ppermute x1, waiting for transfers between devices, on_device(): rows = [by_seq, lax.ppermute(by_seq, 'x', [(0, 1), (1, 0)])]  17.2 us
    ppermute x6, starting transfers between devices, swap_by_steps(): lax.ppermute(sent, name, [(i, (i + step) % size) for i in range(size)])  13 us
    convert_element_type x4, other arithmetic, join(): return (keep.astype(F32) + got.astype(F32)).astype(BF)  12.9 us
  transfers between devices with their start and end apart: 25, of which 11 were waited for; matrix products, arithmetic and copies ran while one was open for 10% of the time, Pallas kernels for 34%

profile of v3, /device:TPU:0, one launch (start us, length us, event | category | flops | bytes accessed | tf_op | source)
XLA Modules:
  0.0 533.7 jit_solution(2242868837645479018)
XLA Ops:
  0.7 6.4 %all-to-all-start = ((bf16[4,128,768]{2,1,0:T(8,128)(2,1)}), bf16[4,128,768]{2,1,0:T(8,128)(2,1)S(1)}, u32[]{:S(2)}, u32[]{:S(2)}) async-start(bf16[4,128,768]{2,1,0:T(8,128)(2,1)} %param.16), calls=%async_computation | async-start | bytes 1572864 | tf_op jit(solution)/shard_map/all_to_all | solution.py:828
  10.3 6.0 %shard_map.255 = bf16[8,208,768]{2,1,0:T(8,128)(2,1)} custom-call(bf16[512,768]{1,0:T(8,128)(2,1)} %bitcast.116, s32[2,512]{1,0:T(2,128)} %copy.74.t_ref, s32[2,512]{1,0:T(2,128)} %copy.75.refs_0_), custom_call_target="tpu_custom_call" | custom-call | flops 1207959552 | bytes 3350528 | tf_op jit(solution)/shard_map/pallas_call | solution.py:33
  19.4 7.8 %all-to-all-done.refs_0_ = bf16[4,128,768]{2,1,0:T(8,128)(2,1)S(1)} async-done(((bf16[4,128,768]{2,1,0:T(8,128)(2,1)}), bf16[4,128,768]{2,1,0:T(8,128)(2,1)S(1)}, u32[]{:S(2)}, u32[]{:S(2)}) %all-to-all-start) | async-done | bytes 786464 | tf_op jit(solution)/shard_map/all_to_all | solution.py:828
  28.6 17.2 %collective-permute-done.refs_1_ = bf16[4,128,768]{2,1,0:T(8,128)(2,1)} collective-permute-done((bf16[4,128,768]{2,1,0:T(8,128)(2,1)S(1)}, bf16[4,128,768]{2,1,0:T(8,128)(2,1)}, u32[]{:S(2)}, u32[]{:S(2)}) %collective-permute-start) | collective-permute-done | bytes 786464 | tf_op jit(solution)/shard_map/ppermute | solution.py:922
  51.7 7.0 %shard_map.256 = (bf16[1024,1152]{1,0:T(8,128)(2,1)}, bf16[1024,768]{1,0:T(8,128)(2,1)}) custom-call(s32[1]{0:T(128)} %bitcast.1.at_ref, bf16[4,128,768]{2,1,0:T(8,128)(2,1)} %copy-done.5, bf16[4,128,768]{2,1,0:T(8,128)(2,1)} %collective-permute-done.refs_1_, f32[1,768]{1,0:T(1,128)} %reshape.193.refs_2_.g_ref, f32[1024,128]{1,0:T(8,128)} %get-tuple-element.68.refs_3_.c_ref, ...), custom_call_target="tpu_custom_call" | custom-call | flops 1811939328 | bytes 17173508 | tf_op jit(solution)/shard_map/pallas_call | solution.py:33
  58.6 13.1 %shard_map.257 = (bf16[1024,384]{1,0:T(8,128)(2,1)}, f32[3,2,1024]{2,1,0:T(2,128)}) custom-call(bf16[1024,1152]{1,0:T(8,128)(2,1)} %get-tuple-element.70.q_ref.k_ref.v_ref, bf16[1024,1152]{1,0:T(8,128)(2,1)} %get-tuple-element.70.q_ref.k_ref.v_ref, bf16[1024,1152]{1,0:T(8,128)(2,1)} %get-tuple-element.70.q_ref.k_ref.v_ref, ...), custom_call_target="tpu_custom_call" | custom-call | flops 1610612736 | bytes 7897088 | tf_op jit(solution)/shard_map/pallas_call | solution.py:33
  71.8 34.4 %all-to-all-done.1 = bf16[8,208,768]{2,1,0:T(8,128)(2,1)S(1)} async-done(((bf16[8,208,768]{2,1,0:T(8,128)(2,1)}), bf16[8,208,768]{2,1,0:T(8,128)(2,1)S(1)}, u32[]{:S(2)}, u32[]{:S(2)}) %all-to-all-start.1) | async-done | bytes 2555936 | tf_op jit(solution)/shard_map/all_to_all | solution.py:828
  110.3 19.8 %all-to-all-done.2 = bf16[8,128,384]{2,1,0:T(8,128)(2,1)S(1)} async-done(((bf16[8,128,384]{2,1,0:T(8,128)(2,1)}), bf16[8,128,384]{2,1,0:T(8,128)(2,1)S(1)}, u32[]{:S(2)}, u32[]{:S(2)}) %all-to-all-start.2) | async-done | bytes 786464 | tf_op jit(solution)/shard_map/all_to_all | solution.py:828
  131.0 4.2 shard_map.258
  135.2 5.7 %shard_map.259 = bf16[8,192,768]{2,1,0:T(8,128)(2,1)} custom-call(bf16[512,768]{1,0:T(8,128)(2,1)} %get-tuple-element.77.r_ref.refs_0_.x_ref, s32[2,512]{1,0:T(2,128)} %copy.74.t_ref), custom_call_target="tpu_custom_call" | custom-call | flops 1207959552 | bytes 3149824 | tf_op jit(solution)/shard_map/pallas_call | solution.py:33
  140.9 4.5 all-to-all-start.3
  145.4 17.8 %shard_map.260 = (f32[512,768]{1,0:T(8,128)}, f32[512,768]{1,0:T(8,128)}, bf16[512,2048]{1,0:T(8,128)(2,1)}, bf16[512,2048]{1,0:T(8,128)(2,1)}, bf16[512,2048]{1,0:T(8,128)(2,1)}) custom-call(bf16[512,768]{1,0:T(8,128)(2,1)} %get-tuple-element.77.r_ref.refs_0_.x_ref, bf16[512,768]{1,0:T(8,128)(2,1)} %bitcast.117, bf16[768,2048]{1,0:T(8,128)(2,1)} %refs_2_.2, ...), custom_call_target="tpu_custom_call" | custom-call | flops 9663676416 | bytes 20447232 | tf_op jit(solution)/shard_map/pallas_call | solution.py:33
  163.2 12.0 %shard_map.261 = (bf16[2,2,4,3,24,2048]{5,4,3,2,1,0:T(8,128)(2,1)}, bf16[2,2,4,3,24,2048]{5,4,3,2,1,0:T(8,128)(2,1)}) custom-call(s32[1]{0:T(128)} %bitcast.12.at_ref, bf16[512,768]{1,0:T(8,128)(2,1)} %get-tuple-element.77.r_ref.refs_0_.x_ref, bf16[512,768]{1,0:T(8,128)(2,1)} %bitcast.118, bf16[512,2048]{1,0:T(8,128)(2,1)} %get-tuple-element.79.dg_ref, ...), custom_call_target="tpu_custom_call" | custom-call | flops 4831838208 | bytes 17301508 | tf_op jit(solution)/shard_map/pallas_call | solution.py:33
  179.0 19.8 %all-to-all-done.3 = bf16[8,192,768]{2,1,0:T(8,128)(2,1)} async-done(((bf16[8,192,768]{2,1,0:T(8,128)(2,1)}), bf16[8,192,768]{2,1,0:T(8,128)(2,1)}, u32[]{:S(2)}, u32[]{:S(2)}) %all-to-all-start.3) | async-done | bytes 2359328 | tf_op jit(solution)/shard_map/all_to_all | solution.py:828
  198.7 49.9 %shard_map.262 = (bf16[1536,768]{1,0:T(8,128)(2,1)}, bf16[1536,768]{1,0:T(8,128)(2,1)}, bf16[1536,2048]{1,0:T(8,128)(2,1)}, bf16[1536,2048]{1,0:T(8,128)(2,1)}, ...) custom-call(s32[1]{0:T(128)} %bitcast.10.refs_0_, ...), custom_call_target="tpu_custom_call" | custom-call | flops 28991029248 | bytes 40704004 | tf_op jit(solution)/shard_map/pallas_call | solution.py:33
  248.7 4.6 all-to-all-start.4
  253.3 6.0 %add_convert_fusion.1 = bf16[2,2,4,3,24,2048]{5,4,3,2,1,0:T(8,128)(2,1)S(1)} fusion(bf16[2,2,4,3,24,2048]{5,4,3,2,1,0:T(8,128)(2,1)} %collective-permute-done.9, bf16[2,2,4,3,24,2048]{5,4,3,2,1,0:T(8,128)(2,1)} %get-tuple-element.112), kind=kLoop, calls=%fused_computation.1 | loop fusion | flops 9437184 | bytes 14155776 | tf_op jit(solution)/shard_map/convert_element_type | solution.py:845
  262.9 24.0 %shard_map.263 = (bf16[2,3,768,512]{3,2,1,0:T(8,128)(2,1)}, bf16[2,3,768,512]{3,2,1,0:T(8,128)(2,1)}, f32[768,128]{1,0:T(8,128)}) custom-call(s32[1]{0:T(128)} %bitcast.12.at_ref, bf16[1536,768]{1,0:T(8,128)(2,1)} %bitcast.11.refs_1_.x_ref, bf16[1536,768]{1,0:T(8,128)(2,1)} %get-tuple-element.87.g_ref, bf16[1536,2048]{1,0:T(8,128)(2,1)} %get-tuple-element.88.dg_ref, ...), custom_call_target="tpu_custom_call" | custom-call | flops 14495514624 | bytes 33816580 | tf_op jit(solution)/shard_map/pallas_call | solution.py:33
  287.0 26.7 %collective-permute-done.10 = bf16[2,4,3,24,2048]{4,3,2,1,0:T(8,128)(2,1)} collective-permute-done((bf16[2,4,3,24,2048]{4,3,2,1,0:T(8,128)(2,1)S(1)}, bf16[2,4,3,24,2048]{4,3,2,1,0:T(8,128)(2,1)}, u32[]{:S(2)}, u32[]{:S(2)}) %collective-permute-start.10) | collective-permute-done | bytes 2359328 | tf_op jit(solution)/shard_map/ppermute | solution.py:839
  319.8 8.4 %shard_map.264 = (f32[512,768]{1,0:T(8,128)}, bf16[512,768]{1,0:T(8,128)(2,1)}, bf16[4,2,128,384]{3,2,1,0:T(8,128)(2,1)}, f32[768,128]{1,0:T(8,128)}) custom-call(f32[512,768]{1,0:T(8,128)} %get-tuple-element.75.h_ref, f32[512,768]{1,0:T(8,128)} %get-tuple-element.85.s_ref, bf16[1536,768]{1,0:T(8,128)(2,1)} %bitcast.18.r_ref, s32[512,2]{1,0:T(8,128)} %copy-done.8, ...), custom_call_target="tpu_custom_call" | custom-call | flops 1811939328 | bytes 11017216 | tf_op jit(solution)/shard_map/pallas_call | solution.py:33
  328.3 4.7 all-to-all-start.5
  339.7 12.2 %collective-permute-done.11 = bf16[4,3,24,2048]{3,2,1,0:T(8,128)(2,1)} collective-permute-done((bf16[4,3,24,2048]{3,2,1,0:T(8,128)(2,1)}, bf16[4,3,24,2048]{3,2,1,0:T(8,128)(2,1)}, u32[]{:S(2)}, u32[]{:S(2)}) %collective-permute-start.11) | collective-permute-done | bytes 1179680 | tf_op jit(solution)/shard_map/ppermute | solution.py:839
  353.6 5.9 %all-to-all-start.6 = ((bf16[8,192,768]{2,1,0:T(8,128)(2,1)}), bf16[8,192,768]{2,1,0:T(8,128)(2,1)S(1)}, u32[]{:S(2)}, u32[]{:S(2)}) async-start(bf16[8,192,768]{2,1,0:T(8,128)(2,1)} %bitcast.112), calls=%async_computation.6 | async-start | bytes 4718592 | tf_op jit(solution)/shard_map/all_to_all | solution.py:828
  359.5 18.9 %shard_map.266 = (bf16[1024,384]{1,0:T(8,128)(2,1)}, bf16[1024,384]{1,0:T(8,128)(2,1)}, bf16[1024,384]{1,0:T(8,128)(2,1)}) custom-call(bf16[1024,1152]{1,0:T(8,128)(2,1)} %get-tuple-element.70.q_ref.k_ref.v_ref, bf16[1024,1152]{1,0:T(8,128)(2,1)} %get-tuple-element.70.q_ref.k_ref.v_ref, bf16[1024,1152]{1,0:T(8,128)(2,1)} %get-tuple-element.70.q_ref.k_ref.v_ref, ...), custom_call_target="tpu_custom_call" | custom-call | flops 4026531840 | bytes 11304960 | tf_op jit(solution)/shard_map/pallas_call | solution.py:33
  378.4 7.3 %shard_map.267 = (bf16[2,4,128,768]{3,2,1,0:T(8,128)(2,1)}, f32[768,128]{1,0:T(8,128)}) custom-call(s32[1]{0:T(128)} %bitcast.1.at_ref, bf16[1024,384]{1,0:T(8,128)(2,1)} %get-tuple-element.98.q_ref.refs_1_, bf16[1024,384]{1,0:T(8,128)(2,1)} %get-tuple-element.99.k_ref.refs_2_, bf16[1024,384]{1,0:T(8,128)(2,1)} %get-tuple-element.100.v_ref.refs_3_, ...), custom_call_target="tpu_custom_call" | custom-call | flops 1811939328 | bytes 16515076 | tf_op jit(solution)/shard_map/pallas_call | solution.py:33
  389.8 6.8 %shard_map.270 = (bf16[2,4,2,24,1280]{4,3,2,1,0:T(8,128)(2,1)}, bf16[2,4,2,24,1280]{4,3,2,1,0:T(8,128)(2,1)}) custom-call(s32[1]{0:T(128)} %bitcast.12.at_ref, bf16[1024,768]{1,0:T(8,128)(2,1)} %get-tuple-element.107.refs_0_, bf16[1024,384]{1,0:T(8,128)(2,1)} %get-tuple-element.98.q_ref.refs_1_, bf16[1024,384]{1,0:T(8,128)(2,1)} %get-tuple-element.99.k_ref.refs_2_, ...), custom_call_target="tpu_custom_call" | custom-call | flops 1811939328 | bytes 6291460 | tf_op jit(solution)/shard_map/pallas_call | solution.py:33
  396.6 5.3 add_convert_fusion
  420.6 45.9 %collective-permute-done.6 = bf16[4,2,24,896]{3,2,1,0:T(8,128)(2,1)S(1)} collective-permute-done((bf16[4,2,24,896]{3,2,1,0:T(8,128)(2,1)S(1)}, bf16[4,2,24,896]{3,2,1,0:T(8,128)(2,1)S(1)}, u32[]{:S(2)}, u32[]{:S(2)}) %collective-permute-start.6) | collective-permute-done | bytes 344096 | tf_op jit(solution)/shard_map/ppermute | solution.py:839
  468.1 6.2 %collective-permute-done.2.refs_1_ = bf16[128,768]{1,0:T(8,128)(2,1)S(1)} collective-permute-done((bf16[128,768]{1,0:T(8,128)(2,1)S(1)}, bf16[128,768]{1,0:T(8,128)(2,1)S(1)}, u32[]{:S(2)}, u32[]{:S(2)}) %collective-permute-start.2) | collective-permute-done | bytes 196640 | tf_op jit(solution)/shard_map/ppermute | solution.py:853
  485.0 4.2 all-to-all-start.7
  490.1 22.7 %collective-permute-done.13 = bf16[3,24,2048]{2,1,0:T(8,128)(2,1)} collective-permute-done((bf16[3,24,2048]{2,1,0:T(8,128)(2,1)}, bf16[3,24,2048]{2,1,0:T(8,128)(2,1)}, u32[]{:S(2)}, u32[]{:S(2)}) %collective-permute-start.13) | collective-permute-done | bytes 294944 | tf_op jit(solution)/shard_map/ppermute | solution.py:853
  523.4 5.1 shard_map.265
  (133 shorter events, 92.1 us)
Async XLA Ops:
  0.7 26.5 %all-to-all-start = ((bf16[4,128,768]{2,1,0:T(8,128)(2,1)}), bf16[4,128,768]{2,1,0:T(8,128)(2,1)S(1)}, u32[]{:S(2)}, u32[]{:S(2)}) async-start(bf16[4,128,768]{2,1,0:T(8,128)(2,1)} %param.16), calls=%async_computation | async-start | bytes 1572864 | tf_op jit(solution)/shard_map/all_to_all | solution.py:828
  27.1 18.7 %copy-start.5 = (bf16[4,128,768]{2,1,0:T(8,128)(2,1)}, bf16[4,128,768]{2,1,0:T(8,128)(2,1)S(1)}, u32[]{:S(2)}) copy-start(bf16[4,128,768]{2,1,0:T(8,128)(2,1)S(1)} %all-to-all-done.refs_0_) | copy-start | bytes 2359300
  27.1 22.3 %copy-start.18 = (bf16[768]{0:T(1024)(128)(2,1)S(1)}, bf16[768]{0:T(1024)(128)(2,1)}, u32[]{:S(2)}) copy-start(bf16[768]{0:T(1024)(128)(2,1)} %param.21) | copy-start | bytes 4612
  27.1 18.7 %collective-permute-start = (bf16[4,128,768]{2,1,0:T(8,128)(2,1)S(1)}, bf16[4,128,768]{2,1,0:T(8,128)(2,1)}, u32[]{:S(2)}, u32[]{:S(2)}) collective-permute-start(bf16[4,128,768]{2,1,0:T(8,128)(2,1)S(1)} %all-to-all-done.refs_0_), channel_id=1, source_target_pairs={{0,1},{1,0},{2,3},{3,2},{4,5},{5,4},{6,7},{7,6},{8,9},{9,8},{10,11... | collective-permute-start | bytes 2359304 | tf_op jit(solution)/shard_map/ppermute | solution.py:922
  45.8 60.3 %all-to-all-start.1 = ((bf16[8,208,768]{2,1,0:T(8,128)(2,1)}), bf16[8,208,768]{2,1,0:T(8,128)(2,1)S(1)}, u32[]{:S(2)}, u32[]{:S(2)}) async-start(bf16[8,208,768]{2,1,0:T(8,128)(2,1)} %shard_map.255), calls=%async_computation.1 | async-start | bytes 5111808 | tf_op jit(solution)/shard_map/all_to_all | solution.py:828
  58.6 51.1 %copy-start.19 = (bf16[768]{0:T(1024)(128)(2,1)S(1)}, bf16[768]{0:T(1024)(128)(2,1)}, u32[]{:S(2)}) copy-start(bf16[768]{0:T(1024)(128)(2,1)} %param.24) | copy-start | bytes 4612
  106.1 24.0 %all-to-all-start.2 = ((bf16[8,128,384]{2,1,0:T(8,128)(2,1)}), bf16[8,128,384]{2,1,0:T(8,128)(2,1)S(1)}, u32[]{:S(2)}, u32[]{:S(2)}) async-start(bf16[8,128,384]{2,1,0:T(8,128)(2,1)} %bitcast.122), calls=%async_computation.2 | async-start | bytes 1572864 | tf_op jit(solution)/shard_map/all_to_all | solution.py:828
  140.9 57.9 %all-to-all-start.3 = ((bf16[8,192,768]{2,1,0:T(8,128)(2,1)}), bf16[8,192,768]{2,1,0:T(8,128)(2,1)}, u32[]{:S(2)}, u32[]{:S(2)}) async-start(bf16[8,192,768]{2,1,0:T(8,128)(2,1)} %shard_map.259), calls=%async_computation.3 | async-start | bytes 4718592 | tf_op jit(solution)/shard_map/all_to_all | solution.py:828
  163.2 12.0 %copy-start.17 = (bf16[768,8]{0,1:T(8,128)(2,1)S(1)}, bf16[768,8]{0,1:T(8,128)(2,1)}, u32[]{:S(2)}) copy-start(bf16[768,8]{0,1:T(8,128)(2,1)} %param.25) | copy-start | bytes 36868
  175.2 78.1 %collective-permute-start.9 = (bf16[2,2,4,3,24,2048]{5,4,3,2,1,0:T(8,128)(2,1)}, bf16[2,2,4,3,24,2048]{5,4,3,2,1,0:T(8,128)(2,1)}, u32[]{:S(2)}, u32[]{:S(2)}) collective-permute-start(bf16[2,2,4,3,24,2048]{5,4,3,2,1,0:T(8,128)(2,1)} %get-tuple-element.82), channel_id=1, source_target_pairs={{0,8},{8,0},{1,9},{9,1},{2,10},{10,2},{3,11},{11,3},{4,12},{12,4},... | collective-permute-start | bytes 14155784 | tf_op jit(solution)/shard_map/ppermute | solution.py:844
  248.7 71.2 %all-to-all-start.4 = ((bf16[8,192,768]{2,1,0:T(8,128)(2,1)}), bf16[8,192,768]{2,1,0:T(8,128)(2,1)}, u32[]{:S(2)}, u32[]{:S(2)}) async-start(bf16[8,192,768]{2,1,0:T(8,128)(2,1)} %bitcast.113), calls=%async_computation.4 | async-start | bytes 4718592 | tf_op jit(solution)/shard_map/all_to_all | solution.py:828
  261.4 52.3 %collective-permute-start.10 = (bf16[2,4,3,24,2048]{4,3,2,1,0:T(8,128)(2,1)S(1)}, bf16[2,4,3,24,2048]{4,3,2,1,0:T(8,128)(2,1)}, u32[]{:S(2)}, u32[]{:S(2)}) collective-permute-start(bf16[2,4,3,24,2048]{4,3,2,1,0:T(8,128)(2,1)S(1)} %dynamic-slice_bitcast_fusion.1), channel_id=1, source_target_pairs={{0,16},{16,0},{1,17},{17,1},{2,18},{18,2},{3,19},{19,3},{4,20},{20... | collective-permute-start | bytes 7077896 | tf_op jit(solution)/shard_map/ppermute | solution.py:839
  286.9 109.7 %collective-permute-start.15 = (bf16[2,3,768,512]{3,2,1,0:T(8,128)(2,1)}, bf16[2,3,768,512]{3,2,1,0:T(8,128)(2,1)}, u32[]{:S(2)}, u32[]{:S(2)}) collective-permute-start(bf16[2,3,768,512]{3,2,1,0:T(8,128)(2,1)} %get-tuple-element.92), channel_id=1, source_target_pairs={{0,8},{8,0},{1,9},{9,1},{2,10},{10,2},{3,11},{11,3},{4,12},{12,4},... | collective-permute-start | bytes 14155784 | tf_op jit(solution)/shard_map/ppermute | solution.py:844
  318.1 33.8 %collective-permute-start.11 = (bf16[4,3,24,2048]{3,2,1,0:T(8,128)(2,1)}, bf16[4,3,24,2048]{3,2,1,0:T(8,128)(2,1)}, u32[]{:S(2)}, u32[]{:S(2)}) collective-permute-start(bf16[4,3,24,2048]{3,2,1,0:T(8,128)(2,1)} %dynamic-slice_bitcast_fusion.2), channel_id=1, source_target_pairs={{0,1},{1,0},{2,3},{3,2},{4,5},{5,4},{6,7},{7,6},{8,9},{9,8},{10,11... | collective-permute-start | bytes 3538952 | tf_op jit(solution)/shard_map/ppermute | solution.py:839
  319.8 13.2 %copy-start.7 = (bf16[8,128,384]{2,1,0:T(8,128)(2,1)S(1)}, bf16[8,128,384]{2,1,0:T(8,128)(2,1)}, u32[]{:S(2)}) copy-start(bf16[8,128,384]{2,1,0:T(8,128)(2,1)} %copy-done.6) | copy-start | bytes 2359300
  328.3 25.3 %all-to-all-start.5 = ((bf16[8,128,384]{2,1,0:T(8,128)(2,1)}), bf16[8,128,384]{2,1,0:T(8,128)(2,1)}, u32[]{:S(2)}, u32[]{:S(2)}) async-start(bf16[8,128,384]{2,1,0:T(8,128)(2,1)} %bitcast.121), calls=%async_computation.5 | async-start | bytes 1572864 | tf_op jit(solution)/shard_map/all_to_all | solution.py:828
  339.7 66.6 %collective-permute-start.5 = (bf16[2,4,2,24,896]{4,3,2,1,0:T(8,128)(2,1)}, bf16[2,4,2,24,896]{4,3,2,1,0:T(8,128)(2,1)}, u32[]{:S(2)}, u32[]{:S(2)}) collective-permute-start(bf16[2,4,2,24,896]{4,3,2,1,0:T(8,128)(2,1)} %get-tuple-element.106), channel_id=1, source_target_pairs={{0,8},{8,0},{1,9},{9,1},{2,10},{10,2},{3,11},{11,3},{4,12},{12,4},... | collective-permute-start | bytes 2064392 | tf_op jit(solution)/shard_map/ppermute | solution.py:844
  353.6 131.4 %all-to-all-start.6 = ((bf16[8,192,768]{2,1,0:T(8,128)(2,1)}), bf16[8,192,768]{2,1,0:T(8,128)(2,1)S(1)}, u32[]{:S(2)}, u32[]{:S(2)}) async-start(bf16[8,192,768]{2,1,0:T(8,128)(2,1)} %bitcast.112), calls=%async_computation.6 | async-start | bytes 4718592 | tf_op jit(solution)/shard_map/all_to_all | solution.py:828
  387.8 20.5 %collective-permute-start.1 = (bf16[4,128,768]{2,1,0:T(8,128)(2,1)}, bf16[4,128,768]{2,1,0:T(8,128)(2,1)}, u32[]{:S(2)}, u32[]{:S(2)}) collective-permute-start(bf16[4,128,768]{2,1,0:T(8,128)(2,1)} %dynamic-slice_bitcast_fusion.3), channel_id=1, source_target_pairs={{0,1},{1,0},{2,3},{3,2},{4,5},{5,4},{6,7},{7,6},{8,9},{9,8},{10,11... | collective-permute-start | bytes 2359304 | tf_op jit(solution)/shard_map/ppermute | solution.py:839
  396.6 13.1 %collective-permute-start.7 = (bf16[2,4,2,24,1280]{4,3,2,1,0:T(8,128)(2,1)}, bf16[2,4,2,24,1280]{4,3,2,1,0:T(8,128)(2,1)S(1)}, u32[]{:S(2)}, u32[]{:S(2)}) collective-permute-start(bf16[2,4,2,24,1280]{4,3,2,1,0:T(8,128)(2,1)} %get-tuple-element.110), channel_id=1, source_target_pairs={{0,8},{8,0},{1,9},{9,1},{2,10},{10,2},{3,11},{11,3},{4,12},{12,4},... | collective-permute-start | bytes 2949128 | tf_op jit(solution)/shard_map/ppermute | solution.py:844
  404.8 110.1 %collective-permute-start.16 = (bf16[3,768,512]{2,1,0:T(8,128)(2,1)}, bf16[3,768,512]{2,1,0:T(8,128)(2,1)}, u32[]{:S(2)}, u32[]{:S(2)}) collective-permute-start(bf16[3,768,512]{2,1,0:T(8,128)(2,1)} %dynamic-slice_bitcast_fusion), channel_id=1, source_target_pairs={{0,16},{16,0},{1,17},{17,1},{2,18},{18,2},{3,19},{19,3},{4,20},{20... | collective-permute-start | bytes 7077896 | tf_op jit(solution)/shard_map/ppermute | solution.py:839
  407.7 58.8 %collective-permute-start.6 = (bf16[4,2,24,896]{3,2,1,0:T(8,128)(2,1)S(1)}, bf16[4,2,24,896]{3,2,1,0:T(8,128)(2,1)S(1)}, u32[]{:S(2)}, u32[]{:S(2)}) collective-permute-start(bf16[4,2,24,896]{3,2,1,0:T(8,128)(2,1)S(1)} %dynamic-slice_bitcast_fusion.5), channel_id=1, source_target_pairs={{0,16},{16,0},{1,17},{17,1},{2,18},{18,2},{3,19},{19,3},{4,20},{20... | collective-permute-start | bytes 1032200 | tf_op jit(solution)/shard_map/ppermute | solution.py:839
  409.9 65.4 %copy-start.9 = (bf16[2,4,2,24,1280]{4,3,2,1,0:T(8,128)(2,1)}, bf16[2,4,2,24,1280]{4,3,2,1,0:T(8,128)(2,1)S(1)}, u32[]{:S(2)}) copy-start(bf16[2,4,2,24,1280]{4,3,2,1,0:T(8,128)(2,1)S(1)} %add_convert_fusion.2) | copy-start | bytes 2949124
  410.8 72.0 %collective-permute-start.8 = (bf16[4,2,24,1280]{3,2,1,0:T(8,128)(2,1)}, bf16[4,2,24,1280]{3,2,1,0:T(8,128)(2,1)}, u32[]{:S(2)}, u32[]{:S(2)}) collective-permute-start(bf16[4,2,24,1280]{3,2,1,0:T(8,128)(2,1)} %dynamic-slice_bitcast_fusion.4), channel_id=1, source_target_pairs={{0,16},{16,0},{1,17},{17,1},{2,18},{18,2},{3,19},{19,3},{4,20},{20... | collective-permute-start | bytes 1474568 | tf_op jit(solution)/shard_map/ppermute | solution.py:839
  413.0 55.0 %collective-permute-start.4 = (bf16[128,768]{1,0:T(8,128)(2,1)S(1)}, bf16[128,768]{1,0:T(8,128)(2,1)S(1)}, u32[]{:S(2)}, u32[]{:S(2)}) collective-permute-start(bf16[128,768]{1,0:T(8,128)(2,1)S(1)} %get-tuple-element.188), channel_id=1, source_target_pairs={{0,6},{2,0},{4,2},{6,4},{1,7},{3,1},{5,3},{7,5},{8,14},{10,8},{12,... | collective-permute-start | bytes 589832 | tf_op jit(solution)/shard_map/ppermute | solution.py:853
  416.4 51.7 %collective-permute-start.3 = (bf16[128,768]{1,0:T(8,128)(2,1)S(1)}, bf16[128,768]{1,0:T(8,128)(2,1)S(1)}, u32[]{:S(2)}, u32[]{:S(2)}) collective-permute-start(bf16[128,768]{1,0:T(8,128)(2,1)S(1)} %get-tuple-element.189), channel_id=1, source_target_pairs={{0,4},{2,6},{4,0},{6,2},{1,5},{3,7},{5,1},{7,3},{8,12},{10,14},{12... | collective-permute-start | bytes 589832 | tf_op jit(solution)/shard_map/ppermute | solution.py:853
  466.5 7.8 %collective-permute-start.2 = (bf16[128,768]{1,0:T(8,128)(2,1)S(1)}, bf16[128,768]{1,0:T(8,128)(2,1)S(1)}, u32[]{:S(2)}, u32[]{:S(2)}) collective-permute-start(bf16[128,768]{1,0:T(8,128)(2,1)S(1)} %get-tuple-element.190), channel_id=1, source_target_pairs={{0,2},{2,4},{4,6},{6,0},{1,3},{3,5},{5,7},{7,1},{8,10},{10,12},{12... | collective-permute-start | bytes 589832 | tf_op jit(solution)/shard_map/ppermute | solution.py:853
  475.3 13.9 %collective-permute-start.12 = (bf16[3,24,2048]{2,1,0:T(8,128)(2,1)}, bf16[3,24,2048]{2,1,0:T(8,128)(2,1)}, u32[]{:S(2)}, u32[]{:S(2)}) collective-permute-start(bf16[3,24,2048]{2,1,0:T(8,128)(2,1)} %get-tuple-element.183), channel_id=1, source_target_pairs={{0,2},{2,4},{4,6},{6,0},{1,3},{3,5},{5,7},{7,1},{8,10},{10,12},{12... | collective-permute-start | bytes 884744 | tf_op jit(solution)/shard_map/ppermute | solution.py:853
  475.5 14.6 %collective-permute-start.14 = (bf16[3,24,2048]{2,1,0:T(8,128)(2,1)}, bf16[3,24,2048]{2,1,0:T(8,128)(2,1)}, u32[]{:S(2)}, u32[]{:S(2)}) collective-permute-start(bf16[3,24,2048]{2,1,0:T(8,128)(2,1)} %get-tuple-element.184), channel_id=1, source_target_pairs={{0,6},{2,0},{4,2},{6,4},{1,7},{3,1},{5,3},{7,5},{8,14},{10,8},{12,... | collective-permute-start | bytes 884744 | tf_op jit(solution)/shard_map/ppermute | solution.py:853
  479.3 33.5 %collective-permute-start.13 = (bf16[3,24,2048]{2,1,0:T(8,128)(2,1)}, bf16[3,24,2048]{2,1,0:T(8,128)(2,1)}, u32[]{:S(2)}, u32[]{:S(2)}) collective-permute-start(bf16[3,24,2048]{2,1,0:T(8,128)(2,1)} %get-tuple-element.185), channel_id=1, source_target_pairs={{0,4},{2,6},{4,0},{6,2},{1,5},{3,7},{5,1},{7,3},{8,12},{10,14},{12... | collective-permute-start | bytes 884744 | tf_op jit(solution)/shard_map/ppermute | solution.py:853
  485.0 33.0 %copy-start.4 = (bf16[8,192,768]{2,1,0:T(8,128)(2,1)}, bf16[8,192,768]{2,1,0:T(8,128)(2,1)S(1)}, u32[]{:S(2)}) copy-start(bf16[8,192,768]{2,1,0:T(8,128)(2,1)S(1)} %all-to-all-done.6) | copy-start | bytes 7077892
  485.0 43.4 %all-to-all-start.7 = ((bf16[8,24,2176]{2,1,0:T(8,128)(2,1)}), bf16[8,24,2176]{2,1,0:T(8,128)(2,1)}, u32[]{:S(2)}, u32[]{:S(2)}) async-start(bf16[8,24,2176]{2,1,0:T(8,128)(2,1)} %bitcast.110), calls=%async_computation.7 | async-start | bytes 1671168 | tf_op jit(solution)/shard_map/all_to_all | solution.py:828
  (13 other events, 69.1 us)

commit v4 on v2

--- a/solution.py
+++ b/solution.py
@@ -401,28 +401,38 @@
     )
 
 
-def pick(target, rows):
-    spot = lax.broadcasted_iota(jnp.int32, (target.shape[0], rows.shape[0]), 1)
-    hit = (spot == target[:, 0:1]) | (spot == target[:, 1:2])
-    return mm(hit.astype(F32).astype(BF), rows)
+def pick(target, row_refs):
+    total = None
+    for index, ref in enumerate(row_refs):
+        rows = ref[...]
+        spot = lax.broadcasted_iota(jnp.int32, (target.shape[0], rows.shape[0]), 1)
+        one, two = target[:, 2 * index : 2 * index + 1], target[:, 2 * index + 1 : 2 * index + 2]
+        found = mm(((spot == one) | (spot == two)).astype(F32).astype(BF), rows)
+        total = found if total is None else total + found
+    return total
 
 
 def layer_end(hidden, shared_out, rows, target):
     count, width = hidden.shape
     high = count // 2
 
-    def body(h_ref, s_ref, r_ref, t_ref, o_ref):
-        o_ref[...] = (h_ref[...] + s_ref[...] + pick(t_ref[...], r_ref[...])).astype(BF)
+    def body(h_ref, s_ref, t_ref, *refs):
+        refs[-1][...] = (h_ref[...] + s_ref[...] + pick(t_ref[...], refs[:-1])).astype(BF)
 
     block = pl.BlockSpec((high, width), lambda i: (i, 0))
     return call(
         body,
         (2,),
-        [block, block, whole(rows.shape), pl.BlockSpec((high, 2), lambda i: (i, 0))],
+        [
+            block,
+            block,
+            pl.BlockSpec((high, target.shape[1]), lambda i: (i, 0)),
+            *[whole(part.shape) for part in rows],
+        ],
         block,
         sds(hidden.shape, BF),
-        (hidden, shared_out, rows, target),
-        flops=2 * count * width * rows.shape[0],
+        (hidden, shared_out, target, *rows),
+        flops=2 * count * width * rows[0].shape[0] * len(rows),
     )
 
 
@@ -434,9 +444,10 @@
     steps = count // high
     group = width // parts
 
-    def body(h_ref, s_ref, r_ref, t_ref, c_ref, g_ref, w_ref, gh_ref, ga_ref, d_ref, n_ref, acc_ref):
+    def body(h_ref, s_ref, t_ref, c_ref, g_ref, w_ref, *refs):
+        gh_ref, ga_ref, d_ref, n_ref, acc_ref = refs[len(rows) :]
         step = pl.program_id(0)
-        branch = s_ref[...] + pick(t_ref[...], r_ref[...])
+        branch = s_ref[...] + pick(t_ref[...], refs[: len(rows)])
         hidden = h_ref[...]
         scale = rms(hidden)
         weighted = branch * g_ref[...]
@@ -468,11 +479,11 @@
         [
             block,
             block,
-            whole(rows.shape),
-            pl.BlockSpec((high, 2), lambda i: (i, 0)),
+            pl.BlockSpec((high, target.shape[1]), lambda i: (i, 0)),
             block,
             whole(gain.shape),
             whole(w_out.shape),
+            *[whole(part.shape) for part in rows],
         ],
         [
             block,
@@ -486,9 +497,9 @@
             sds((seqs, parts, span, group), BF),
             sds((width, 128), F32),
         ],
-        (hidden, grad_shared, rows, target, cotangent, gain, w_out),
+        (hidden, grad_shared, target, cotangent, gain, w_out, *rows),
         scratch=[pltpu.VMEM((8, width), F32)],
-        flops=2 * count * width * (rows.shape[0] + width),
+        flops=2 * count * width * (rows[0].shape[0] * len(rows) + width),
     )
 
 
@@ -633,19 +644,21 @@
     )
 
 
-def expert_weight_grads(rows, grads, dg, du, hid, grad_logits, sizes, core_at):
+def expert_weight_grads(halves, sizes, core_at):
     outer, cores = sizes["y"], sizes["core"]
-    count, width = rows.shape
-    units = dg.shape[1]
+    count, width = halves[0][0].shape
+    units = halves[0][2].shape[1]
     wide = units // (outer * cores)
 
-    def body(at_ref, x_ref, g_ref, dg_ref, du_ref, hid_ref, gl_ref, keep_ref, give_ref, r_ref):
+    def body(at_ref, *refs):
+        keep_ref, give_ref, r_ref = refs[-3:]
+        groups = [refs[6 * at : 6 * at + 6] for at in range(len(halves))]
         step = pl.program_id(0)
-        found = [
-            mm(x_ref[...], dg_ref[...], TN).astype(BF),
-            mm(x_ref[...], du_ref[...], TN).astype(BF),
-            mm(g_ref[...], hid_ref[...], TN).astype(BF),
-        ]
+
+        def over(left, right):
+            return sum(mm(group[left][...], group[right][...], TN) for group in groups)
+
+        found = [over(0, 2).astype(BF), over(0, 3).astype(BF), over(1, 4).astype(BF)]
 
         @pl.when(step < outer)
         def _():
@@ -659,7 +672,7 @@
 
         @pl.when(step == 0)
         def _():
-            r_ref[...] = mm(x_ref[...], gl_ref[...], TN)
+            r_ref[...] = over(0, 5)
 
     def taken(i, at):
         core = jnp.where(i < outer, 1 - at[0], at[0])
@@ -670,16 +683,24 @@
     return call(
         body,
         (outer * cores,),
-        [whole(rows.shape), whole(grads.shape), hidden, hidden, hidden, whole(grad_logits.shape)],
+        [
+            whole((count, width)),
+            whole((count, width)),
+            hidden,
+            hidden,
+            hidden,
+            whole((count, 128)),
+        ]
+        * len(halves),
         [
             pl.BlockSpec(part, lambda i, *_: (jnp.maximum(i - outer, 0), 0, 0, 0)),
             pl.BlockSpec(part, lambda i, *_: (jnp.minimum(i, outer - 1), 0, 0, 0)),
             whole((width, 128)),
         ],
         [sds((outer, *part[1:]), BF)] * 2 + [sds((width, 128), F32)],
-        (core_at, rows, grads, dg, du, hid, grad_logits),
+        (core_at, *[value for half in halves for value in half]),
         prefetch=1,
-        flops=6 * count * width * units,
+        flops=6 * count * len(halves) * width * units,
     )
 
 
@@ -832,17 +853,26 @@
     return lax.dynamic_index_in_dim(value, index, 0, keepdims=False)
 
 
-def fold(value, name):
+def total(terms):
+    return sum(term.astype(F32) for term in terms)
+
+
+def both(keep, give):
+    return [keep, lax.ppermute(give, "core", [(0, 1), (1, 0)])]
+
+
+def fold(terms, name, *others):
     if lax.axis_size(name) != 2:
-        return scatter_sum(value, name)
+        sent = total(terms).astype(BF)
+        if others:
+            sent = after(sent, *others)
+        return [scatter_sum(sent, name)], sent
     at = lax.axis_index(name)
-    got = lax.ppermute(at_index(value, 1 - at), name, [(0, 1), (1, 0)])
-    return (at_index(value, at).astype(F32) + got.astype(F32)).astype(BF)
-
-
-def join(keep, give, name):
-    got = lax.ppermute(give, name, [(0, 1), (1, 0)])
-    return (keep.astype(F32) + got.astype(F32)).astype(BF)
+    sent = total([at_index(term, 1 - at) for term in terms]).astype(BF)
+    if others:
+        sent = after(sent, *others)
+    got = lax.ppermute(sent, name, [(0, 1), (1, 0)])
+    return [at_index(term, at) for term in terms] + [got], sent
 
 
 def swap_by_steps(value, name):
@@ -896,9 +926,15 @@
 
     route_rows = routes.reshape(count, 2)
     slot_rows = slots.reshape(count, 2)
-    target = jnp.where(slot_rows >= 0, route_rows * capacity + slot_rows, -1)
-    target_rows = jnp.transpose(target)
-    grad_sent = dispatch(flat_cot, target_rows, experts, capacity, jnp.transpose(route_rows))
+    half = capacity // 2
+    targets = []
+    for first in (0, half):
+        here = (slot_rows >= first) & (slot_rows < first + half)
+        targets.append(jnp.where(here, route_rows * half + slot_rows - first, -1))
+    target_rows = [jnp.transpose(target) for target in targets]
+    target = jnp.concatenate(targets, axis=1)
+    route_flat = jnp.transpose(route_rows)
+    grad_sent = [dispatch(flat_cot, to, experts, half, route_flat) for to in target_rows]
 
     frequency = jnp.power(10000.0, -2.0 * jnp.arange(32, dtype=F32) / HEAD_DIM)
     angles = jnp.arange(length, dtype=jnp.int32).astype(F32)[:, None] * jnp.tile(frequency, 4)
@@ -915,45 +951,53 @@
         weights = [picked.reshape(width, 3 * group)]
 
     by_seq = swap_all(tokens, "z")
-    by_seq, cosine, sine, seg_col, grad_sent = lax.optimization_barrier(
-        (by_seq, cosine, sine, seg_col, grad_sent)
-    )
-    grad_came = swap_all(grad_sent, ranks)
+    by_seq, cosine, sine, seg_col, *grad_sent = lax.optimization_barrier(
+        (by_seq, cosine, sine, seg_col, *grad_sent)
+    )
     if parts == 2:
         rows = [by_seq, lax.ppermute(by_seq, "x", [(0, 1), (1, 0)])]
     else:
         rows = [lax.all_gather(by_seq, "x", axis=0, tiled=False)]
+    *rows, grad_sent[0] = lax.optimization_barrier((*rows, grad_sent[0]))
+    grad_came = [swap_all(grad_sent[0], ranks)]
 
     qkv, normed = project(rows, attn_scale, weights, group, cosine, sine, x_ref, parts)
     attended, lse = (attend if fused else plain_attend)(qkv, seg_row, seg_col)
-    attended = after(attended, grad_came)
+    attended = after(attended, grad_came[0])
     attended = swap_all(attended.reshape(experts, span, group), ranks)
+    attended, grad_sent[1] = lax.optimization_barrier((attended, grad_sent[1]))
+    grad_came.append(swap_all(grad_sent[1], ranks))
     attended = attended.reshape(seqs, parts, span, group)
 
     hidden, branch_in = after_attention(flat_tokens, attended, w_out, ffn_scale)
-    sent = dispatch(branch_in, target_rows, experts, capacity)
-    received = swap_all(sent, ranks).reshape(-1, width)
-
+    sent = [dispatch(branch_in, target_rows[0], experts, half)]
+    sent.append(dispatch(after(branch_in, sent[0]), target_rows[1], experts, half))
     shared_out, shared_back, hid, dg, du = feed_forward(
-        branch_in, flat_cot, shared_gate, shared_up, shared_down
-    )
+        after(branch_in, sent[1]), flat_cot, shared_gate, shared_up, shared_down
+    )
+    sent[0] = after(sent[0], grad_came[1], shared_out)
+    received = [swap_all(value, ranks).reshape(-1, width) for value in sent]
     keep, give = shared_weight_grads(branch_in, flat_cot, dg, du, hid, sizes, core_ref)
-    shared_sums = fold(join(keep, give, "core"), "y")
-    grad_rows = grad_came[:, :capacity, :].reshape(-1, width)
-    other = grad_came[:, capacity, :capacity].astype(jnp.int32).reshape(-1, 1)
-    received = after(received, give, grad_rows, other)
+    shared_sums, shared_sent = fold(both(keep, give), "y")
 
     router = jnp.pad(w_router, ((0, 0), (0, 128 - experts)))
-    made, made_back, hid, dg, du, gated_grads, grad_logits = feed_forward(
-        received, grad_rows, expert_gate[0], expert_up[0], expert_down[0], router, other, own
-    )
-    back_rows = swap_all(made_back.reshape(experts, capacity, width), ranks).reshape(-1, width)
-    keep, give, grad_router = expert_weight_grads(
-        received, gated_grads, dg, du, hid, grad_logits, sizes, core_ref
-    )
-    back_rows = after(back_rows, give)
-    expert_sums = fold(join(keep, give, "core"), "y")
-    shared_sums = swap_by_steps(fold(shared_sums, "x"), "z")
+    made, back_rows, halves = [], [], []
+    before = (give,)
+    for at in range(2):
+        grad_rows = grad_came[at][:, :half, :].reshape(-1, width)
+        other = grad_came[at][:, half, :half].astype(jnp.int32).reshape(-1, 1)
+        rows_at = after(received[at], grad_rows, other, *before)
+        out, back, hid, dg, du, gated_grads, grad_logits = feed_forward(
+            rows_at, grad_rows, expert_gate[0], expert_up[0], expert_down[0], router, other, own
+        )
+        made.append(out)
+        back_rows.append(swap_all(back.reshape(experts, half, width), ranks).reshape(-1, width))
+        halves.append((rows_at, gated_grads, dg, du, hid, grad_logits))
+        before = (out,)
+    halves[1] = (after(halves[1][0], back_rows[0], shared_sent), *halves[1][1:])
+    keep, give, grad_router = expert_weight_grads(halves, sizes, core_ref)
+    back_rows[1] = after(back_rows[1], give)
+    expert_sums, expert_sent = fold(both(keep, give), "y")
 
     grad_hidden, grad_attn, grad_att, grad_ffn = middle_back(
         hidden, shared_back, back_rows, target, flat_cot, ffn_scale, w_out, parts, span
@@ -969,23 +1013,32 @@
         sizes,
         core_ref,
     )
-    out_sums = fold(join(*out_sums, "core"), "y")
-
-    made = after(made, grad_att)
-    made_rows = swap_all(made.reshape(experts, capacity, width), ranks).reshape(-1, width)
-    grads = (attend_back if fused else plain_attend_back)(
-        qkv, grad_att, lse, seg_row, seg_col, cosine, sine
-    )
+    out_sums, _ = fold(both(*out_sums), "y")
+    out_sums = total(out_sums).astype(BF)
+
+    made_rows = []
+    for value in made:
+        value = after(value.reshape(experts, half, width), grad_att)
+        made_rows.append(swap_all(value, ranks).reshape(-1, width))
+    grads = list(
+        (attend_back if fused else plain_attend_back)(
+            qkv, grad_att, lse, seg_row, seg_col, cosine, sine
+        )
+    )
+    shared_sums, _ = fold([after(term, grads[0]) for term in shared_sums], "x")
+    grads[0] = after(grads[0], expert_sent)
     normed_back, grad_gain = project_back(grads, weights, rows, x_ref, parts)
-    normed_back = fold(normed_back, "x")
-    pieces = swap_by_steps(normed_back, "z")
+    normed_back, _ = fold([normed_back], "x")
+    pieces = swap_by_steps(total(normed_back).astype(BF), "z")
 
     qkv_sums = tall_weight_grads([normed], list(grads), [grad_gain], sizes, core_ref)
-    qkv_sums = fold(join(*qkv_sums, "core"), "y")
+    qkv_sums, _ = fold(both(*qkv_sums), "y", expert_sums[-1])
+    qkv_sums = total(qkv_sums).astype(BF)
     token_grad = first_norm_back(flat_tokens, attn_scale, pieces, grad_hidden, z_ref)
     layer_out = layer_end(hidden, shared_out, made_rows, target).reshape(tokens.shape)
 
-    last = after(jnp.concatenate([out_sums, qkv_sums], axis=-1), made_rows)
+    shared_sums = swap_by_steps(after(total(shared_sums).astype(BF), *pieces), "z")
+    last = after(jnp.concatenate([out_sums, qkv_sums], axis=-1), *made_rows)
     each, cols = last.shape[-2:]
     last = swap_all(last.reshape(experts, each, cols), ranks).astype(F32)
     last = jnp.sum(last.reshape(blocks, parts, each, cols), axis=0)
@@ -995,8 +1048,7 @@
     grad_w_qkv = qkv_sums[:, :, : 3 * group].reshape(parts, each, 3, group)
     grad_w_qkv = jnp.transpose(grad_w_qkv, (1, 2, 0, 3)).reshape(each, 3 * width)
 
-    shared_sums = sum(part.astype(F32) for part in shared_sums)
-    expert_sums = expert_sums.astype(F32)
+    shared_sums, expert_sums = total(shared_sums), total(expert_sums)
     return (
         layer_out,
         token_grad.reshape(tokens.shape),

time: 593 us -> 500 us (0.84)
  waiting for transfers between devices: 266 us -> 119 us
  blocking collectives: 0 us -> 23.8 us
  Pallas kernels: 194 us -> 215 us
  starting transfers between devices: 57.5 us -> 73.3 us
  local copies, waits for them, and re-layouts: 34.1 us -> 27.4 us
    all_to_all x8 -> x11, waiting for transfers between devices: 97.5 us -> 51.1 us  [swap_all(): return lax.all_to_all(value, names, 0, 0, tiled=True)]
    ppermute x6, waiting for transfers between devices: 62.8 us -> 23.3 us  [swap_by_steps(): lax.ppermute(sent, name, [(i, (i + step) % size) for i in range(size)])]
    ppermute x10, waiting for transfers between devices: 64 us -> 27.5 us  [the longest x6 27.5 us: fold(): got = lax.ppermute(sent, name, [(0, 1), (1, 0)])]
    ppermute x1, waiting for transfers between devices: 41.9 us -> 17.1 us  [on_device(): rows = [by_seq, lax.ppermute(by_seq, 'x', [(0, 1), (1, 0)])]]
    all_to_all x0 -> x1, blocking collectives: none -> 23.8 us  [swap_all(): return lax.all_to_all(value, names, 0, 0, tiled=True)]
    pallas_call x16 -> x19, Pallas kernels: 194 us -> 215 us  [call(): pl.pallas_call(body, out_shape=out_shape, grid_spec=pltpu.PrefetchScalarG...]
    all_to_all x8 -> x11, starting transfers between devices: 37 us -> 53 us  [swap_all(): return lax.all_to_all(value, names, 0, 0, tiled=True)]
    unnamed x51, local copies, waits for them, and re-layouts: 11.9 us -> 3.71 us
  transfers between devices with their start and end apart: 25 -> 28, of which waited for: 12 -> 10; matrix products, arithmetic and copies ran while one was open for 8% -> 11% of each run, Pallas kernels for 27% -> 43%
where the time goes in v4:
time: 500 us; the launch traced here: 494 us
  Pallas kernels  215 us (43%)
  waiting for transfers between devices  119 us (24%)
  starting transfers between devices  73.3 us (15%)
  other arithmetic  34.6 us (7%)
  local copies, waits for them, and re-layouts  27.4 us (5%)
  blocking collectives  23.8 us (5%)
    pallas_call x19, Pallas kernels, call(): pl.pallas_call(body, out_shape=out_shape, grid_spec=pltpu.PrefetchScalarG...  215 us
    all_to_all x11, starting transfers between devices, swap_all(): return lax.all_to_all(value, names, 0, 0, tiled=True)  53 us
    all_to_all x11, waiting for transfers between devices, swap_all(): return lax.all_to_all(value, names, 0, 0, tiled=True)  51.1 us
    ppermute x6, waiting for transfers between devices, fold(): got = lax.ppermute(sent, name, [(0, 1), (1, 0)])  27.5 us
    all_to_all x1, blocking collectives, swap_all(): return lax.all_to_all(value, names, 0, 0, tiled=True)  23.8 us
    ppermute x6, waiting for transfers between devices, swap_by_steps(): lax.ppermute(sent, name, [(i, (i + step) % size) for i in range(size)])  23.3 us
    ppermute x1, waiting for transfers between devices, on_device(): rows = [by_seq, lax.ppermute(by_seq, 'x', [(0, 1), (1, 0)])]  17.1 us
    convert_element_type x5, other arithmetic, fold(): sent = total([at_index(term, 1 - at) for term in terms]).astype(BF)  13.7 us
  transfers between devices with their start and end apart: 28, of which 10 were waited for; matrix products, arithmetic and copies ran while one was open for 11% of the time, Pallas kernels for 43%

profile of v4, /device:TPU:0, one launch (start us, length us, event | category | flops | bytes accessed | tf_op | source)
XLA Modules:
  0.0 494.1 jit_solution(7839430477209976606)
XLA Ops:
  0.7 6.4 %all-to-all-start = ((bf16[4,128,768]{2,1,0:T(8,128)(2,1)}), bf16[4,128,768]{2,1,0:T(8,128)(2,1)S(1)}, u32[]{:S(2)}, u32[]{:S(2)}) async-start(bf16[4,128,768]{2,1,0:T(8,128)(2,1)} %param.16), calls=%async_computation | async-start | bytes 1572864 | tf_op jit(solution)/shard_map/all_to_all | solution.py:849
  8.4 5.3 %shard_map.255 = bf16[8,112,768]{2,1,0:T(8,128)(2,1)} custom-call(bf16[512,768]{1,0:T(8,128)(2,1)} %bitcast.134, s32[2,512]{1,0:T(2,128)} %bitcast.148, s32[2,512]{1,0:T(2,128)} %bitcast.150), custom_call_target="tpu_custom_call" | custom-call | flops 603979776 | bytes 2170880 | tf_op jit(solution)/shard_map/pallas_call | solution.py:33
  13.8 5.4 %shard_map.256 = bf16[8,112,768]{2,1,0:T(8,128)(2,1)} custom-call(bf16[512,768]{1,0:T(8,128)(2,1)} %bitcast.135, s32[2,512]{1,0:T(2,128)} %bitcast.146, s32[2,512]{1,0:T(2,128)} %bitcast.151), custom_call_target="tpu_custom_call" | custom-call | flops 603979776 | bytes 2170880 | tf_op jit(solution)/shard_map/pallas_call | solution.py:33
  22.2 4.9 all-to-all-done.refs_0_
  28.6 17.1 %collective-permute-done.refs_1_ = bf16[4,128,768]{2,1,0:T(8,128)(2,1)S(1)} collective-permute-done((bf16[4,128,768]{2,1,0:T(8,128)(2,1)S(1)}, bf16[4,128,768]{2,1,0:T(8,128)(2,1)S(1)}, u32[]{:S(2)}, u32[]{:S(2)}) %collective-permute-start) | collective-permute-done | bytes 786464 | tf_op jit(solution)/shard_map/ppermute | solution.py:958
  51.6 7.0 %shard_map.257 = (bf16[1024,1152]{1,0:T(8,128)(2,1)}, bf16[1024,768]{1,0:T(8,128)(2,1)}) custom-call(s32[1]{0:T(128)} %bitcast.1.at_ref, bf16[4,128,768]{2,1,0:T(8,128)(2,1)} %copy-done.3, bf16[4,128,768]{2,1,0:T(8,128)(2,1)} %copy-done.8, f32[1,768]{1,0:T(1,128)} %reshape.256.refs_2_.g_ref, f32[1024,128]{1,0:T(8,128)} %get-tuple-element.88.refs_3_.c_ref, ...), custom_call_target="tpu_custom_call" | custom-call | flops 1811939328 | bytes 17173508 | tf_op jit(solution)/shard_map/pallas_call | solution.py:33
  58.6 13.1 %shard_map.258 = (bf16[1024,384]{1,0:T(8,128)(2,1)}, f32[3,2,1024]{2,1,0:T(2,128)}) custom-call(bf16[1024,1152]{1,0:T(8,128)(2,1)} %get-tuple-element.90.q_ref.k_ref.v_ref, bf16[1024,1152]{1,0:T(8,128)(2,1)} %get-tuple-element.90.q_ref.k_ref.v_ref, bf16[1024,1152]{1,0:T(8,128)(2,1)} %get-tuple-element.90.q_ref.k_ref.v_ref, ...), custom_call_target="tpu_custom_call" | custom-call | flops 1610612736 | bytes 7897088 | tf_op jit(solution)/shard_map/pallas_call | solution.py:33
  71.7 9.2 %all-to-all-done.1 = bf16[8,112,768]{2,1,0:T(8,128)(2,1)S(1)} async-done(((bf16[8,112,768]{2,1,0:T(8,128)(2,1)}), bf16[8,112,768]{2,1,0:T(8,128)(2,1)S(1)}, u32[]{:S(2)}, u32[]{:S(2)}) %all-to-all-start.1) | async-done | bytes 1376288 | tf_op jit(solution)/shard_map/all_to_all | solution.py:849
  80.9 23.8 %all_to_all.60 = bf16[8,128,384]{2,1,0:T(8,128)(2,1)} all-to-all(bf16[8,128,384]{2,1,0:T(8,128)(2,1)} %bitcast.142), channel_id=1, replica_groups=mesh['y'=2,'core'=2,'z'=4,'x'=2] {'z','x'}, dimensions={0} | all-to-all | bytes 1572864 | tf_op jit(solution)/shard_map/all_to_all | solution.py:849
  113.0 5.1 %shard_map.260 = bf16[8,96,768]{2,1,0:T(8,128)(2,1)} custom-call(bf16[512,768]{1,0:T(8,128)(2,1)} %get-tuple-element.100.r_ref.refs_0_.x_ref, s32[2,512]{1,0:T(2,128)} %bitcast.149), custom_call_target="tpu_custom_call" | custom-call | flops 603979776 | bytes 1970176 | tf_op jit(solution)/shard_map/pallas_call | solution.py:33
  118.1 5.1 %shard_map.261 = bf16[8,96,768]{2,1,0:T(8,128)(2,1)} custom-call(bf16[512,768]{1,0:T(8,128)(2,1)} %get-tuple-element.100.r_ref.refs_0_.x_ref, s32[2,512]{1,0:T(2,128)} %bitcast.147), custom_call_target="tpu_custom_call" | custom-call | flops 603979776 | bytes 1970176 | tf_op jit(solution)/shard_map/pallas_call | solution.py:33
  123.3 17.8 %shard_map.262 = (f32[512,768]{1,0:T(8,128)}, f32[512,768]{1,0:T(8,128)}, bf16[512,2048]{1,0:T(8,128)(2,1)}, bf16[512,2048]{1,0:T(8,128)(2,1)}, bf16[512,2048]{1,0:T(8,128)(2,1)}) custom-call(bf16[512,768]{1,0:T(8,128)(2,1)} %get-tuple-element.100.r_ref.refs_0_.x_ref, bf16[512,768]{1,0:T(8,128)(2,1)} %bitcast.136, bf16[768,2048]{1,0:T(8,128)(2,1)} %refs_2_.2, ...), custom_call_target="tpu_custom_call" | custom-call | flops 9663676416 | bytes 20447232 | tf_op jit(solution)/shard_map/pallas_call | solution.py:33
  141.1 6.0 %all-to-all-start.4 = ((bf16[8,96,768]{2,1,0:T(8,128)(2,1)}), bf16[8,96,768]{2,1,0:T(8,128)(2,1)}, u32[]{:S(2)}, u32[]{:S(2)}) async-start(bf16[8,96,768]{2,1,0:T(8,128)(2,1)} %shard_map.260), calls=%async_computation.4 | async-start | bytes 2359296 | tf_op jit(solution)/shard_map/all_to_all | solution.py:849
  147.1 12.0 %shard_map.263 = (bf16[2,2,4,3,24,2048]{5,4,3,2,1,0:T(8,128)(2,1)}, bf16[2,2,4,3,24,2048]{5,4,3,2,1,0:T(8,128)(2,1)}) custom-call(s32[1]{0:T(128)} %bitcast.15.at_ref, bf16[512,768]{1,0:T(8,128)(2,1)} %get-tuple-element.100.r_ref.refs_0_.x_ref, bf16[512,768]{1,0:T(8,128)(2,1)} %bitcast.137, bf16[512,2048]{1,0:T(8,128)(2,1)} %get-tuple-element.104.dg_ref, ...), custom_call_target="tpu_custom_call" | custom-call | flops 4831838208 | bytes 17301508 | tf_op jit(solution)/shard_map/pallas_call | solution.py:33
  159.1 15.9 %all-to-all-done.4 = bf16[8,96,768]{2,1,0:T(8,128)(2,1)} async-done(((bf16[8,96,768]{2,1,0:T(8,128)(2,1)}), bf16[8,96,768]{2,1,0:T(8,128)(2,1)}, u32[]{:S(2)}, u32[]{:S(2)}) %all-to-all-start.4) | async-done | bytes 1179680 | tf_op jit(solution)/shard_map/all_to_all | solution.py:849
  182.6 26.5 %shard_map.264 = (bf16[768,768]{1,0:T(8,128)(2,1)}, bf16[768,768]{1,0:T(8,128)(2,1)}, bf16[768,2048]{1,0:T(8,128)(2,1)}, bf16[768,2048]{1,0:T(8,128)(2,1)}, bf16...) custom-call(s32[1]{0:T(128)} %bitcast.12.refs_0_, ...), custom_call_target="tpu_custom_call" | custom-call | flops 14495514624 | bytes 25168900 | tf_op jit(solution)/shard_map/pallas_call | solution.py:33
  209.2 6.0 %all-to-all-start.5 = ((bf16[8,96,768]{2,1,0:T(8,128)(2,1)}), bf16[8,96,768]{2,1,0:T(8,128)(2,1)S(1)}, u32[]{:S(2)}, u32[]{:S(2)}) async-start(bf16[8,96,768]{2,1,0:T(8,128)(2,1)} %bitcast.129), calls=%async_computation.5 | async-start | bytes 2359296 | tf_op jit(solution)/shard_map/all_to_all | solution.py:849
  217.3 26.6 %shard_map.265 = (bf16[768,768]{1,0:T(8,128)(2,1)}, bf16[768,768]{1,0:T(8,128)(2,1)}, bf16[768,2048]{1,0:T(8,128)(2,1)}, bf16[768,2048]{1,0:T(8,128)(2,1)}, bf16...) custom-call(s32[1]{0:T(128)} %bitcast.12.refs_0_, ...), custom_call_target="tpu_custom_call" | custom-call | flops 14495514624 | bytes 25168900 | tf_op jit(solution)/shard_map/pallas_call | solution.py:33
  244.0 4.9 fusion
  248.8 6.0 %all-to-all-start.7 = ((bf16[8,96,768]{2,1,0:T(8,128)(2,1)}), bf16[8,96,768]{2,1,0:T(8,128)(2,1)S(1)}, u32[]{:S(2)}, u32[]{:S(2)}) async-start(bf16[8,96,768]{2,1,0:T(8,128)(2,1)} %bitcast.130), calls=%async_computation.7 | async-start | bytes 2359296 | tf_op jit(solution)/shard_map/all_to_all | solution.py:849
  254.8 24.2 %shard_map.266 = (bf16[2,3,768,512]{3,2,1,0:T(8,128)(2,1)}, bf16[2,3,768,512]{3,2,1,0:T(8,128)(2,1)}, f32[768,128]{1,0:T(8,128)}) custom-call(s32[1]{0:T(128)} %bitcast.15.at_ref, bf16[768,768]{1,0:T(8,128)(2,1)} %bitcast.13.refs_1_.refs_0_, bf16[768,768]{1,0:T(8,128)(2,1)} %get-tuple-element.114.refs_1_, bf16[768,2048]{1,0:T(8,128)(2,1)} %get-tuple-element.115.refs_2_, ...), custom_call_target="tpu_custom_call" | custom-call | flops 14495514624 | bytes 33816580 | tf_op jit(solution)/shard_map/pallas_call | solution.py:33
  283.0 8.4 %shard_map.267 = (f32[512,768]{1,0:T(8,128)}, bf16[512,768]{1,0:T(8,128)(2,1)}, bf16[4,2,128,384]{3,2,1,0:T(8,128)(2,1)}, f32[768,128]{1,0:T(8,128)}) custom-call(f32[512,768]{1,0:T(8,128)} %get-tuple-element.97.h_ref, f32[512,768]{1,0:T(8,128)} %get-tuple-element.110.s_ref, s32[512,4]{1,0:T(8,128)} %copy.90.t_ref, bf16[512,768]{1,0:T(8,128)(2,1)} %bitcast.138, ...), custom_call_target="tpu_custom_call" | custom-call | flops 1811939328 | bytes 11021312 | tf_op jit(solution)/shard_map/pallas_call | solution.py:33
  297.2 19.2 %all-to-all-done.8 = bf16[8,128,384]{2,1,0:T(8,128)(2,1)S(1)} async-done(((bf16[8,128,384]{2,1,0:T(8,128)(2,1)}), bf16[8,128,384]{2,1,0:T(8,128)(2,1)S(1)}, u32[]{:S(2)}, u32[]{:S(2)}) %all-to-all-start.8) | async-done | bytes 786464 | tf_op jit(solution)/shard_map/all_to_all | solution.py:849
  321.9 12.6 %shard_map.272 = (bf16[2,4,2,24,896]{4,3,2,1,0:T(8,128)(2,1)}, bf16[2,4,2,24,896]{4,3,2,1,0:T(8,128)(2,1)}) custom-call(s32[1]{0:T(128)} %bitcast.15.at_ref, bf16[512,384]{1,0:T(8,128)(2,1)} %bitcast.145, bf16[512,384]{1,0:T(8,128)(2,1)} %bitcast.144, bf16[512,768]{1,0:T(8,128)(2,1)} %get-tuple-element.140.refs_2_, f32[768,128]{1,0:T(8,128)} %select_select_fusion.refs_3_), custom_call_target="tpu_custom_call" | custom-call | flops 603979776 | bytes 3342340 | tf_op jit(solution)/shard_map/pallas_call | solution.py:33
  346.7 19.0 %shard_map.269 = (bf16[1024,384]{1,0:T(8,128)(2,1)}, bf16[1024,384]{1,0:T(8,128)(2,1)}, bf16[1024,384]{1,0:T(8,128)(2,1)}) custom-call(bf16[1024,1152]{1,0:T(8,128)(2,1)} %get-tuple-element.90.q_ref.k_ref.v_ref, bf16[1024,1152]{1,0:T(8,128)(2,1)} %get-tuple-element.90.q_ref.k_ref.v_ref, bf16[1024,1152]{1,0:T(8,128)(2,1)} %get-tuple-element.90.q_ref.k_ref.v_ref, ...), custom_call_target="tpu_custom_call" | custom-call | flops 4026531840 | bytes 11304960 | tf_op jit(solution)/shard_map/pallas_call | solution.py:33
  365.7 7.4 %shard_map.270 = (bf16[2,4,128,768]{3,2,1,0:T(8,128)(2,1)}, f32[768,128]{1,0:T(8,128)}) custom-call(s32[1]{0:T(128)} %bitcast.1.at_ref, bf16[1024,384]{1,0:T(8,128)(2,1)} %get-tuple-element.136.q_ref.refs_1_, bf16[1024,384]{1,0:T(8,128)(2,1)} %get-tuple-element.137.k_ref.refs_2_, bf16[1024,384]{1,0:T(8,128)(2,1)} %get-tuple-element.138.v_ref.refs_3_, ...), custom_call_target="tpu_custom_call" | custom-call | flops 1811939328 | bytes 16515076 | tf_op jit(solution)/shard_map/pallas_call | solution.py:33
  377.2 4.5 all-to-all-start.10
  381.7 6.8 %shard_map.273 = (bf16[2,4,2,24,1280]{4,3,2,1,0:T(8,128)(2,1)}, bf16[2,4,2,24,1280]{4,3,2,1,0:T(8,128)(2,1)}) custom-call(s32[1]{0:T(128)} %bitcast.15.at_ref, bf16[1024,768]{1,0:T(8,128)(2,1)} %get-tuple-element.145.refs_0_, bf16[1024,384]{1,0:T(8,128)(2,1)} %get-tuple-element.136.q_ref.refs_1_, bf16[1024,384]{1,0:T(8,128)(2,1)} %get-tuple-element.137.k_ref.refs_2_, ...), custom_call_target="tpu_custom_call" | custom-call | flops 1811939328 | bytes 6291460 | tf_op jit(solution)/shard_map/pallas_call | solution.py:33
  392.8 14.5 %collective-permute-done.8 = bf16[4,2,24,896]{3,2,1,0:T(8,128)(2,1)} collective-permute-done((bf16[4,2,24,896]{3,2,1,0:T(8,128)(2,1)}, bf16[4,2,24,896]{3,2,1,0:T(8,128)(2,1)}, u32[]{:S(2)}, u32[]{:S(2)}) %collective-permute-start.8) | collective-permute-done | bytes 344096 | tf_op jit(solution)/shard_map/ppermute | solution.py:874
  420.2 12.9 %collective-permute-done.13 = bf16[4,3,24,2048]{3,2,1,0:T(8,128)(2,1)} collective-permute-done((bf16[4,3,24,2048]{3,2,1,0:T(8,128)(2,1)S(1)}, bf16[4,3,24,2048]{3,2,1,0:T(8,128)(2,1)}, u32[]{:S(2)}, u32[]{:S(2)}) %collective-permute-start.13) | collective-permute-done | bytes 1179680 | tf_op jit(solution)/shard_map/ppermute | solution.py:874
  435.6 4.9 shard_map.268
  456.5 22.4 %collective-permute-done.15 = bf16[3,24,2048]{2,1,0:T(8,128)(2,1)} collective-permute-done((bf16[3,24,2048]{2,1,0:T(8,128)(2,1)S(1)}, bf16[3,24,2048]{2,1,0:T(8,128)(2,1)}, u32[]{:S(2)}, u32[]{:S(2)}) %collective-permute-start.15) | collective-permute-done | bytes 294944 | tf_op jit(solution)/shard_map/ppermute | solution.py:883
  (151 shorter events, 111.9 us)
Async XLA Ops:
  0.7 26.5 %all-to-all-start = ((bf16[4,128,768]{2,1,0:T(8,128)(2,1)}), bf16[4,128,768]{2,1,0:T(8,128)(2,1)S(1)}, u32[]{:S(2)}, u32[]{:S(2)}) async-start(bf16[4,128,768]{2,1,0:T(8,128)(2,1)} %param.16), calls=%async_computation | async-start | bytes 1572864 | tf_op jit(solution)/shard_map/all_to_all | solution.py:849
  19.1 30.2 %copy-start.20 = (bf16[768]{0:T(1024)(128)(2,1)S(1)}, bf16[768]{0:T(1024)(128)(2,1)}, u32[]{:S(2)}) copy-start(bf16[768]{0:T(1024)(128)(2,1)} %param.21) | copy-start | bytes 4612
  27.1 18.6 %collective-permute-start = (bf16[4,128,768]{2,1,0:T(8,128)(2,1)S(1)}, bf16[4,128,768]{2,1,0:T(8,128)(2,1)S(1)}, u32[]{:S(2)}, u32[]{:S(2)}) collective-permute-start(bf16[4,128,768]{2,1,0:T(8,128)(2,1)S(1)} %all-to-all-done.refs_0_), channel_id=1, source_target_pairs={{0,1},{1,0},{2,3},{3,2},{4,5},{5,4},{6,7},{7,6},{8,9},{9,8},{10,11... | collective-permute-start | bytes 2359304 | tf_op jit(solution)/shard_map/ppermute | solution.py:958
  45.7 35.2 %all-to-all-start.1 = ((bf16[8,112,768]{2,1,0:T(8,128)(2,1)}), bf16[8,112,768]{2,1,0:T(8,128)(2,1)S(1)}, u32[]{:S(2)}, u32[]{:S(2)}) async-start(bf16[8,112,768]{2,1,0:T(8,128)(2,1)} %shard_map.255), calls=%async_computation.1 | async-start | bytes 2752512 | tf_op jit(solution)/shard_map/all_to_all | solution.py:849
  71.7 36.6 %copy-start.21 = (bf16[768]{0:T(1024)(128)(2,1)S(1)}, bf16[768]{0:T(1024)(128)(2,1)}, u32[]{:S(2)}) copy-start(bf16[768]{0:T(1024)(128)(2,1)} %param.24) | copy-start | bytes 4612
  104.7 36.4 %all-to-all-start.3 = ((bf16[8,112,768]{2,1,0:T(8,128)(2,1)}), bf16[8,112,768]{2,1,0:T(8,128)(2,1)S(1)}, u32[]{:S(2)}, u32[]{:S(2)}) async-start(bf16[8,112,768]{2,1,0:T(8,128)(2,1)} %shard_map.256), calls=%async_computation.3 | async-start | bytes 2752512 | tf_op jit(solution)/shard_map/all_to_all | solution.py:849
  141.1 33.9 %all-to-all-start.4 = ((bf16[8,96,768]{2,1,0:T(8,128)(2,1)}), bf16[8,96,768]{2,1,0:T(8,128)(2,1)}, u32[]{:S(2)}, u32[]{:S(2)}) async-start(bf16[8,96,768]{2,1,0:T(8,128)(2,1)} %shard_map.260), calls=%async_computation.4 | async-start | bytes 2359296 | tf_op jit(solution)/shard_map/all_to_all | solution.py:849
  159.1 84.9 %collective-permute-start.1 = (bf16[2,2,4,3,24,2048]{5,4,3,2,1,0:T(8,128)(2,1)}, bf16[2,2,4,3,24,2048]{5,4,3,2,1,0:T(8,128)(2,1)}, u32[]{:S(2)}, u32[]{:S(2)}) collective-permute-start(bf16[2,2,4,3,24,2048]{5,4,3,2,1,0:T(8,128)(2,1)} %get-tuple-element.107), channel_id=1, source_target_pairs={{0,8},{8,0},{1,9},{9,1},{2,10},{10,2},{3,11},{11,3},{4,12},{12,4},... | collective-permute-start | bytes 14155784 | tf_op jit(solution)/shard_map/ppermute | solution.py:861
  175.0 34.2 %all-to-all-start.6 = ((bf16[8,96,768]{2,1,0:T(8,128)(2,1)}), bf16[8,96,768]{2,1,0:T(8,128)(2,1)}, u32[]{:S(2)}, u32[]{:S(2)}) async-start(bf16[8,96,768]{2,1,0:T(8,128)(2,1)} %shard_map.261), calls=%async_computation.6 | async-start | bytes 2359296 | tf_op jit(solution)/shard_map/all_to_all | solution.py:849
  209.2 39.6 %all-to-all-start.5 = ((bf16[8,96,768]{2,1,0:T(8,128)(2,1)}), bf16[8,96,768]{2,1,0:T(8,128)(2,1)S(1)}, u32[]{:S(2)}, u32[]{:S(2)}) async-start(bf16[8,96,768]{2,1,0:T(8,128)(2,1)} %bitcast.129), calls=%async_computation.5 | async-start | bytes 2359296 | tf_op jit(solution)/shard_map/all_to_all | solution.py:849
  248.8 30.2 %copy-start.6 = (bf16[8,96,768]{2,1,0:T(8,128)(2,1)}, bf16[8,96,768]{2,1,0:T(8,128)(2,1)S(1)}, u32[]{:S(2)}) copy-start(bf16[8,96,768]{2,1,0:T(8,128)(2,1)S(1)} %all-to-all-done.5) | copy-start | bytes 3538948
  248.8 33.1 %all-to-all-start.7 = ((bf16[8,96,768]{2,1,0:T(8,128)(2,1)}), bf16[8,96,768]{2,1,0:T(8,128)(2,1)S(1)}, u32[]{:S(2)}, u32[]{:S(2)}) async-start(bf16[8,96,768]{2,1,0:T(8,128)(2,1)} %bitcast.130), calls=%async_computation.7 | async-start | bytes 2359296 | tf_op jit(solution)/shard_map/all_to_all | solution.py:849
  279.0 60.9 %collective-permute-start.2 = (bf16[2,3,768,512]{3,2,1,0:T(8,128)(2,1)}, bf16[2,3,768,512]{3,2,1,0:T(8,128)(2,1)}, u32[]{:S(2)}, u32[]{:S(2)}) collective-permute-start(bf16[2,3,768,512]{3,2,1,0:T(8,128)(2,1)} %get-tuple-element.126), channel_id=1, source_target_pairs={{0,8},{8,0},{1,9},{9,1},{2,10},{10,2},{3,11},{11,3},{4,12},{12,4},... | collective-permute-start | bytes 14155784 | tf_op jit(solution)/shard_map/ppermute | solution.py:861
  291.4 28.7 %copy-start.4 = (bf16[8,128,384]{2,1,0:T(8,128)(2,1)S(1)}, bf16[8,128,384]{2,1,0:T(8,128)(2,1)}, u32[]{:S(2)}) copy-start(bf16[8,128,384]{2,1,0:T(8,128)(2,1)} %all_to_all.60) | copy-start | bytes 2359300
  291.4 25.0 %all-to-all-start.8 = ((bf16[8,128,384]{2,1,0:T(8,128)(2,1)}), bf16[8,128,384]{2,1,0:T(8,128)(2,1)S(1)}, u32[]{:S(2)}, u32[]{:S(2)}) async-start(bf16[8,128,384]{2,1,0:T(8,128)(2,1)} %bitcast.141), calls=%async_computation.8 | async-start | bytes 1572864 | tf_op jit(solution)/shard_map/all_to_all | solution.py:849
  295.7 70.1 %collective-permute-start.12 = (bf16[2,4,3,24,2048]{4,3,2,1,0:T(8,128)(2,1)}, bf16[2,4,3,24,2048]{4,3,2,1,0:T(8,128)(2,1)}, u32[]{:S(2)}, u32[]{:S(2)}) collective-permute-start(bf16[2,4,3,24,2048]{4,3,2,1,0:T(8,128)(2,1)} %fusion), channel_id=1, source_target_pairs={{0,16},{16,0},{1,17},{17,1},{2,18},{18,2},{3,19},{19,3},{4,20},{20... | collective-permute-start | bytes 7077896 | tf_op jit(solution)/shard_map/ppermute | solution.py:874
  316.4 60.7 %all-to-all-start.9 = ((bf16[8,96,768]{2,1,0:T(8,128)(2,1)}), bf16[8,96,768]{2,1,0:T(8,128)(2,1)S(1)}, u32[]{:S(2)}, u32[]{:S(2)}) async-start(bf16[8,96,768]{2,1,0:T(8,128)(2,1)} %bitcast.19), calls=%async_computation.9 | async-start | bytes 2359296 | tf_op jit(solution)/shard_map/all_to_all | solution.py:849
  334.5 10.7 %collective-permute-start.7 = (bf16[2,4,2,24,896]{4,3,2,1,0:T(8,128)(2,1)}, bf16[2,4,2,24,896]{4,3,2,1,0:T(8,128)(2,1)S(1)}, u32[]{:S(2)}, u32[]{:S(2)}) collective-permute-start(bf16[2,4,2,24,896]{4,3,2,1,0:T(8,128)(2,1)} %get-tuple-element.144), channel_id=1, source_target_pairs={{0,8},{8,0},{1,9},{9,1},{2,10},{10,2},{3,11},{11,3},{4,12},{12,4},... | collective-permute-start | bytes 2064392 | tf_op jit(solution)/shard_map/ppermute | solution.py:861
  343.7 75.0 %collective-permute-start.10 = (bf16[3,768,512]{2,1,0:T(8,128)(2,1)}, bf16[3,768,512]{2,1,0:T(8,128)(2,1)}, u32[]{:S(2)}, u32[]{:S(2)}) collective-permute-start(bf16[3,768,512]{2,1,0:T(8,128)(2,1)} %fusion.1), channel_id=1, source_target_pairs={{0,16},{16,0},{1,17},{17,1},{2,18},{18,2},{3,19},{19,3},{4,20},{20... | collective-permute-start | bytes 7077896 | tf_op jit(solution)/shard_map/ppermute | solution.py:874
  346.2 61.1 %collective-permute-start.8 = (bf16[4,2,24,896]{3,2,1,0:T(8,128)(2,1)}, bf16[4,2,24,896]{3,2,1,0:T(8,128)(2,1)}, u32[]{:S(2)}, u32[]{:S(2)}) collective-permute-start(bf16[4,2,24,896]{3,2,1,0:T(8,128)(2,1)} %fusion.11), channel_id=1, source_target_pairs={{0,16},{16,0},{1,17},{17,1},{2,18},{18,2},{3,19},{19,3},{4,20},{20... | collective-permute-start | bytes 1032200 | tf_op jit(solution)/shard_map/ppermute | solution.py:874
  375.1 34.2 %collective-permute-start.3 = (bf16[4,128,768]{2,1,0:T(8,128)(2,1)}, bf16[4,128,768]{2,1,0:T(8,128)(2,1)}, u32[]{:S(2)}, u32[]{:S(2)}) collective-permute-start(bf16[4,128,768]{2,1,0:T(8,128)(2,1)} %dynamic-slice_bitcast_fusion.2), channel_id=1, source_target_pairs={{0,1},{1,0},{2,3},{3,2},{4,5},{5,4},{6,7},{7,6},{8,9},{9,8},{10,11... | collective-permute-start | bytes 2359304 | tf_op jit(solution)/shard_map/ppermute | solution.py:874
  377.2 58.4 %all-to-all-start.10 = ((bf16[8,96,768]{2,1,0:T(8,128)(2,1)}), bf16[8,96,768]{2,1,0:T(8,128)(2,1)}, u32[]{:S(2)}, u32[]{:S(2)}) async-start(bf16[8,96,768]{2,1,0:T(8,128)(2,1)} %bitcast.128), calls=%async_computation.10 | async-start | bytes 2359296 | tf_op jit(solution)/shard_map/all_to_all | solution.py:849
  388.5 26.9 %collective-permute-start.9 = (bf16[2,4,2,24,1280]{4,3,2,1,0:T(8,128)(2,1)}, bf16[2,4,2,24,1280]{4,3,2,1,0:T(8,128)(2,1)}, u32[]{:S(2)}, u32[]{:S(2)}) collective-permute-start(bf16[2,4,2,24,1280]{4,3,2,1,0:T(8,128)(2,1)} %get-tuple-element.148), channel_id=1, source_target_pairs={{0,8},{8,0},{1,9},{9,1},{2,10},{10,2},{3,11},{11,3},{4,12},{12,4},... | collective-permute-start | bytes 2949128 | tf_op jit(solution)/shard_map/ppermute | solution.py:861
  390.7 42.4 %collective-permute-start.13 = (bf16[4,3,24,2048]{3,2,1,0:T(8,128)(2,1)S(1)}, bf16[4,3,24,2048]{3,2,1,0:T(8,128)(2,1)}, u32[]{:S(2)}, u32[]{:S(2)}) collective-permute-start(bf16[4,3,24,2048]{3,2,1,0:T(8,128)(2,1)S(1)} %fusion.4), channel_id=1, source_target_pairs={{0,1},{1,0},{2,3},{3,2},{4,5},{5,4},{6,7},{7,6},{8,9},{9,8},{10,11... | collective-permute-start | bytes 3538952 | tf_op jit(solution)/shard_map/ppermute | solution.py:874
  412.0 28.5 %collective-permute-start.6 = (bf16[128,768]{1,0:T(8,128)(2,1)}, bf16[128,768]{1,0:T(8,128)(2,1)}, u32[]{:S(2)}, u32[]{:S(2)}) collective-permute-start(bf16[128,768]{1,0:T(8,128)(2,1)} %get-tuple-element.228), channel_id=1, source_target_pairs={{0,6},{2,0},{4,2},{6,4},{1,7},{3,1},{5,3},{7,5},{8,14},{10,8},{12,... | collective-permute-start | bytes 589832 | tf_op jit(solution)/shard_map/ppermute | solution.py:883
  415.4 25.1 %collective-permute-start.5 = (bf16[128,768]{1,0:T(8,128)(2,1)}, bf16[128,768]{1,0:T(8,128)(2,1)}, u32[]{:S(2)}, u32[]{:S(2)}) collective-permute-start(bf16[128,768]{1,0:T(8,128)(2,1)} %get-tuple-element.229), channel_id=1, source_target_pairs={{0,4},{2,6},{4,0},{6,2},{1,5},{3,7},{5,1},{7,3},{8,12},{10,14},{12... | collective-permute-start | bytes 589832 | tf_op jit(solution)/shard_map/ppermute | solution.py:883
  415.4 25.1 %collective-permute-start.4 = (bf16[128,768]{1,0:T(8,128)(2,1)}, bf16[128,768]{1,0:T(8,128)(2,1)}, u32[]{:S(2)}, u32[]{:S(2)}) collective-permute-start(bf16[128,768]{1,0:T(8,128)(2,1)} %get-tuple-element.230), channel_id=1, source_target_pairs={{0,2},{2,4},{4,6},{6,0},{1,3},{3,5},{5,7},{7,1},{8,10},{10,12},{12... | collective-permute-start | bytes 589832 | tf_op jit(solution)/shard_map/ppermute | solution.py:883
  418.7 30.1 %collective-permute-start.11 = (bf16[4,2,24,1280]{3,2,1,0:T(8,128)(2,1)}, bf16[4,2,24,1280]{3,2,1,0:T(8,128)(2,1)}, u32[]{:S(2)}, u32[]{:S(2)}) collective-permute-start(bf16[4,2,24,1280]{3,2,1,0:T(8,128)(2,1)} %fusion.10), channel_id=1, source_target_pairs={{0,16},{16,0},{1,17},{17,1},{2,18},{18,2},{3,19},{19,3},{4,20},{20... | collective-permute-start | bytes 1474568 | tf_op jit(solution)/shard_map/ppermute | solution.py:874
  440.6 15.1 %collective-permute-start.14 = (bf16[3,24,2048]{2,1,0:T(8,128)(2,1)S(1)}, bf16[3,24,2048]{2,1,0:T(8,128)(2,1)S(1)}, u32[]{:S(2)}, u32[]{:S(2)}) collective-permute-start(bf16[3,24,2048]{2,1,0:T(8,128)(2,1)S(1)} %get-tuple-element.223), channel_id=1, source_target_pairs={{0,2},{2,4},{4,6},{6,0},{1,3},{3,5},{5,7},{7,1},{8,10},{10,12},{12... | collective-permute-start | bytes 884744 | tf_op jit(solution)/shard_map/ppermute | solution.py:883
  442.4 14.1 %collective-permute-start.16 = (bf16[3,24,2048]{2,1,0:T(8,128)(2,1)S(1)}, bf16[3,24,2048]{2,1,0:T(8,128)(2,1)S(1)}, u32[]{:S(2)}, u32[]{:S(2)}) collective-permute-start(bf16[3,24,2048]{2,1,0:T(8,128)(2,1)S(1)} %get-tuple-element.224), channel_id=1, source_target_pairs={{0,6},{2,0},{4,2},{6,4},{1,7},{3,1},{5,3},{7,5},{8,14},{10,8},{12,... | collective-permute-start | bytes 884744 | tf_op jit(solution)/shard_map/ppermute | solution.py:883
  444.5 34.4 %collective-permute-start.15 = (bf16[3,24,2048]{2,1,0:T(8,128)(2,1)S(1)}, bf16[3,24,2048]{2,1,0:T(8,128)(2,1)}, u32[]{:S(2)}, u32[]{:S(2)}) collective-permute-start(bf16[3,24,2048]{2,1,0:T(8,128)(2,1)S(1)} %get-tuple-element.225), channel_id=1, source_target_pairs={{0,4},{2,6},{4,0},{6,2},{1,5},{3,7},{5,1},{7,3},{8,12},{10,14},{12... | collective-permute-start | bytes 884744 | tf_op jit(solution)/shard_map/ppermute | solution.py:883
  451.2 37.6 %all-to-all-start.11 = ((bf16[8,24,2176]{2,1,0:T(8,128)(2,1)}), bf16[8,24,2176]{2,1,0:T(8,128)(2,1)}, u32[]{:S(2)}, u32[]{:S(2)}) async-start(bf16[8,24,2176]{2,1,0:T(8,128)(2,1)} %bitcast.48), calls=%async_computation.11 | async-start | bytes 1671168 | tf_op jit(solution)/shard_map/all_to_all | solution.py:849
  (20 other events, 283.8 us)
